TPU v7x, 32 devices: a whole 2x2x4 slice. The times are simulated.
32 devices in a mesh: gx: 4 (over y, core), gy: 8 (over z, x).
Axes of the slice: x: 2, y: 2, z: 4, core: 2. Of those that a mesh axis runs over, the one named last changes fastest.
Arguments:
- forcing: float32 [2, 20, 64, 1024], P(None, None, 'gx', 'gy'), may hold values from -6 to 6
- viscosity: float32 [20, 64, 1024], P(None, 'gx', 'gy'), may hold values from 0.5 to 8
- spread: float32 [20, 64, 1024], P(None, 'gx', 'gy'), may hold values from 0.2 to 2
- coupling: float32 [64, 1024], P('gx', 'gy'), may hold values from -0.5 to 0.5
- friction: float32 [64, 1024], P('gx', 'gy'), may hold values from 0.05 to 5
- ice_mask: int32 [64, 1024], P('gx', 'gy'), may hold values 0 or 1
- aggregates: int32 [64, 1024], P('gx', 'gy'), may hold values from 0 to 127, as said below
Outputs:
- solution: float32 [2, 20, 64, 1024], P(None, None, 'gx', 'gy')
- residual: float32 [2, 20, 64, 1024], P(None, None, 'gx', 'gy')
Inputs may be any that keep to these rules, and one draw needn't show every extreme that they name: `aggregates`: within each device block of 16 x 128 columns, every number from 0 to 127 names some columns of that block.
All inputs are finite; a program needn't handle non-finite values. No bound on the sum of `ice_mask` on one device may be relied on, other than what follows from the above.
Results may differ from a plain program's by a relative error of at most 0.0013.
Values sent between devices are 32-bit elements; how exact they have to be, the bound alone decides.
No kernel may reach another device: no remote copies, remote signals or barrier semaphores. Data moves between devices by JAX's collectives and lax.ppermute only.
A program may use at most 128 MiB of HBM per device.

v0:
```python
import jax
import jax.numpy as jnp
from jax import lax
from jax.sharding import PartitionSpec as P

ITERS = 3
SWEEPS = 2
CSWEEPS = 4


LINE_WEIGHT = 0.8
POINT_WEIGHT = 0.7
COARSE_WEIGHT = 0.7


def extended(cells, sides, width):
    for axis, dim in sides:
        count = lax.axis_size(axis)
        ends = count - 1
        head = lax.slice_in_dim(cells, 0, width, axis=dim)
        tail = lax.slice_in_dim(cells, cells.shape[dim] - width, cells.shape[dim], axis=dim)
        cells = jnp.concatenate(
            [
                lax.ppermute(tail, axis, [(i, (i + 1) % count) for i in range(ends)]),
                cells,
                lax.ppermute(head, axis, [((i + 1) % count, i) for i in range(ends)]),
            ],
            axis=dim,
        )
    return cells


def beside_all(padded):
    return (
        padded[..., 2:, 1:-1],
        padded[..., :-2, 1:-1],
        padded[..., 1:-1, 2:],
        padded[..., 1:-1, :-2],
    )


def fine_coefficients(viscosity, spread, coupling, friction, ice_float, mask_padded):
    east_mask, west_mask, north_mask, south_mask = beside_all(mask_padded)
    vertical = 0.5 * (viscosity[:-1] + viscosity[1:]) * ice_float
    face_total = jnp.pad(vertical, ((0, 1), (0, 0), (0, 0))) + jnp.pad(
        vertical, ((1, 0), (0, 0), (0, 0))
    )
    bottom = jnp.pad(friction[None], ((0, viscosity.shape[0] - 1), (0, 0), (0, 0)))
    diagonal = ice_float * (face_total + 4.0 * spread + bottom) + (1.0 - ice_float)
    owned_spread = spread * ice_float
    return (
        diagonal,
        vertical,
        owned_spread * east_mask,
        owned_spread * west_mask,
        owned_spread * north_mask,
        owned_spread * south_mask,
        bottom * coupling * ice_float,
    )


def group_layers(level_coefs, group_size):
    diagonal, vertical, to_east, to_west, to_north, to_south, crossed = level_coefs
    group_count = diagonal.shape[0] // group_size

    def fold_layers(values):
        return values.reshape((group_count, group_size) + values.shape[1:]).sum(axis=1)

    padded = jnp.concatenate([vertical, jnp.zeros_like(diagonal[:1])], axis=0)
    blocks = padded.reshape((group_count, group_size) + padded.shape[1:])
    inner_sum = blocks[:, : group_size - 1].sum(axis=1)
    return (
        fold_layers(diagonal) - 2.0 * inner_sum,
        blocks[:-1, group_size - 1],
        fold_layers(to_east),
        fold_layers(to_west),
        fold_layers(to_north),
        fold_layers(to_south),
        fold_layers(crossed),
    )


def apply_stencil(level_coefs, grid_field, padded):
    diagonal, vertical, to_east, to_west, to_north, to_south, crossed = level_coefs
    east_value, west_value, north_value, south_value = beside_all(padded)
    result = (
        diagonal * grid_field
        + crossed * grid_field[::-1]
        - (
            to_east * east_value
            + to_west * west_value
            + to_north * north_value
            + to_south * south_value
        )
    )
    if vertical.shape[0] > 0:
        upward = vertical * grid_field[:, 1:]
        downward = vertical * grid_field[:, :-1]
        result = result - (
            jnp.pad(upward, ((0, 0), (0, 1), (0, 0), (0, 0)))
            + jnp.pad(downward, ((0, 0), (1, 0), (0, 0), (0, 0)))
        )
    return result


def line_factor(level_coefs):
    diagonal, vertical = (level_coefs[0], level_coefs[1])
    inverse = [1.0 / diagonal[0]]
    upper = []
    for layer_at in range(1, diagonal.shape[0]):
        ratio_value = -vertical[layer_at - 1] * inverse[-1]
        upper.append(ratio_value)
        inverse.append(1.0 / (diagonal[layer_at] + vertical[layer_at - 1] * ratio_value))
    return (inverse, upper, vertical)


def line_solve(factor, right_side):
    inverse, upper, vertical = factor
    layers = len(inverse)
    forward = [right_side[:, 0] * inverse[0]]
    for layer_at in range(1, layers):
        forward.append(
            (right_side[:, layer_at] + vertical[layer_at - 1] * forward[-1]) * inverse[layer_at]
        )
    backward = [forward[-1]]
    for layer_at in range(layers - 2, -1, -1):
        backward.append(forward[layer_at] - upper[layer_at] * backward[-1])
    return jnp.stack(backward[::-1], axis=1)


def group_sum(grid_field, group_size):
    return grid_field.reshape(
        (2, grid_field.shape[1] // group_size, group_size) + grid_field.shape[2:]
    ).sum(axis=2)


def expand_layers(grid_field, group_size):
    return jnp.repeat(grid_field, group_size, axis=1)


def point_diagonal(column_coefs, group_ids, group_count):
    ids_padded = jnp.pad(group_ids, 1, constant_values=-1)
    east_id, west_id, north_id, south_id = beside_all(ids_padded)
    inner_sum = (
        jnp.where(east_id == group_ids, column_coefs[2][0], 0.0)
        + jnp.where(west_id == group_ids, column_coefs[3][0], 0.0)
        + jnp.where(north_id == group_ids, column_coefs[4][0], 0.0)
        + jnp.where(south_id == group_ids, column_coefs[5][0], 0.0)
    )
    return jax.ops.segment_sum(
        (column_coefs[0][0] - inner_sum).reshape(-1),
        group_ids.reshape(-1),
        num_segments=group_count,
    )


def coarse_coefficients(column_coefs, blocks_first, blocks_second):
    diagonal, vertical, to_east, to_west, to_north, to_south, crossed = column_coefs

    def split_block(values):
        plane = values[0]
        return plane.reshape(
            blocks_first,
            plane.shape[0] // blocks_first,
            blocks_second,
            plane.shape[1] // blocks_second,
        )

    east_block = split_block(to_east)
    west_block = split_block(to_west)
    north_block = split_block(to_north)
    south_block = split_block(to_south)
    inner_sum = (
        east_block[:, :-1].sum(axis=(1, 3))
        + west_block[:, 1:].sum(axis=(1, 3))
        + north_block[:, :, :, :-1].sum(axis=(1, 3))
        + south_block[:, :, :, 1:].sum(axis=(1, 3))
    )
    return (
        split_block(diagonal).sum(axis=(1, 3)) - inner_sum,
        split_block(crossed).sum(axis=(1, 3)),
        east_block[:, -1].sum(axis=2),
        west_block[:, 0].sum(axis=2),
        north_block[:, :, :, -1].sum(axis=1),
        south_block[:, :, :, 0].sum(axis=1),
    )


def coarse_apply(block_table, grid_field, padded):
    diagonal, crossed, to_east, to_west, to_north, to_south = block_table
    east_value, west_value, north_value, south_value = beside_all(padded)
    return (
        diagonal * grid_field
        + crossed * grid_field[::-1]
        - (
            to_east * east_value
            + to_west * west_value
            + to_north * north_value
            + to_south * south_value
        )
    )


def coarse_jacobi(block_table, right_side, widen_rim):
    answer = COARSE_WEIGHT * right_side / block_table[0]
    for sweep_at in range(CSWEEPS - 1):
        answer = (
            answer
            + COARSE_WEIGHT
            * (right_side - coarse_apply(block_table, answer, widen_rim(answer)))
            / block_table[0]
        )
    return answer


def least_squares(columns, initial_norm):
    steps_count = len(columns)
    matrix_rows = [
        [columns[column_at][row_at] for column_at in range(steps_count)]
        for row_at in range(steps_count + 1)
    ]
    target = [initial_norm] + [jnp.zeros_like(initial_norm) for row_at in range(steps_count)]
    for pivot_at in range(steps_count):
        top_value = matrix_rows[pivot_at][pivot_at]
        low_value = matrix_rows[pivot_at + 1][pivot_at]
        radius = jnp.sqrt(top_value * top_value + low_value * low_value)
        cosine = top_value / radius
        sine_value = low_value / radius
        for column_at in range(pivot_at, steps_count):
            upper_entry = matrix_rows[pivot_at][column_at]
            lower_entry = matrix_rows[pivot_at + 1][column_at]
            matrix_rows[pivot_at][column_at] = cosine * upper_entry + sine_value * lower_entry
            matrix_rows[pivot_at + 1][column_at] = cosine * lower_entry - sine_value * upper_entry
        upper_entry = target[pivot_at]
        lower_entry = target[pivot_at + 1]
        target[pivot_at] = cosine * upper_entry + sine_value * lower_entry
        target[pivot_at + 1] = cosine * lower_entry - sine_value * upper_entry
    weights = [None] * steps_count
    for pivot_at in reversed(range(steps_count)):
        partial_sum = target[pivot_at]
        for column_at in range(pivot_at + 1, steps_count):
            partial_sum = partial_sum - matrix_rows[pivot_at][column_at] * weights[column_at]
        weights[pivot_at] = partial_sum / matrix_rows[pivot_at][pivot_at]
    return weights


def body(forcing, viscosity, spread, coupling, friction, ice_mask, aggregates):
    layer_count = forcing.shape[1]
    ice_float = ice_mask.astype(jnp.float32)
    mask_padded = extended(ice_mask, (("gx", 0), ("gy", 1)), 1).astype(jnp.float32)
    fine_coefs = fine_coefficients(viscosity, spread, coupling, friction, ice_float, mask_padded)
    middle = group_layers(fine_coefs, 2)
    stencils = [fine_coefs, middle, group_layers(middle, layer_count // 2)]
    factors = [line_factor(level_coefs) for level_coefs in stencils]
    group_count = aggregates.shape[0] * aggregates.shape[1] // 16
    ids_flat = aggregates.reshape(-1)
    point_diag = point_diagonal(stencils[2], aggregates, group_count)
    block_table = coarse_coefficients(stencils[2], 1, 1)

    def fine_apply(grid_field):
        padded = extended(grid_field, (("gx", 2), ("gy", 3)), 1)
        return apply_stencil(stencils[0], grid_field, padded)

    def restrict_points(grid_field):
        flattened = grid_field.reshape(2, -1)
        return jnp.stack(
            [
                jax.ops.segment_sum(flattened[0], ids_flat, num_segments=group_count),
                jax.ops.segment_sum(flattened[1], ids_flat, num_segments=group_count),
            ]
        )

    def prolong_points(values):
        return values[:, ids_flat].reshape((2, 1) + aggregates.shape)

    def point_apply(values):
        prolonged = prolong_points(values)
        padded = extended(prolonged, (("gx", 2), ("gy", 3)), 1)
        return restrict_points(apply_stencil(stencils[2], prolonged, padded))

    def neighbour_widen(values):
        return extended(values, (("gx", 1), ("gy", 2)), 1)

    def coarse_correction(values):
        coarse_rhs = jnp.sum(values, axis=1).reshape(2, 1, 1)
        answer = coarse_jacobi(block_table, coarse_rhs, neighbour_widen)
        return answer.reshape(2, 1)

    def point_cycle(right_side):
        answer = POINT_WEIGHT * right_side / point_diag
        answer = answer + POINT_WEIGHT * (right_side - point_apply(answer)) / point_diag
        answer = answer + coarse_correction(right_side - point_apply(answer))
        for sweep_at in range(SWEEPS):
            answer = answer + POINT_WEIGHT * (right_side - point_apply(answer)) / point_diag
        return answer

    def descend(level_number, leftover):
        if level_number == 0:
            return expand_layers(line_cycle(1, group_sum(leftover, 2)), 2)
        if level_number == 1:
            depth_count = leftover.shape[1]
            return expand_layers(line_cycle(2, group_sum(leftover, depth_count)), depth_count)
        return prolong_points(point_cycle(restrict_points(leftover)))

    def sweep_apply(level_number, grid_field):
        if level_number == 0:
            padded = extended(grid_field, (("gx", 2), ("gy", 3)), 1)
        elif level_number == 1:
            padded = extended(grid_field, (("gx", 2), ("gy", 3)), 1)
        else:
            padded = extended(grid_field, (("gx", 2), ("gy", 3)), 1)
        return apply_stencil(stencils[level_number], grid_field, padded)

    def line_cycle(level_number, right_side):
        factor = factors[level_number]
        answer = LINE_WEIGHT * line_solve(factor, right_side)
        answer = answer + LINE_WEIGHT * line_solve(
            factor, right_side - sweep_apply(level_number, answer)
        )
        answer = answer + descend(level_number, right_side - sweep_apply(level_number, answer))
        for sweep_at in range(SWEEPS):
            answer = answer + LINE_WEIGHT * line_solve(
                factor, right_side - sweep_apply(level_number, answer)
            )
        return answer

    initial_norm = jnp.sqrt(lax.psum(jnp.sum(forcing * forcing), ("gx", "gy")))
    basis = [forcing / initial_norm]
    stored = []
    columns = []
    for step_at in range(ITERS):
        search = line_cycle(0, basis[step_at])
        stored.append(search)
        image = fine_apply(search)
        local_dots = jnp.stack([jnp.sum(vector * image) for vector in basis])
        projected, square_sum = lax.psum((local_dots, jnp.sum(image * image)), ("gx", "gy"))
        for index_at in range(len(basis)):
            image = image - projected[index_at] * basis[index_at]
        height = jnp.sqrt(square_sum - jnp.sum(projected * projected))
        columns.append(
            [projected[index_at] for index_at in range(len(basis))]
            + [height]
            + [jnp.zeros_like(height) for row_at in range(ITERS - 1 - step_at)]
        )
        if step_at + 1 < ITERS:
            basis.append(image / height)
    weights = least_squares(columns, initial_norm)
    solution = weights[0] * stored[0]
    for index_at in range(1, ITERS):
        solution = solution + weights[index_at] * stored[index_at]
    residual = forcing - fine_apply(solution)
    return (solution, residual)


def solution(mesh):
    return jax.shard_map(
        body,
        mesh=mesh,
        in_specs=(
            P(None, None, "gx", "gy"),
            P(None, "gx", "gy"),
            P(None, "gx", "gy"),
            P("gx", "gy"),
            P("gx", "gy"),
            P("gx", "gy"),
            P("gx", "gy"),
        ),
        out_specs=(P(None, None, "gx", "gy"), P(None, None, "gx", "gy")),
        check_vma=False,
    )
```

profile of v0, /device:TPU:0, one launch (start us, length us, event | category | flops | bytes accessed | tf_op | source)
XLA Modules:
  0.0 2252.2 jit_solution(12265902826835605389)
XLA Ops:
  8.1 42.2 %psum.49 = f32[]{:T(128)} all-reduce(f32[]{:T(128)} %multiply_reduce_fusion.9), channel_id=1, replica_groups=mesh['gx'=4,'gy'=8] {'gx','gy'}, use_global_device_ids=true, to_apply=%region_1.2 | all-reduce | flops 1 | bytes 8 | tf_op jit(solution)/shard_map/psum | solution.py:327
  88.1 20.5 collective-permute-done.7
  122.0 20.3 collective-permute-done.11
  221.2 14.7 scatter_custom_fusion.2
  236.0 14.9 scatter_custom_fusion.1
  250.9 14.7 scatter_custom_fusion
  292.1 14.7 scatter_custom_fusion.4
  306.8 14.7 scatter_custom_fusion.3
  348.6 14.7 scatter_custom_fusion.6
  363.3 14.7 scatter_custom_fusion.5
  460.2 14.7 scatter_custom_fusion.8
  474.8 14.7 scatter_custom_fusion.7
  515.1 14.7 scatter_custom_fusion.10
  529.8 14.7 scatter_custom_fusion.9
  640.7 18.1 collective-permute-done.75
  674.1 17.9 collective-permute-done.79
  726.4 48.6 %all-reduce.63 = (f32[]{:T(128)}, f32[1]{0:T(128)}) all-reduce(f32[]{:T(128)} %get-tuple-element.10, f32[1]{0:T(128)} %bitcast.151), channel_id=1, replica_groups=mesh['gx'=4,'gy'=8] {'gx','gy'}, use_global_device_ids=true, to_apply=%region_42.43 | all-reduce | flops 2 | bytes 16 | tf_op jit(solution)/shard_map/psum | solution.py:336
  790.3 20.2 collective-permute-done.87
  824.0 20.2 collective-permute-done.91
  926.9 14.8 scatter_custom_fusion.12
  941.7 14.8 scatter_custom_fusion.11
  981.3 14.8 scatter_custom_fusion.14
  996.1 14.8 scatter_custom_fusion.13
  1035.9 14.8 scatter_custom_fusion.16
  1050.7 14.8 scatter_custom_fusion.15
  1148.3 14.8 scatter_custom_fusion.18
  1163.1 14.8 scatter_custom_fusion.17
  1202.8 14.8 scatter_custom_fusion.20
  1217.6 14.8 scatter_custom_fusion.19
  1328.7 18.1 collective-permute-done.155
  1362.3 17.9 collective-permute-done.159
  1416.7 48.5 %all-reduce.62 = (f32[]{:T(128)}, f32[2]{0:T(128)S(1)}) all-reduce(f32[]{:T(128)} %get-tuple-element.7, f32[2]{0:T(128)S(1)} %pad_maximum_fusion.480), channel_id=1, replica_groups=mesh['gx'=4,'gy'=8] {'gx','gy'}, use_global_device_ids=true, to_apply=%region_60.61 | all-reduce | flops 3 | bytes 24 | tf_op jit(solution)/shard_map/psum | solution.py:336
  1482.7 20.2 collective-permute-done.167
  1516.7 20.2 collective-permute-done.171
  1623.5 15.4 scatter_custom_fusion.22
  1638.9 15.4 scatter_custom_fusion.21
  1685.3 15.3 scatter_custom_fusion.24
  1700.6 15.4 scatter_custom_fusion.23
  1747.8 15.3 scatter_custom_fusion.26
  1763.1 15.3 scatter_custom_fusion.25
  1875.5 15.4 scatter_custom_fusion.28
  1890.9 15.3 scatter_custom_fusion.27
  1938.3 15.3 scatter_custom_fusion.30
  1953.6 15.3 scatter_custom_fusion.29
  2071.7 18.1 collective-permute-done.235
  2105.8 17.7 collective-permute-done.239
  2164.2 48.5 %all-reduce.61 = (f32[3]{0:T(128)S(1)}, f32[]{:T(128)}) all-reduce(f32[3]{0:T(128)S(1)} %pad_maximum_fusion.481, f32[]{:T(128)} %get-tuple-element.2), channel_id=1, replica_groups=mesh['gx'=4,'gy'=8] {'gx','gy'}, use_global_device_ids=true, to_apply=%region_78.79 | all-reduce | flops 4 | bytes 32 | tf_op jit(solution)/shard_map/psum | solution.py:336
  2230.4 20.1 collective-permute-done.247
  (1685 shorter events, 1325.1 us)
Async XLA Ops:
  1.4 51.3 %collective-permute-start.1 = (s32[1,128]{1,0:T(1,128)S(1)}, s32[1,128]{1,0:T(1,128)S(1)}, u32[]{:S(2)}, u32[]{:S(2)}) collective-permute-start(s32[1,128]{1,0:T(1,128)S(1)} %get-tuple-element.789), channel_id=1, source_target_pairs={{8,0},{16,8},{24,16},{9,1},{17,9},{25,17},{10,2},{18,10},{26,18},{... | collective-permute-start | bytes 1544 | tf_op jit(solution)/shard_map/ppermute | solution.py:26
  2.7 50.0 %collective-permute-start = (s32[1,128]{1,0:T(1,128)S(1)}, s32[1,128]{1,0:T(1,128)S(1)}, u32[]{:S(2)}, u32[]{:S(2)}) collective-permute-start(s32[1,128]{1,0:T(1,128)S(1)} %get-tuple-element.788), channel_id=1, source_target_pairs={{0,8},{8,16},{16,24},{1,9},{9,17},{17,25},{2,10},{10,18},{18,26},{... | collective-permute-start | bytes 1544 | tf_op jit(solution)/shard_map/ppermute | solution.py:24
  71.0 10.5 collective-permute-start.4
  81.8 26.8 %collective-permute-start.7 = (f32[2,20,18,1]{3,2,1,0:T(8,128)S(1)}, f32[2,20,18,1]{3,2,1,0:T(8,128)S(1)}, u32[]{:S(2)}, u32[]{:S(2)}) collective-permute-start(f32[2,20,18,1]{3,2,1,0:T(8,128)S(1)} %get-tuple-element.449), channel_id=1, source_target_pairs={{0,1},{1,2},{2,3},{3,4},{4,5},{5,6},{6,7},{8,9},{9,10},{10,11},{11... | collective-permute-start | bytes 8648 | tf_op jit(solution)/shard_map/ppermute | solution.py:24
  86.7 21.9 collective-permute-start.6
  116.2 26.1 %collective-permute-start.11 = (f32[2,20,18,1]{3,2,1,0:T(8,128)S(1)}, f32[2,20,18,1]{3,2,1,0:T(8,128)S(1)}, u32[]{:S(2)}, u32[]{:S(2)}) collective-permute-start(f32[2,20,18,1]{3,2,1,0:T(8,128)S(1)} %get-tuple-element.447), channel_id=1, source_target_pairs={{0,1},{1,2},{2,3},{3,4},{4,5},{5,6},{6,7},{8,9},{9,10},{10,11},{11... | collective-permute-start | bytes 8648 | tf_op jit(solution)/shard_map/ppermute | solution.py:24
  120.6 21.7 collective-permute-start.10
  153.8 13.4 collective-permute-start.14
  174.8 11.1 collective-permute-start.19
  180.0 11.7 collective-permute-start.18
  214.8 21.1 collective-permute-start.27
  219.9 16.0 collective-permute-start.26
  635.2 23.6 %collective-permute-start.75 = (f32[2,20,18,1]{3,2,1,0:T(8,128)S(1)}, f32[2,20,18,1]{3,2,1,0:T(8,128)S(1)}, u32[]{:S(2)}, u32[]{:S(2)}) collective-permute-start(f32[2,20,18,1]{3,2,1,0:T(8,128)S(1)} %get-tuple-element.445), channel_id=1, source_target_pairs={{0,1},{1,2},{2,3},{3,4},{4,5},{5,6},{6,7},{8,9},{9,10},{10,11},{11... | collective-permute-start | bytes 8648 | tf_op jit(solution)/shard_map/ppermute | solution.py:24
  639.3 19.5 collective-permute-start.74
  668.6 23.4 %collective-permute-start.79 = (f32[2,20,18,1]{3,2,1,0:T(8,128)S(1)}, f32[2,20,18,1]{3,2,1,0:T(8,128)S(1)}, u32[]{:S(2)}, u32[]{:S(2)}) collective-permute-start(f32[2,20,18,1]{3,2,1,0:T(8,128)S(1)} %get-tuple-element.443), channel_id=1, source_target_pairs={{0,1},{1,2},{2,3},{3,4},{4,5},{5,6},{6,7},{8,9},{9,10},{10,11},{11... | collective-permute-start | bytes 8648 | tf_op jit(solution)/shard_map/ppermute | solution.py:24
  672.7 19.3 collective-permute-start.78
  702.0 13.0 collective-permute-start.83
  706.1 19.2 collective-permute-start.82
  784.6 26.0 %collective-permute-start.87 = (f32[2,20,18,1]{3,2,1,0:T(8,128)S(1)}, f32[2,20,18,1]{3,2,1,0:T(8,128)S(1)}, u32[]{:S(2)}, u32[]{:S(2)}) collective-permute-start(f32[2,20,18,1]{3,2,1,0:T(8,128)S(1)} %get-tuple-element.439), channel_id=1, source_target_pairs={{0,1},{1,2},{2,3},{3,4},{4,5},{5,6},{6,7},{8,9},{9,10},{10,11},{11... | collective-permute-start | bytes 8648 | tf_op jit(solution)/shard_map/ppermute | solution.py:24
  788.8 21.7 collective-permute-start.86
  818.2 26.0 %collective-permute-start.91 = (f32[2,20,18,1]{3,2,1,0:T(8,128)S(1)}, f32[2,20,18,1]{3,2,1,0:T(8,128)S(1)}, u32[]{:S(2)}, u32[]{:S(2)}) collective-permute-start(f32[2,20,18,1]{3,2,1,0:T(8,128)S(1)} %get-tuple-element.437), channel_id=1, source_target_pairs={{0,1},{1,2},{2,3},{3,4},{4,5},{5,6},{6,7},{8,9},{9,10},{10,11},{11... | collective-permute-start | bytes 8648 | tf_op jit(solution)/shard_map/ppermute | solution.py:24
  822.7 21.6 collective-permute-start.90
  857.4 11.0 collective-permute-start.94
  876.0 11.1 collective-permute-start.99
  881.2 11.7 collective-permute-start.98
  1323.2 23.6 %collective-permute-start.155 = (f32[2,20,18,1]{3,2,1,0:T(8,128)S(1)}, f32[2,20,18,1]{3,2,1,0:T(8,128)S(1)}, u32[]{:S(2)}, u32[]{:S(2)}) collective-permute-start(f32[2,20,18,1]{3,2,1,0:T(8,128)S(1)} %get-tuple-element.435), channel_id=1, source_target_pairs={{0,1},{1,2},{2,3},{3,4},{4,5},{5,6},{6,7},{8,9},{9,10},{10,11},{11... | collective-permute-start | bytes 8648 | tf_op jit(solution)/shard_map/ppermute | solution.py:24
  1327.3 19.5 collective-permute-start.154
  1356.8 23.4 %collective-permute-start.159 = (f32[2,20,18,1]{3,2,1,0:T(8,128)S(1)}, f32[2,20,18,1]{3,2,1,0:T(8,128)S(1)}, u32[]{:S(2)}, u32[]{:S(2)}) collective-permute-start(f32[2,20,18,1]{3,2,1,0:T(8,128)S(1)} %get-tuple-element.433), channel_id=1, source_target_pairs={{0,1},{1,2},{2,3},{3,4},{4,5},{5,6},{6,7},{8,9},{9,10},{10,11},{11... | collective-permute-start | bytes 8648 | tf_op jit(solution)/shard_map/ppermute | solution.py:24
  1361.0 19.3 collective-permute-start.158
  1390.2 13.0 collective-permute-start.163
  1394.3 19.2 collective-permute-start.162
  1477.0 26.0 %collective-permute-start.167 = (f32[2,20,18,1]{3,2,1,0:T(8,128)S(1)}, f32[2,20,18,1]{3,2,1,0:T(8,128)S(1)}, u32[]{:S(2)}, u32[]{:S(2)}) collective-permute-start(f32[2,20,18,1]{3,2,1,0:T(8,128)S(1)} %get-tuple-element.429), channel_id=1, source_target_pairs={{0,1},{1,2},{2,3},{3,4},{4,5},{5,6},{6,7},{8,9},{9,10},{10,11},{11... | collective-permute-start | bytes 8648 | tf_op jit(solution)/shard_map/ppermute | solution.py:24
  1481.2 21.7 collective-permute-start.166
  1510.9 26.0 %collective-permute-start.171 = (f32[2,20,18,1]{3,2,1,0:T(8,128)S(1)}, f32[2,20,18,1]{3,2,1,0:T(8,128)S(1)}, u32[]{:S(2)}, u32[]{:S(2)}) collective-permute-start(f32[2,20,18,1]{3,2,1,0:T(8,128)S(1)} %get-tuple-element.427), channel_id=1, source_target_pairs={{0,1},{1,2},{2,3},{3,4},{4,5},{5,6},{6,7},{8,9},{9,10},{10,11},{11... | collective-permute-start | bytes 8648 | tf_op jit(solution)/shard_map/ppermute | solution.py:24
  1515.3 21.6 collective-permute-start.170
  1552.9 10.9 collective-permute-start.174
  1571.6 11.1 collective-permute-start.179
  1576.9 11.9 collective-permute-start.178
  2066.2 23.6 %collective-permute-start.235 = (f32[2,20,18,1]{3,2,1,0:T(8,128)S(1)}, f32[2,20,18,1]{3,2,1,0:T(8,128)S(1)}, u32[]{:S(2)}, u32[]{:S(2)}) collective-permute-start(f32[2,20,18,1]{3,2,1,0:T(8,128)S(1)} %get-tuple-element.425), channel_id=1, source_target_pairs={{0,1},{1,2},{2,3},{3,4},{4,5},{5,6},{6,7},{8,9},{9,10},{10,11},{11... | collective-permute-start | bytes 8648 | tf_op jit(solution)/shard_map/ppermute | solution.py:24
  2070.3 19.5 collective-permute-start.234
  2100.1 23.4 %collective-permute-start.239 = (f32[2,20,18,1]{3,2,1,0:T(8,128)S(1)}, f32[2,20,18,1]{3,2,1,0:T(8,128)S(1)}, u32[]{:S(2)}, u32[]{:S(2)}) collective-permute-start(f32[2,20,18,1]{3,2,1,0:T(8,128)S(1)} %get-tuple-element.423), channel_id=1, source_target_pairs={{0,1},{1,2},{2,3},{3,4},{4,5},{5,6},{6,7},{8,9},{9,10},{10,11},{11... | collective-permute-start | bytes 8648 | tf_op jit(solution)/shard_map/ppermute | solution.py:24
  2104.2 19.3 collective-permute-start.238
  2125.6 11.8 collective-permute-start.240
  2126.9 10.5 collective-permute-start.241
  2137.6 13.0 collective-permute-start.243
  2141.8 19.2 collective-permute-start.242
  2224.8 25.7 %collective-permute-start.247 = (f32[2,20,18,1]{3,2,1,0:T(8,128)S(1)}, f32[2,20,18,1]{3,2,1,0:T(8,128)S(1)}, u32[]{:S(2)}, u32[]{:S(2)}) collective-permute-start(f32[2,20,18,1]{3,2,1,0:T(8,128)S(1)} %get-tuple-element.419), channel_id=1, source_target_pairs={{0,1},{1,2},{2,3},{3,4},{4,5},{5,6},{6,7},{8,9},{9,10},{10,11},{11... | collective-permute-start | bytes 8648 | tf_op jit(solution)/shard_map/ppermute | solution.py:24
  2229.1 21.5 collective-permute-start.246
  (398 other events, 44572.0 us)
where the time goes:
time: 2270 us; the launch traced here: 2250 us
  starting transfers between devices  667 us (29%)
  waiting for transfers between devices  592 us (26%)
  other arithmetic  589 us (26%)
  local copies, waits for them, and re-layouts  190 us (8%)
  blocking collectives  188 us (8%)
  between operations  26.5 us (1%)
    ppermute x124, starting transfers between devices, extended(): lax.ppermute(tail, axis, [(i, (i + 1) % count) for i in range(ends)])  506 us
    ppermute x124, waiting for transfers between devices, extended(): lax.ppermute(tail, axis, [(i, (i + 1) % count) for i in range(ends)])  360 us
    ppermute x124, waiting for transfers between devices, extended(): lax.ppermute(head, axis, [((i + 1) % count, i) for i in range(ends)])  233 us
    scatter-add x15, other arithmetic, restrict_points(): jax.ops.segment_sum(flattened[1], ids_flat, num_segments=group_count)  224 us
    scatter-add x15, other arithmetic, restrict_points(): jax.ops.segment_sum(flattened[0], ids_flat, num_segments=group_count)  224 us
    ppermute x124, starting transfers between devices, extended(): lax.ppermute(head, axis, [((i + 1) % count, i) for i in range(ends)])  161 us
    psum x3, blocking collectives, body(): lax.psum((local_dots, jnp.sum(image * image)), ('gx', 'gy'))  146 us
    gather x15, local copies, waits for them, and re-layouts, prolong_points(): return values[:, ids_flat].reshape((2, 1) + aggregates.shape)  122 us
  transfers between devices with their start and end apart: 248, of which 149 were waited for; matrix products, arithmetic and copies ran while one was open for 1% of the time, Pallas kernels for 0%

commit v1 on v0

v1 whole, which is shorter than its diff:
```python
import functools

import jax
import jax.numpy as jnp
from jax import lax
from jax.experimental import pallas as pl
from jax.experimental.pallas import tpu as pltpu
from jax.sharding import PartitionSpec as P

ITERS = 3
LINE_WEIGHT = 0.8
POINT_WEIGHT = 0.7
COARSE_WEIGHT = 0.7
CSWEEPS = 4
REACH = 13 * ITERS + 1

VMEM = pl.BlockSpec(memory_space=pltpu.VMEM)
SMEM = pl.BlockSpec(memory_space=pltpu.SMEM)
F32 = jnp.float32


def call(kernel, outs, args, scratch=(), name=None):
    specs = [SMEM if a.dtype == jnp.int32 and a.ndim == 1 else VMEM for a in args]
    return pl.pallas_call(
        kernel,
        out_shape=[jax.ShapeDtypeStruct(s, F32) for s in outs],
        in_specs=specs,
        out_specs=[VMEM] * len(outs),
        scratch_shapes=[pltpu.VMEM(s, F32) for s in scratch],
        name=name,
    )(*args)


class Dims:
    def __init__(self, ngx, ngy, layers, cx, cy):
        self.ngx, self.ngy, self.n = ngx, ngy, ngx * ngy
        self.layers, self.cx, self.cy = layers, cx, cy
        self.rows = ngx * cx
        self.strip = cy // ngx
        self.halo = (cy - self.strip) // 2
        self.groups = self.rows // 8
        self.slots = cy // REACH
        self.packed = -(-self.groups // self.slots)
        self.planes = 4 * layers + 4
        self.parts = -(-2 * ngx // 8) * 8


def lanes(shape):
    return lax.broadcasted_iota(jnp.int32, shape, len(shape) - 1)


def turn(x, shift, axis):
    return pltpu.roll(x, shift, axis)


class Level:
    def __init__(self, d, n, g, s, inv, face, cross, mask, mu, fw):
        self.d, self.n, self.g, self.s, self.inv, self.face = d, n, g, s, inv, face
        self.cross, self.mask, self.mu, self.fw = cross, mask, mu, fw

    def clear_rim(self):
        rows, cy = self.d.rows, self.d.cy
        for v in range(2):
            self.mu[v, :, 0:8, :] = jnp.zeros((self.n, 8, cy), F32)
            self.mu[v, :, 8 + rows : 16 + rows, :] = jnp.zeros((self.n, 8, cy), F32)

    def put_masked(self, v, k, value):
        self.mu[v, k, 8 : 8 + self.d.rows, :] = self.mask[...] * value

    def beside(self, v, k):
        rows, cy = self.d.rows, self.d.cy
        here = self.mu[v, k, 8 : 8 + rows, :]
        return (
            self.mu[v, k, 7 : 7 + rows, :]
            + self.mu[v, k, 9 : 9 + rows, :]
            + (turn(here, 1, 1) + turn(here, cy - 1, 1))
        )

    def apply(self, u, v, k, bottom=False):
        out = self.g[k] * u[v, k] - self.s[k] * self.beside(v, k)
        if self.n > 1:
            above = jnp.minimum(k + 1, self.n - 1)
            below = jnp.maximum(k - 1, 0)
            out = out - (self.face[k + 1] * u[v, above] + self.face[k] * u[v, below])
        if bottom:
            out = out + self.cross[...] * u[1 - v, k]
        return out

    def sweep(self, r, u, first=False):
        n = self.n
        start = []
        for v in range(2):
            right = r[v, 0]
            if not first:
                right = right - self.apply(u, v, 0, True)
            start.append(right * self.inv[0])
        for v in range(2):
            self.fw[v, 0] = start[v]

        def forward(k, carry):
            out = []
            for v in range(2):
                right = r[v, k]
                if not first:
                    right = right - self.apply(u, v, k)
                value = (right + self.face[k] * carry[v]) * self.inv[k]
                self.fw[v, k] = value
                out.append(value)
            return tuple(out)

        last = lax.fori_loop(1, n, forward, tuple(start)) if n > 1 else tuple(start)

        def store(v, k, value):
            new = LINE_WEIGHT * value
            if not first:
                new = u[v, k] + new
            u[v, k] = new
            self.put_masked(v, k, new)

        for v in range(2):
            store(v, n - 1, last[v])

        def backward(t, carry):
            k = n - 1 - t
            out = []
            factor = self.face[k + 1] * self.inv[k]
            for v in range(2):
                value = self.fw[v, k] + factor * carry[v]
                store(v, k, value)
                out.append(value)
            return tuple(out)

        if n > 1:
            lax.fori_loop(1, n, backward, last)


def level_set(d, coefs, mu0, fw0, mu1, fw1, mu2, fw2):
    g0, s0, i0, f0, g1, s1, i1, f1, low = coefs
    cross, mask = low.at[3], low.at[4]
    rows = d.rows
    one = lambda at: low.at[at : at + 1]
    return (
        Level(d, d.layers, g0, s0, i0, f0, cross, mask, mu0, fw0),
        Level(d, d.layers // 2, g1, s1, i1, f1, cross, mask, mu1, fw1),
        Level(d, 1, one(0), one(1), one(2), None, cross, mask, mu2, fw2),
    )


def coef_shapes(d):
    n0, n1, r, c = d.layers, d.layers // 2, d.rows, d.cy
    plane = lambda n: (n, r, c)
    return [
        plane(n0), plane(n0), plane(n0), plane(n0 + 1),
        plane(n1), plane(n1), plane(n1), plane(n1 + 1),
        plane(6),
    ]


def field(d, n):
    return (2, n, d.rows, d.cy)


def work_shapes(d):
    out = []
    for n in (d.layers, d.layers // 2, 1):
        out += [(2, n, d.rows + 16, d.cy), field(d, n)]
    return out


def own_lanes(d, shape):
    lane = lanes(shape)
    return (lane >= d.halo) & (lane < d.halo + d.strip)


def segment_acc(d, ids_ref, fetch, count):
    cy = d.cy
    wanted = lax.broadcasted_iota(jnp.int32, (cy, cy), 0).astype(F32)
    acc = [jnp.zeros((cy, cy), F32) for _ in range(count)]
    for r in range(d.cx):
        hit = ids_ref[r : r + 1, :] == wanted
        for t in range(count):
            acc[t] = acc[t] + jnp.where(hit, fetch(t, r), 0.0)
    return acc


def restrict_strip(d, strip_ids, e_ref, pack, chunk):
    lane = lanes((d.cx, d.cy))
    for v in range(2):
        out = jnp.zeros((d.cx, d.cy), F32)
        for g in range(d.ngx):
            shift = (d.strip * g - d.halo) % d.cy
            part = turn(e_ref[v, g * d.cx : (g + 1) * d.cx, :], shift, 1)
            out = jnp.where(lane // d.strip == g, part, out)
        pack[v] = out
    acc = segment_acc(d, strip_ids, lambda t, r: pack[t, r : r + 1, :], 2)
    for v in range(2):
        sums = acc[v].T.reshape(d.ngx, d.strip, d.cy).sum(axis=1)
        chunk[v * d.ngx : (v + 1) * d.ngx, :] = sums


def descend(d, levels, r0, u0, r1, u1, r2, u2, strip_ids, e2, pack, chunk):
    l0, l1, l2 = levels
    half = l0.n // 2
    l0.sweep(r0, u0, first=True)
    l0.sweep(r0, u0)

    def residual_pair(kk, bottom):
        for v in range(2):
            low = r0[v, 2 * kk] - l0.apply(u0, v, 2 * kk, bottom)
            high = r0[v, 2 * kk + 1] - l0.apply(u0, v, 2 * kk + 1)
            r1[v, kk] = low + high

    residual_pair(0, True)
    lax.fori_loop(1, half, lambda k, c: (residual_pair(k, False), c)[1], 0)
    l1.sweep(r1, u1, first=True)
    l1.sweep(r1, u1)
    zero = tuple(r1[v, 0] - l1.apply(u1, v, 0, True) for v in range(2))
    total = lax.fori_loop(
        1,
        half,
        lambda k, c: tuple(c[v] + (r1[v, k] - l1.apply(u1, v, k)) for v in range(2)),
        zero,
    )
    for v in range(2):
        r2[v, 0] = total[v]
    l2.sweep(r2, u2, first=True)
    l2.sweep(r2, u2)
    for v in range(2):
        e2[v] = r2[v, 0] - l2.apply(u2, v, 0, True)
    restrict_strip(d, strip_ids, e2, pack, chunk)


def ascend(d, levels, r0, u0, r1, u1, r2, u2):
    l0, l1, l2 = levels
    for v in range(2):
        l2.put_masked(v, 0, u2[v, 0])
    for _ in range(2):
        l2.sweep(r2, u2)

    def add1(k, c):
        for v in range(2):
            value = u1[v, k] + u2[v, 0]
            u1[v, k] = value
            l1.put_masked(v, k, value)
        return c

    lax.fori_loop(0, l1.n, add1, 0)
    for _ in range(2):
        l1.sweep(r1, u1)

    def add0(k, c):
        for v in range(2):
            for p in range(2):
                value = u0[v, 2 * k + p] + u1[v, k]
                u0[v, 2 * k + p] = value
                l0.put_masked(v, 2 * k + p, value)
        return c

    lax.fori_loop(0, l1.n, add0, 0)
    for _ in range(2):
        l0.sweep(r0, u0)


def pick(row, ids):
    return jnp.take_along_axis(
        jnp.broadcast_to(row, ids.shape), ids, axis=1, mode="promise_in_bounds"
    )


def spread_chunk(d, out, chunk):
    value = chunk[...]
    for i in range(d.n):
        out[i] = value


def pack_kernel(d, place, gathered, out):
    first = place[3]

    def body(p, c):
        lane = lanes((8, d.cy))
        for o in range(d.packed):
            value = jnp.zeros((8, d.cy), F32)
            for s in range(d.slots):
                rg = o * d.slots + s
                if rg >= d.groups:
                    break
                block, at = rg * 8 // d.cx, rg * 8 % d.cx
                x = gathered[block, p, at : at + 8, :]
                x = turn(x, lax.rem(REACH * s - first + d.cy, d.cy), 1)
                keep = (lane >= REACH * s) & (lane < REACH * (s + 1))
                value = jnp.where(keep, x, value)
            out[p, o] = value
        return c

    lax.fori_loop(0, d.planes, body, 0)


def setup_kernel(d, place, gathered, packed, left, right, mine, *rest):
    (f, g0, s0, i0, f0, g1, s1, i1, f1, low, blk, strip_ids) = rest[:12]
    (u0, r1, u1, r2, u2, big) = rest[12:18]
    (win, chunk, e2, pack, mu0, fw0, mu1, fw1, mu2, fw2) = rest[18:]
    n0, n1, rows, cy, cx = d.layers, d.layers // 2, d.rows, d.cy, d.cx
    gx, off, is_left = place[1], place[4], place[5]

    def window(p, put):
        lane = lanes((8, cy))
        off_own = lax.rem(off + cy, cy)
        own = jnp.where(is_left == 1, (lane >= off).astype(jnp.int32), (lane < cy + off).astype(jnp.int32)) == 1
        lo = jnp.where(is_left == 1, off - REACH, cy + off)
        near = (lane >= lo) & (lane < lo + REACH)
        for rg in range(d.groups):
            block, at = rg * 8 // cx, rg * 8 % cx
            mid = turn(gathered[block, p, at : at + 8, :], off_own, 1)
            o, s = rg // d.slots, rg % d.slots
            side = turn(packed[p, o], lax.rem(lo - REACH * s + 2 * cy, cy), 1)
            put(rg, jnp.where(own, mid, jnp.where(near, side, 0.0)))

    def put_forcing(p, c):
        for v in range(2):
            def put(rg, value, v=v):
                f[v, p, rg * 8 : rg * 8 + 8, :] = value
            window(v * n0 + p, put)
        return c

    lax.fori_loop(0, n0, put_forcing, 0)

    def put_rest(p, c):
        def put(rg, value):
            win[p, rg * 8 : rg * 8 + 8, :] = value
        window(2 * n0 + p, put)
        return c

    lax.fori_loop(0, 2 * n0 + 4, put_rest, 0)

    cpl, frc, msk = win[2 * n0], win[2 * n0 + 1], win[2 * n0 + 2]
    low[4] = msk
    low[5] = win[2 * n0 + 3]
    low[3] = frc * cpl * msk
    mask = low.at[4]
    nil = jnp.zeros((rows, cy), F32)
    f0[0] = nil
    f0[n0] = nil

    def faces(k, c):
        f0[k + 1] = 0.5 * (win[k] + win[k + 1]) * mask[...]
        return c

    lax.fori_loop(0, n0 - 1, faces, 0)

    def diag(k, extra):
        m = mask[...]
        sp = win[n0 + k]
        s0[k] = sp * m
        inner = f0[k] + f0[k + 1] + 4.0 * sp
        if extra is not None:
            inner = inner + extra
        value = m * inner + (1.0 - m)
        g0[k] = value
        return value

    i0[0] = 1.0 / diag(0, frc)

    def factor0(k, prev):
        face = f0[k]
        inv = 1.0 / (diag(k, None) - face * face * prev)
        i0[k] = inv
        return inv

    lax.fori_loop(1, n0, factor0, i0[0])

    def fold(k, total):
        g1[k] = g0[2 * k] + g0[2 * k + 1] - 2.0 * f0[2 * k + 1]
        s = s0[2 * k] + s0[2 * k + 1]
        s1[k] = s
        f1[k] = f0[2 * k]
        return total + s

    low[1] = lax.fori_loop(0, n1, fold, nil)
    f1[n1] = nil
    i1[0] = 1.0 / g1[0]

    def factor1(k, prev):
        face = f1[k]
        inv = 1.0 / (g1[k] - face * face * prev)
        i1[k] = inv
        return inv

    lax.fori_loop(1, n1, factor1, i1[0])
    diag2 = 4.0 * low[1] + mask[...] * win[2 * n0 + 1] + n0 * (1.0 - mask[...])
    low[0] = diag2
    low[2] = 1.0 / diag2

    def column_sum(block):
        def add(k, t):
            return t + gathered[block, 3 * n0 + k]
        total = lax.fori_loop(0, n0, add, jnp.zeros((cx, cy), F32))
        return total * gathered[block, 4 * n0 + 2]

    prev_at, next_at = jnp.maximum(gx - 1, 0), jnp.minimum(gx + 1, d.ngx - 1)
    has_prev, has_next = (gx > 0).astype(F32), (gx < d.ngx - 1).astype(F32)
    m, ids, s2 = mine[0], mine[1], mine[2]
    fr, cp = gathered[gx, 4 * n0 + 1], gathered[gx, 4 * n0]
    row = lax.broadcasted_iota(jnp.int32, (cx, cy), 0)
    lane = lanes((cx, cy))
    prev = (gathered[prev_at, 4 * n0 + 2] * has_prev, gathered[prev_at, 4 * n0 + 3], column_sum(prev_at) * has_prev)
    after = (gathered[next_at, 4 * n0 + 2] * has_next, gathered[next_at, 4 * n0 + 3], column_sum(next_at) * has_next)
    inside = (row > 0, row < cx - 1, lane > 0, lane < cy - 1)

    def around(t, q):
        return (
            jnp.where(inside[0], turn(q, 1, 0), turn(prev[t], 1, 0)),
            jnp.where(inside[1], turn(q, cx - 1, 0), turn(after[t], cx - 1, 0)),
            jnp.where(inside[2], turn(q, 1, 1), turn(left[t], 1, 1)),
            jnp.where(inside[3], turn(q, cy - 1, 1), turn(right[t], cy - 1, 1)),
        )

    m_d, ids_d, s_d = around(0, m), around(1, ids), around(2, s2)
    g2b = 4.0 * s2 + m * fr + n0 * (1.0 - m)
    cb = fr * cp * m
    blk[0], blk[1], blk[2], blk[7] = g2b, s2, cb, ids
    weight3, weight4 = g2b, g2b
    for t in range(4):
        blk[3 + t] = m_d[t]
        blk[8 + t] = ids_d[t]
        weight3 = weight3 - jnp.where(inside[t] & (ids_d[t] == ids), s2 * m_d[t], 0.0)
        weight4 = weight4 - jnp.where(inside[t], s_d[t] * m, 0.0)
        blk[15 + t] = jnp.where(inside[t], 0.0, s_d[t] * m)
    blk[12], blk[13], blk[14] = weight3, cb, weight4
    chunk[...] = jnp.zeros(chunk.shape, F32)
    for t in range(7):
        acc = segment_acc(d, blk.at[7], lambda _, r: blk[12 + t, r : r + 1, :], 1)
        chunk[d.parts + t : d.parts + t + 1, :] = acc[0].T.sum(axis=0, keepdims=True)

    packed_ids = jnp.zeros((cx, cy), F32)
    for g in range(d.ngx):
        part = turn(low[5, g * cx : (g + 1) * cx, :], (d.strip * g - d.halo) % cy, 1)
        packed_ids = jnp.where(lane // d.strip == g, part, packed_ids)
    strip_ids[...] = packed_ids

    def square(k, t):
        return t + f[0, k] * f[0, k] + f[1, k] * f[1, k]

    total = lax.fori_loop(0, n0, square, nil)
    total = jnp.where(own_lanes(d, (rows, cy)), total, 0.0)
    chunk[d.parts + 7 : d.parts + 8, :] = total.sum(axis=0, keepdims=True)

    levels = level_set(d, (g0, s0, i0, f0, g1, s1, i1, f1, low), mu0, fw0, mu1, fw1, mu2, fw2)
    for one in levels:
        one.clear_rim()
    descend(d, levels, f, u0, r1, u1, r2, u2, strip_ids, e2, pack, chunk)
    spread_chunk(d, big, chunk)


def apply_own(d, place, y, blk, tmp, chunk):
    me, n, ngy = place[0], d.n, d.ngy
    shape = (d.cx, d.cy)
    row = lax.broadcasted_iota(jnp.int32, shape, 0)
    lane = lanes(shape)
    inside = (row > 0, row < d.cx - 1, lane > 0, lane < d.cy - 1)
    at = (
        jnp.maximum(me - ngy, 0),
        jnp.minimum(me + ngy, n - 1),
        jnp.maximum(me - 1, 0),
        jnp.minimum(me + 1, n - 1),
    )
    ids = blk[7].astype(jnp.int32)
    mine = [y[v, pl.ds(me, 1), :] for v in range(2)]
    here = [pick(mine[v], ids) for v in range(2)]
    side = [jnp.zeros(shape, F32), jnp.zeros(shape, F32)]
    for t in range(4):
        ids_t = blk[8 + t].astype(jnp.int32)
        for v in range(2):
            outer = pick(y[v, pl.ds(at[t], 1), :], ids_t)
            value = jnp.where(inside[t], pick(mine[v], ids_t), outer)
            side[v] = side[v] + blk[3 + t] * value
    for v in range(2):
        tmp[v] = blk[0] * here[v] + blk[2] * here[1 - v] - blk[1] * side[v]
    acc = segment_acc(d, blk.at[7], lambda t, r: tmp[t, r : r + 1, :], 2)
    for v in range(2):
        chunk[v : v + 1, :] = acc[v].T.sum(axis=0, keepdims=True)


def point_first(d, place, parts, table, blk, dots, y, r3, big, tmp, chunk):
    n, ngx, ngy = d.n, d.ngx, d.ngy
    for v in range(2):
        for g in range(ngx):
            total = parts[0:ngy, v * ngx + g, :]
            for i in range(1, ngx):
                total = total + parts[i * ngy : (i + 1) * ngy, v * ngx + g, :]
            r3[v, g * ngy : (g + 1) * ngy, :] = total
    diag = table[:, d.parts, :]
    for v in range(2):
        y[v] = POINT_WEIGHT * r3[v] / diag
    chunk[2:8, :] = dots[2:8, :]
    apply_own(d, place, y, blk, tmp, chunk)
    spread_chunk(d, big, chunk)


def point_middle(d, place, parts, table, blk, y_in, r3, y, big, tmp, chunk):
    n, ngy = d.n, d.ngy
    base = d.parts
    diag = table[:, base, :]
    cross = table[:, base + 1, :]
    inner = table[:, base + 2, :]
    sides = [table[:, base + 3 + t, :] for t in range(4)]
    shape = (n, d.cy)

    def total(x):
        return jnp.broadcast_to(x.sum(axis=1, keepdims=True), shape)

    def couple(values):
        return (
            turn(values[1], ngy, 0)
            + turn(values[0], n - ngy, 0)
            + turn(values[3], 1, 0)
            + turn(values[2], n - 1, 0)
        )

    y2 = [y_in[v] + POINT_WEIGHT * (r3[v] - parts[:, v, :]) / diag for v in range(2)]
    right = []
    for v in range(2):
        local = total(r3[v] - (inner * y2[v] + cross * y2[1 - v]))
        right.append(local + couple([total(s * y2[v]) for s in sides]))
    diag4, cross4 = total(inner), total(cross)
    sides4 = [total(s) for s in sides]
    x = [COARSE_WEIGHT * right[v] / diag4 for v in range(2)]
    for _ in range(CSWEEPS - 1):
        x = [
            x[v]
            + COARSE_WEIGHT
            * (right[v] - (diag4 * x[v] + cross4 * x[1 - v] - couple([s * x[v] for s in sides4])))
            / diag4
            for v in range(2)
        ]
    for v in range(2):
        y[v] = y2[v] + x[v]
    chunk[...] = jnp.zeros(chunk.shape, F32)
    apply_own(d, place, y, blk, tmp, chunk)
    spread_chunk(d, big, chunk)


def point_last(d, place, parts, table, blk, y_in, r3, y, big, tmp, chunk):
    diag = table[:, d.parts, :]
    for v in range(2):
        y[v] = y_in[v] + POINT_WEIGHT * (r3[v] - parts[:, v, :]) / diag
    chunk[...] = jnp.zeros(chunk.shape, F32)
    apply_own(d, place, y, blk, tmp, chunk)
    spread_chunk(d, big, chunk)


def correct_columns(d, place, parts, table, y_in, r3, y, low, u2):
    diag = table[:, d.parts, :]
    for v in range(2):
        y[v] = y_in[v] + POINT_WEIGHT * (r3[v] - parts[:, v, :]) / diag
    gy, off, is_left = place[2], place[4], place[5]
    shape = (d.cx, d.cy)
    lane = lanes(shape)
    own = jnp.where(is_left == 1, (lane >= off).astype(jnp.int32), (lane < d.cy + off).astype(jnp.int32)) == 1
    other = jnp.where(is_left == 1, jnp.maximum(gy - 1, 0), jnp.minimum(gy + 1, d.ngy - 1))
    for g in range(d.ngx):
        at = slice(g * d.cx, (g + 1) * d.cx)
        ids = low[5, at, :].astype(jnp.int32)
        for v in range(2):
            here = pick(y[v, pl.ds(g * d.ngy + gy, 1), :], ids)
            there = pick(y[v, pl.ds(g * d.ngy + other, 1), :], ids)
            u2[v, 0, at, :] = u2[v, 0, at, :] + jnp.where(own, here, there)


def grid_total(d, dots, row):
    x = dots[:, row, :].sum(axis=0, keepdims=True)
    return jnp.broadcast_to(x.sum(axis=1, keepdims=True), (1, d.cy))


def column_of(d, dots, step):
    inner = [grid_total(d, dots, 2 + i) for i in range(step + 1)]
    square = grid_total(d, dots, 3 + step)
    for value in inner:
        square = square - value * value
    return inner + [jnp.sqrt(square)]


def step_kernel(d, step, last, *refs):
    it = iter(refs)
    take = lambda count: [next(it) for _ in range(count)]
    (place,) = take(1)
    coefs = take(9)
    (strip_ids, r_in, u0i, r1i, u1i, r2i, u2i) = take(7)
    (parts, table, y_in, r3, dots) = take(5)
    olds_v = take(step)
    olds_z = take(step)
    (v_out, z_out, col) = take(3)
    if last:
        (dots_out, big) = take(2)
        w = take(1)[0]
        u0n = None
    else:
        (w, u0n, r1n, u1n, r2n, u2n, dots_out, big) = take(8)
    (u0, u1, u2, y, chunk, e2, pack, mu0, fw0, mu1, fw1, mu2, fw2) = take(13)
    low = coefs[8]
    levels = level_set(d, coefs, mu0, fw0, mu1, fw1, mu2, fw2)
    for one in levels:
        one.clear_rim()
    n0, n1 = d.layers, d.layers // 2

    for v in range(2):
        u2[v, 0] = u2i[v, 0]
    correct_columns(d, place, parts, table, y_in, r3, y, low, u2)

    def copy1(k, c):
        for v in range(2):
            u1[v, k] = u1i[v, k]
        return c

    def copy0(k, c):
        for v in range(2):
            u0[v, k] = u0i[v, k]
        return c

    lax.fori_loop(0, n1, copy1, 0)
    lax.fori_loop(0, n0, copy0, 0)
    ascend(d, levels, r_in, u0, r1i, u1, r2i, u2)

    if step == 0:
        norm = jnp.sqrt(grid_total(d, table, d.parts + 7))
        inner, height = [], norm
        col[...] = jnp.broadcast_to(norm, col.shape)
    else:
        column = column_of(d, dots, step - 1)
        inner, height = column[:-1], column[-1]
        for t, value in enumerate(column):
            col[t : t + 1, :] = value
    scale = 1.0 / height
    l0 = levels[0]

    def scaled(k, c):
        for v in range(2):
            vec, z = r_in[v, k], u0[v, k]
            for t in range(step):
                vec = vec - inner[t] * olds_v[t][v, k]
                z = z - inner[t] * olds_z[t][v, k]
            v_out[v, k] = vec * scale
            z = z * scale
            z_out[v, k] = z
            l0.put_masked(v, k, z)
        return c

    lax.fori_loop(0, n0, scaled, 0)
    basis = list(olds_v) + [v_out]

    def image(k, acc, bottom=False):
        acc = list(acc)
        for v in range(2):
            value = l0.apply(z_out, v, k, bottom)
            w[v, k] = value
            for t, vec in enumerate(basis):
                acc[t] = acc[t] + vec[v, k] * value
            acc[-1] = acc[-1] + value * value
        return tuple(acc)

    nil = jnp.zeros((d.rows, d.cy), F32)
    acc = image(0, (nil,) * (step + 2), True)
    acc = lax.fori_loop(1, n0, image, acc)
    own = own_lanes(d, (d.rows, d.cy))
    dots_out[...] = jnp.zeros(dots_out.shape, F32)
    for t in range(step + 2):
        dots_out[2 + t : 3 + t, :] = jnp.where(own, acc[t], 0.0).sum(axis=0, keepdims=True)
    if last:
        spread_chunk(d, big, dots_out)
    else:
        descend(d, levels, w, u0n, r1n, u1n, r2n, u2n, strip_ids, e2, pack, chunk)
        spread_chunk(d, big, chunk)


def least_squares(columns, initial_norm):
    count = len(columns)
    rows = [[columns[c][r] for c in range(count)] for r in range(count + 1)]
    target = [initial_norm] + [jnp.zeros_like(initial_norm) for _ in range(count)]
    for p in range(count):
        top, low = rows[p][p], rows[p + 1][p]
        radius = jnp.sqrt(top * top + low * low)
        cosine, sine = top / radius, low / radius
        for c in range(p, count):
            upper, lower = rows[p][c], rows[p + 1][c]
            rows[p][c] = cosine * upper + sine * lower
            rows[p + 1][c] = cosine * lower - sine * upper
        upper, lower = target[p], target[p + 1]
        target[p] = cosine * upper + sine * lower
        target[p + 1] = cosine * lower - sine * upper
    weights = [None] * count
    for p in reversed(range(count)):
        partial = target[p]
        for c in range(p + 1, count):
            partial = partial - rows[p][c] * weights[c]
        weights[p] = partial / rows[p][p]
    return weights


def final_kernel(d, g0, s0, i0, f0, low, f, dots, *refs):
    cols, zs = refs[:ITERS], refs[ITERS : 2 * ITERS]
    out, x, res, mu0 = refs[2 * ITERS :]
    n0 = d.layers
    norm = cols[0][0:1, :]
    nil = jnp.zeros_like(norm)
    columns = []
    for j in range(ITERS):
        if j + 1 < ITERS:
            column = [cols[j + 1][t : t + 1, :] for t in range(j + 2)]
        else:
            column = column_of(d, dots, j)
        columns.append(column + [nil] * (ITERS - 1 - j))
    weights = least_squares(columns, norm)
    l0 = Level(d, n0, g0, s0, i0, f0, low.at[3], low.at[4], mu0, None)
    l0.clear_rim()

    def combine(k, c):
        for v in range(2):
            value = weights[0] * zs[0][v, k]
            for j in range(1, ITERS):
                value = value + weights[j] * zs[j][v, k]
            x[v, k] = value
            l0.put_masked(v, k, value)
        return c

    lax.fori_loop(0, n0, combine, 0)

    def rest(k, bottom):
        for v in range(2):
            res[v, k] = f[v, k] - l0.apply(x, v, k, bottom)

    rest(0, True)
    lax.fori_loop(1, n0, lambda k, c: (rest(k, False), c)[1], 0)

    per = 4 * n0 // d.ngx
    lane = lanes((d.cx, d.cy))
    for q in range(d.ngx):
        shift = (d.strip * q - d.halo) % d.cy
        keep = lane // d.strip == q

        def place_plane(p, c, q=q, shift=shift, keep=keep):
            plane = q * per + p
            for dest in range(d.ngx):
                at = slice(dest * d.cx, (dest + 1) * d.cx)
                source = x if (q * per) < 2 * n0 else res
                local = plane if (q * per) < 2 * n0 else plane - 2 * n0
                v = (q * per) // n0 % 2
                value = turn(source[v, local - v * n0, at, :], shift, 1)
                if q == 0:
                    out[dest, p] = value
                else:
                    out[dest, p] = jnp.where(keep, value, out[dest, p])
            return c

        lax.fori_loop(0, per, place_plane, 0)


def unpack_kernel(d, got, solution_out, residual_out):
    n0 = d.layers
    per = 4 * n0 // d.ngx
    lane = lanes((d.cx, d.cy))
    for q in range(d.ngx):
        def body(p, c, q=q):
            value = None
            for src in range(d.ngx):
                part = turn(got[src, p], (d.strip * (src - q)) % d.cy, 1)
                value = part if value is None else jnp.where(lane // d.strip == src, part, value)
            first = q * per
            target = solution_out if first < 2 * n0 else residual_out
            v = first // n0 % 2
            target[v, first % n0 + p] = value
            return c

        lax.fori_loop(0, per, body, 0)


def body(forcing, viscosity, spread, coupling, friction, ice_mask, aggregates):
    ngx, ngy = lax.axis_size("gx"), lax.axis_size("gy")
    layers, cx, cy = viscosity.shape
    d = Dims(ngx, ngy, layers, cx, cy)
    both = ("gx", "gy")
    gx, gy = lax.axis_index("gx"), lax.axis_index("gy")
    is_left = gx < ngx // 2
    off = d.halo - d.strip * gx
    first = jnp.where(is_left, cy - REACH, 0)
    place = jnp.stack([gx * ngy + gy, gx, gy, first, off, is_left.astype(jnp.int32)]).astype(jnp.int32)

    mask_f, ids_f = ice_mask.astype(F32), aggregates.astype(F32)
    stacked = jnp.concatenate(
        [
            forcing.reshape(2 * layers, cx, cy),
            viscosity,
            spread,
            jnp.stack([coupling, friction, mask_f, ids_f]),
        ]
    )
    mine = jnp.stack([mask_f, ids_f, spread.sum(axis=0) * mask_f])
    east = [(i, i + 1) for i in range(ngy - 1)]
    west = [(i + 1, i) for i in range(ngy - 1)]
    left = lax.ppermute(mine, "gy", east)
    right = lax.ppermute(mine, "gy", west)
    gathered = lax.all_gather(stacked, "gx")
    (packed,) = call(
        functools.partial(pack_kernel, d),
        [(d.planes, d.packed, 8, cy)],
        [place, gathered],
        name="pack",
    )
    pairs = []
    for i in range(ngx):
        for j in range(ngy):
            to = j + 1 if i < ngx // 2 else j - 1
            if 0 <= to < ngy:
                pairs.append((i * ngy + j, i * ngy + to))
    packed = lax.ppermute(packed, both, pairs)

    n0, n1, rows = layers, layers // 2, d.rows
    fields = [field(d, n0), field(d, n1), field(d, n1), field(d, 1), field(d, 1)]
    big_shape = lambda count: (d.n, count, cy)
    wide = d.parts + 8
    state_work = [(2, rows, cy), (2, cx, cy)] + work_shapes(d)
    outs = call(
        functools.partial(setup_kernel, d),
        [field(d, n0)] + coef_shapes(d) + [(19, cx, cy), (cx, cy)] + fields + [big_shape(wide)],
        [place, gathered, packed, left, right, mine],
        [(2 * n0 + 4, rows, cy), (wide, cy)] + state_work,
        name="setup",
    )
    f, coefs, blk, strip_ids, state, big = (
        outs[0], outs[1:10], outs[10], outs[11], outs[12:17], outs[17],
    )

    def share(x):
        return lax.all_to_all(x, both, 0, 0)

    table = parts = share(big)
    dots = jnp.zeros((8, cy), F32)
    vs, zs, cols = [], [], []
    pair = (2, d.n, cy)
    small = [(2, cx, cy), (8, cy)]
    r_in = f
    for step in range(ITERS):
        y, r3, big = call(
            functools.partial(point_first, d),
            [pair, pair, big_shape(8)],
            [place, parts, table, blk, dots],
            small,
            name="point_first",
        )
        with_dots = parts = share(big)
        y, big = call(
            functools.partial(point_middle, d),
            [pair, big_shape(8)],
            [place, parts, table, blk, y, r3],
            small,
            name="point_middle",
        )
        parts = share(big)
        y, big = call(
            functools.partial(point_last, d),
            [pair, big_shape(8)],
            [place, parts, table, blk, y, r3],
            small,
            name="point_last",
        )
        parts = share(big)
        last = step + 1 == ITERS
        outs_shapes = [field(d, n0), field(d, n0), (8, cy)]
        if last:
            outs_shapes += [(8, cy), big_shape(8)]
        else:
            outs_shapes += [field(d, n0)] + fields + [(8, cy), big_shape(d.parts)]
        scratch = [field(d, n0)] if last else []
        scratch += [field(d, n0), field(d, n1), field(d, 1), pair, (d.parts, cy)] + state_work
        outs = call(
            functools.partial(step_kernel, d, step, last),
            outs_shapes,
            [place, *coefs, strip_ids, r_in, *state, parts, table, y, r3, with_dots, *vs, *zs],
            scratch,
            name="step",
        )
        vs.append(outs[0])
        zs.append(outs[1])
        cols.append(outs[2])
        if last:
            dots_all = share(outs[4])
        else:
            r_in, state, dots = outs[3], outs[4:9], outs[9]
            parts = share(outs[10])

    (out,) = call(
        functools.partial(final_kernel, d),
        [(ngx, 4 * n0 // ngx, cx, cy)],
        [*coefs[:4], coefs[8], f, dots_all, *cols, *zs],
        [field(d, n0), field(d, n0), (2, n0, rows + 16, cy)],
        name="final",
    )
    got = lax.all_to_all(out, "gx", 0, 0)
    return tuple(
        call(
            functools.partial(unpack_kernel, d),
            [forcing.shape, forcing.shape],
            [got],
            name="unpack",
        )
    )


def solution(mesh):
    return jax.shard_map(
        body,
        mesh=mesh,
        in_specs=(
            P(None, None, "gx", "gy"),
            P(None, "gx", "gy"),
            P(None, "gx", "gy"),
            P("gx", "gy"),
            P("gx", "gy"),
            P("gx", "gy"),
            P("gx", "gy"),
        ),
        out_specs=(P(None, None, "gx", "gy"), P(None, None, "gx", "gy")),
        check_vma=False,
    )
```

time: 2270 us -> 385 us (0.17)
  starting transfers between devices: 667 us -> 9.3 us
  other arithmetic: 589 us -> 0.97 us
  waiting for transfers between devices: 592 us -> 46.3 us
  local copies, waits for them, and re-layouts: 190 us -> 5.58 us
  Pallas kernels: 0 us -> 144 us
  blocking collectives: 188 us -> 164 us
    ppermute x248 -> x3, starting transfers between devices: 667 us -> 9.26 us  [the longest x1 4.55 us: body(): left = lax.ppermute(mine, 'gy', east)]
    ppermute x248 -> x3, waiting for transfers between devices: 592 us -> 17.7 us  [the longest x1 17.7 us: body(): left = lax.ppermute(mine, 'gy', east)]
    scatter-add x31 -> x0, other arithmetic: 463 us -> none  [the longest x15 224 us: restrict_points(): jax.ops.segment_sum(flattened[1], ids_flat, num_segments=group_count)]
    psum x4 -> x0, blocking collectives: 188 us -> none  [the longest x3 146 us: body(): lax.psum((local_dots, jnp.sum(image * image)), ('gx', 'gy'))]
    all_to_all x0 -> x14, blocking collectives: none -> 164 us  [the longest x13 149 us: share(): return lax.all_to_all(x, both, 0, 0)]
    pallas_call x0 -> x16, Pallas kernels: none -> 144 us  [call(): pl.pallas_call(kernel, out_shape=[jax.ShapeDtypeStruct(s, F32) for s in o...]
    gather x15 -> x0, local copies, waits for them, and re-layouts: 122 us -> none  [prolong_points(): return values[:, ids_flat].reshape((2, 1) + aggregates.shape)]
    add x58 -> x0, other arithmetic: 38.8 us -> none  [the longest x6 21.6 us: coarse_jacobi(): answer + COARSE_WEIGHT * (right_side - coarse_apply(block_table, answer,...]
  transfers between devices with their start and end apart: 248 -> 4, of which waited for: 149 -> 2; matrix products, arithmetic and copies ran while one was open for 1% -> 0% of each run, Pallas kernels for 0% -> 0%
where the time goes in v1:
time: 385 us; the launch traced here: 384 us
  blocking collectives  164 us (43%)
  Pallas kernels  144 us (37%)
  waiting for transfers between devices  46.3 us (12%)
  between operations  14.2 us (4%)
  starting transfers between devices  9.3 us (2%)
  local copies, waits for them, and re-layouts  5.58 us (1%)
    all_to_all x13, blocking collectives, share(): return lax.all_to_all(x, both, 0, 0)  149 us
    pallas_call x16, Pallas kernels, call(): pl.pallas_call(kernel, out_shape=[jax.ShapeDtypeStruct(s, F32) for s in o...  144 us
    all_gather x1, waiting for transfers between devices, body(): gathered = lax.all_gather(stacked, 'gx')  28.5 us
    ppermute x1, waiting for transfers between devices, body(): left = lax.ppermute(mine, 'gy', east)  17.7 us
    all_to_all x1, blocking collectives, body(): got = lax.all_to_all(out, 'gx', 0, 0)  14.4 us
  transfers between devices with their start and end apart: 4, of which 2 were waited for; matrix products, arithmetic and copies ran while one was open for 0% of the time, Pallas kernels for 0%

profile of v1, /device:TPU:0, one launch (start us, length us, event | category | flops | bytes accessed | tf_op | source)
XLA Modules:
  0.0 384.2 jit_solution(150403707463534966)
XLA Ops:
  7.2 0.0 copy-start.7
  7.2 0.0 all-gather.3.cloned.1.call-start
  7.3 1.0 constant_dynamic-update-slice_fusion.6
  8.2 0.9 constant_dynamic-update-slice_fusion.5
  9.2 0.9 fusion
  10.2 0.9 copy-done
  11.1 0.0 all-gather.3.cloned.1.call-update
  11.1 0.6 stack.51.place.refs_0_
  11.7 28.5 %all-gather.3.cloned.1.call-done = f32[336,16,128]{2,1,0:T(8,128)} async-done(((f32[84,16,128]{2,1,0:T(8,128)}), f32[336,16,128]{2,1,0:T(8,128)}) %all-gather.3.cloned.1.call-update) | async-done | bytes 2752528 | tf_op jit(solution)/shard_map/all_gather | solution.py:800
  40.3 9.5 %pack.1 = f32[84,3,8,128]{3,2,1,0:T(8,128)} custom-call(s32[6]{0:T(128)} %stack.51.place.refs_0_, f32[4,84,16,128]{3,2,1,0:T(8,128)} %bitcast.22), custom_call_target="tpu_custom_call" | custom-call | tf_op jit(solution)/shard_map/pack/pallas_call | solution.py:24
  49.7 3.4 collective-permute-start
  53.2 1.3 collective-permute-start.2
  54.5 4.5 %collective-permute-start.1 = (f32[3,16,128]{2,1,0:T(8,128)S(1)}, f32[3,16,128]{2,1,0:T(8,128)S(1)}, u32[]{:S(2)}, u32[]{:S(2)}) collective-permute-start(f32[3,16,128]{2,1,0:T(8,128)S(1)} %pad_maximum_fusion.mine), channel_id=1, source_target_pairs={{0,1},{1,2},{2,3},{3,4},{4,5},{5,6},{6,7},{8,9},{9,10},{10,11},{11... | collective-permute-start | bytes 73736 | tf_op jit(solution)/shard_map/ppermute | solution.py:798
  59.1 0.0 collective-permute-done.2.right
  59.1 17.7 %collective-permute-done.1.left = f32[3,16,128]{2,1,0:T(8,128)S(1)} collective-permute-done((f32[3,16,128]{2,1,0:T(8,128)S(1)}, f32[3,16,128]{2,1,0:T(8,128)S(1)}, u32[]{:S(2)}, u32[]{:S(2)}) %collective-permute-start.1) | collective-permute-done | bytes 24608 | tf_op jit(solution)/shard_map/ppermute | solution.py:798
  76.8 0.0 collective-permute-done.packed
  76.8 0.6 copy-done.6
  77.4 1.0 copy-done.1
  78.4 21.2 %setup.1 = (f32[2,20,64,128]{3,2,1,0:T(8,128)}, f32[20,64,128]{2,1,0:T(8,128)}, f32[20,64,128]{2,1,0:T(8,128)}, f32[20,64,128]{2,1,0:T(8,128)}, f32[21,64,128]{2...) custom-call(s32[6]{0:T(128)} %stack.51.place.refs_0_, ...), custom_call_target="tpu_custom_call" | custom-call | tf_op jit(solution)/shard_map/setup/pallas_call | solution.py:24
  99.6 16.2 %all_to_all.70.parts.table.refs_18_ = f32[32,16,128]{2,1,0:T(8,128)} all-to-all(f32[32,16,128]{2,1,0:T(8,128)} %get-tuple-element.82), channel_id=1, replica_groups=mesh['gx'=4,'gy'=8] {'gx','gy'}, dimensions={0} | all-to-all | bytes 524288 | tf_op jit(solution)/shard_map/all_to_all | solution.py:832
  115.8 0.6 broadcast_in_dim.3.dots
  116.4 2.2 point_first.3
  118.6 11.1 %all_to_all.71.parts.refs_21_ = f32[32,8,128]{2,1,0:T(8,128)} all-to-all(f32[32,8,128]{2,1,0:T(8,128)} %get-tuple-element.84), channel_id=1, replica_groups=mesh['gx'=4,'gy'=8] {'gx','gy'}, dimensions={0} | all-to-all | bytes 262144 | tf_op jit(solution)/shard_map/all_to_all | solution.py:832
  129.6 2.4 point_middle.3
  132.0 11.1 %all_to_all.72.parts = f32[32,8,128]{2,1,0:T(8,128)} all-to-all(f32[32,8,128]{2,1,0:T(8,128)} %get-tuple-element.87), channel_id=1, replica_groups=mesh['gx'=4,'gy'=8] {'gx','gy'}, dimensions={0} | all-to-all | bytes 262144 | tf_op jit(solution)/shard_map/all_to_all | solution.py:832
  143.1 2.2 point_last.3
  145.2 11.1 %all_to_all.73.refs_17_ = f32[32,8,128]{2,1,0:T(8,128)} all-to-all(f32[32,8,128]{2,1,0:T(8,128)} %get-tuple-element.89), channel_id=1, replica_groups=mesh['gx'=4,'gy'=8] {'gx','gy'}, dimensions={0} | all-to-all | bytes 262144 | tf_op jit(solution)/shard_map/all_to_all | solution.py:832
  156.3 26.1 %step.3 = (f32[2,20,64,128]{3,2,1,0:T(8,128)}, f32[2,20,64,128]{3,2,1,0:T(8,128)}, f32[8,128]{1,0:T(8,128)}, f32[2,20,64,128]{3,2,1,0:T(8,128)}, f32[2,20,64,128...) custom-call(s32[6]{0:T(128)} %stack.51.place.refs_0_, ...), custom_call_target="tpu_custom_call" | custom-call | tf_op jit(solution)/shard_map/step/pallas_call | solution.py:24
  182.4 11.1 %all_to_all.74.parts = f32[32,8,128]{2,1,0:T(8,128)} all-to-all(f32[32,8,128]{2,1,0:T(8,128)} %get-tuple-element.97), channel_id=1, replica_groups=mesh['gx'=4,'gy'=8] {'gx','gy'}, dimensions={0} | all-to-all | bytes 262144 | tf_op jit(solution)/shard_map/all_to_all | solution.py:832
  193.4 2.2 point_first.4
  195.6 11.1 %all_to_all.75.parts.refs_21_ = f32[32,8,128]{2,1,0:T(8,128)} all-to-all(f32[32,8,128]{2,1,0:T(8,128)} %get-tuple-element.99), channel_id=1, replica_groups=mesh['gx'=4,'gy'=8] {'gx','gy'}, dimensions={0} | all-to-all | bytes 262144 | tf_op jit(solution)/shard_map/all_to_all | solution.py:832
  206.7 2.4 point_middle.4
  209.0 11.1 %all_to_all.76.parts = f32[32,8,128]{2,1,0:T(8,128)} all-to-all(f32[32,8,128]{2,1,0:T(8,128)} %get-tuple-element.102), channel_id=1, replica_groups=mesh['gx'=4,'gy'=8] {'gx','gy'}, dimensions={0} | all-to-all | bytes 262144 | tf_op jit(solution)/shard_map/all_to_all | solution.py:832
  220.1 2.1 point_last.4
  222.2 11.1 %all_to_all.77.refs_17_ = f32[32,8,128]{2,1,0:T(8,128)} all-to-all(f32[32,8,128]{2,1,0:T(8,128)} %get-tuple-element.104), channel_id=1, replica_groups=mesh['gx'=4,'gy'=8] {'gx','gy'}, dimensions={0} | all-to-all | bytes 262144 | tf_op jit(solution)/shard_map/all_to_all | solution.py:832
  233.3 27.4 %step.4 = (f32[2,20,64,128]{3,2,1,0:T(8,128)}, f32[2,20,64,128]{3,2,1,0:T(8,128)}, f32[8,128]{1,0:T(8,128)}, f32[2,20,64,128]{3,2,1,0:T(8,128)}, f32[2,20,64,128...) custom-call(s32[6]{0:T(128)} %stack.51.place.refs_0_, ...), custom_call_target="tpu_custom_call" | custom-call | tf_op jit(solution)/shard_map/step/pallas_call | solution.py:24
  260.7 11.3 %all_to_all.78.parts = f32[32,8,128]{2,1,0:T(8,128)} all-to-all(f32[32,8,128]{2,1,0:T(8,128)} %get-tuple-element.114), channel_id=1, replica_groups=mesh['gx'=4,'gy'=8] {'gx','gy'}, dimensions={0} | all-to-all | bytes 262144 | tf_op jit(solution)/shard_map/all_to_all | solution.py:832
  271.9 2.2 point_first.5
  274.1 11.1 %all_to_all.79.parts.refs_21_ = f32[32,8,128]{2,1,0:T(8,128)} all-to-all(f32[32,8,128]{2,1,0:T(8,128)} %get-tuple-element.116), channel_id=1, replica_groups=mesh['gx'=4,'gy'=8] {'gx','gy'}, dimensions={0} | all-to-all | bytes 262144 | tf_op jit(solution)/shard_map/all_to_all | solution.py:832
  285.2 2.4 point_middle.5
  287.6 11.1 %all_to_all.80.parts = f32[32,8,128]{2,1,0:T(8,128)} all-to-all(f32[32,8,128]{2,1,0:T(8,128)} %get-tuple-element.119), channel_id=1, replica_groups=mesh['gx'=4,'gy'=8] {'gx','gy'}, dimensions={0} | all-to-all | bytes 262144 | tf_op jit(solution)/shard_map/all_to_all | solution.py:832
  298.6 2.1 point_last.5
  300.8 11.1 %all_to_all.81.refs_17_ = f32[32,8,128]{2,1,0:T(8,128)} all-to-all(f32[32,8,128]{2,1,0:T(8,128)} %get-tuple-element.121), channel_id=1, replica_groups=mesh['gx'=4,'gy'=8] {'gx','gy'}, dimensions={0} | all-to-all | bytes 262144 | tf_op jit(solution)/shard_map/all_to_all | solution.py:832
  311.8 19.2 %step.5 = (f32[2,20,64,128]{3,2,1,0:T(8,128)}, f32[2,20,64,128]{3,2,1,0:T(8,128)}, f32[8,128]{1,0:T(8,128)}, f32[8,128]{1,0:T(8,128)}, f32[32,8,128]{2,1,0:T(8,128)}) custom-call(s32[6]{0:T(128)} %stack.51.place.refs_0_, f32[20,64,128]{2,1,0:T(8,128)} %get-tuple-element.66.refs_1_.g0, f32[20,64,128]{2,1,0:T(8,128)} %get-tuple-element.67.refs_2_.s0, ...), custom_call_target="tpu_custom_call" | custom-call | tf_op jit(solution)/shard_map/step/pallas_call | solution.py:24
  331.0 11.1 %all_to_all.82.dots = f32[32,8,128]{2,1,0:T(8,128)} all-to-all(f32[32,8,128]{2,1,0:T(8,128)} %get-tuple-element.125), channel_id=1, replica_groups=mesh['gx'=4,'gy'=8] {'gx','gy'}, dimensions={0} | all-to-all | bytes 262144 | tf_op jit(solution)/shard_map/all_to_all | solution.py:832
  342.1 13.0 %final.1 = f32[4,20,16,128]{3,2,1,0:T(8,128)} custom-call(f32[20,64,128]{2,1,0:T(8,128)} %get-tuple-element.66.refs_1_.g0, f32[20,64,128]{2,1,0:T(8,128)} %get-tuple-element.67.refs_2_.s0, f32[20,64,128]{2,1,0:T(8,128)} %get-tuple-element.68.refs_3_.i0, f32[21,64,128]{2,1,0:T(8,128)} %get-tuple-element.69.refs_4_.f0, ...), custom_call_target="tpu_custom_call" | custom-call | tf_op jit(solution)/shard_map/final/pallas_call | solution.py:24
  355.1 14.4 %all_to_all.83.got = f32[4,20,16,128]{3,2,1,0:T(8,128)} all-to-all(f32[4,20,16,128]{3,2,1,0:T(8,128)} %final.1), channel_id=1, replica_groups=mesh['gx'=4,'gy'=8] {'gx'}, dimensions={0} | all-to-all | bytes 1310720 | tf_op jit(solution)/shard_map/all_to_all | solution.py:896
  369.6 7.8 %unpack.1 = (f32[2,20,16,128]{3,2,1,0:T(8,128)}, f32[2,20,16,128]{3,2,1,0:T(8,128)}) custom-call(f32[4,20,16,128]{3,2,1,0:T(8,128)} %all_to_all.83.got), custom_call_target="tpu_custom_call" | custom-call | tf_op jit(solution)/shard_map/unpack/pallas_call | solution.py:24
  (21 shorter events, 0.1 us)
Async XLA Ops:
  7.2 3.0 copy-start.7
  7.2 3.0 copy-start.8
  7.2 3.0 copy-start.3
  7.2 3.0 copy-start.4
  7.2 33.0 %all-gather.3.cloned.1.call-start = ((), (), s32[]{:S(2)}) async-start(), calls=%async_computation.14 | async-start | bytes 3440640 | tf_op jit(solution)/shard_map/all_gather | solution.py:800
  10.2 0.9 copy-start
  49.7 27.1 %collective-permute-start = (f32[84,3,8,128]{3,2,1,0:T(8,128)}, f32[84,3,8,128]{3,2,1,0:T(8,128)S(1)}, u32[]{:S(2)}, u32[]{:S(2)}) collective-permute-start(f32[84,3,8,128]{3,2,1,0:T(8,128)} %pack.1), channel_id=1, source_target_pairs={{0,1},{1,2},{2,3},{3,4},{4,5},{5,6},{6,7},{8,9},{9,10},{10,11},{11... | collective-permute-start | bytes 3096584 | tf_op jit(solution)/shard_map/ppermute | solution.py:813
  53.2 23.6 %copy-start.2 = (f32[3,16,128]{2,1,0:T(8,128)}, f32[3,16,128]{2,1,0:T(8,128)S(1)}, u32[]{:S(2)}) copy-start(f32[3,16,128]{2,1,0:T(8,128)S(1)} %pad_maximum_fusion.mine) | copy-start | bytes 73732
  53.2 5.9 %collective-permute-start.2 = (f32[3,16,128]{2,1,0:T(8,128)S(1)}, f32[3,16,128]{2,1,0:T(8,128)S(1)}, u32[]{:S(2)}, u32[]{:S(2)}) collective-permute-start(f32[3,16,128]{2,1,0:T(8,128)S(1)} %pad_maximum_fusion.mine), channel_id=1, source_target_pairs={{1,0},{2,1},{3,2},{4,3},{5,4},{6,5},{7,6},{9,8},{10,9},{11,10},{12... | collective-permute-start | bytes 73736 | tf_op jit(solution)/shard_map/ppermute | solution.py:799
  54.5 22.3 %collective-permute-start.1 = (f32[3,16,128]{2,1,0:T(8,128)S(1)}, f32[3,16,128]{2,1,0:T(8,128)S(1)}, u32[]{:S(2)}, u32[]{:S(2)}) collective-permute-start(f32[3,16,128]{2,1,0:T(8,128)S(1)} %pad_maximum_fusion.mine), channel_id=1, source_target_pairs={{0,1},{1,2},{2,3},{3,4},{4,5},{5,6},{6,7},{8,9},{9,10},{10,11},{11... | collective-permute-start | bytes 73736 | tf_op jit(solution)/shard_map/ppermute | solution.py:798
  59.1 17.7 %copy-start.5 = (f32[3,16,128]{2,1,0:T(8,128)}, f32[3,16,128]{2,1,0:T(8,128)S(1)}, u32[]{:S(2)}) copy-start(f32[3,16,128]{2,1,0:T(8,128)S(1)} %collective-permute-done.2.right) | copy-start | bytes 73732
  76.8 0.6 copy-start.6
  77.4 1.0 copy-start.1
Sparse Core Ops, SparseCore 0:
  11.2 28.9 all-gather.2

commit v2 on v1

--- a/solution.py
+++ b/solution.py
@@ -19,14 +19,29 @@
 F32 = jnp.float32
 
 
+MOST_VMEM = 60 * 1024 * 1024
+UNROLL = 3
+PIECES = 3
+
+
+def size_of(shape):
+    count = 4
+    for extent in shape[:-2]:
+        count *= extent
+    return count * (-(-shape[-2] // 8) * 8) * (-(-shape[-1] // 128) * 128)
+
+
 def call(kernel, outs, args, scratch=(), name=None):
     specs = [SMEM if a.dtype == jnp.int32 and a.ndim == 1 else VMEM for a in args]
+    shapes = [a.shape for a in args if a.ndim > 1] + list(outs) + list(scratch)
+    room = sum(size_of(shape) for shape in shapes) * 9 // 8 + 4 * 1024 * 1024
     return pl.pallas_call(
         kernel,
         out_shape=[jax.ShapeDtypeStruct(s, F32) for s in outs],
         in_specs=specs,
         out_specs=[VMEM] * len(outs),
         scratch_shapes=[pltpu.VMEM(s, F32) for s in scratch],
+        compiler_params=pltpu.CompilerParams(vmem_limit_bytes=min(room, MOST_VMEM)),
         name=name,
     )(*args)
 
@@ -43,6 +58,22 @@
         self.packed = -(-self.groups // self.slots)
         self.planes = 4 * layers + 4
         self.parts = -(-2 * ngx // 8) * 8
+        self.piece = self.planes // PIECES
+        assert self.piece * PIECES == self.planes and self.piece >= layers + 4
+
+
+def loop(lo, hi, step, init, by=UNROLL):
+    trips = (hi - lo) // by
+
+    def trip(t, carry):
+        for q in range(by):
+            carry = step(lo + t * by + q, carry)
+        return carry
+
+    carry = lax.fori_loop(0, trips, trip, init)
+    for k in range(lo + trips * by, hi):
+        carry = step(k, carry)
+    return carry
 
 
 def lanes(shape):
@@ -79,8 +110,9 @@
     def apply(self, u, v, k, bottom=False):
         out = self.g[k] * u[v, k] - self.s[k] * self.beside(v, k)
         if self.n > 1:
-            above = jnp.minimum(k + 1, self.n - 1)
-            below = jnp.maximum(k - 1, 0)
+            pick_int = isinstance(k, int)
+            above = min(k + 1, self.n - 1) if pick_int else jnp.minimum(k + 1, self.n - 1)
+            below = max(k - 1, 0) if pick_int else jnp.maximum(k - 1, 0)
             out = out - (self.face[k + 1] * u[v, above] + self.face[k] * u[v, below])
         if bottom:
             out = out + self.cross[...] * u[1 - v, k]
@@ -108,7 +140,7 @@
                 out.append(value)
             return tuple(out)
 
-        last = lax.fori_loop(1, n, forward, tuple(start)) if n > 1 else tuple(start)
+        last = loop(1, n, forward, tuple(start)) if n > 1 else tuple(start)
 
         def store(v, k, value):
             new = LINE_WEIGHT * value
@@ -131,7 +163,7 @@
             return tuple(out)
 
         if n > 1:
-            lax.fori_loop(1, n, backward, last)
+            loop(1, n, backward, last)
 
 
 def level_set(d, coefs, mu0, fw0, mu1, fw1, mu2, fw2):
@@ -211,11 +243,11 @@
             r1[v, kk] = low + high
 
     residual_pair(0, True)
-    lax.fori_loop(1, half, lambda k, c: (residual_pair(k, False), c)[1], 0)
+    loop(1, half, lambda k, c: (residual_pair(k, False), c)[1], 0)
     l1.sweep(r1, u1, first=True)
     l1.sweep(r1, u1)
     zero = tuple(r1[v, 0] - l1.apply(u1, v, 0, True) for v in range(2))
-    total = lax.fori_loop(
+    total = loop(
         1,
         half,
         lambda k, c: tuple(c[v] + (r1[v, k] - l1.apply(u1, v, k)) for v in range(2)),
@@ -230,7 +262,7 @@
     restrict_strip(d, strip_ids, e2, pack, chunk)
 
 
-def ascend(d, levels, r0, u0, r1, u1, r2, u2):
+def ascend(d, levels, r0, u0, u0i, r1, u1, u1i, r2, u2):
     l0, l1, l2 = levels
     for v in range(2):
         l2.put_masked(v, 0, u2[v, 0])
@@ -239,24 +271,24 @@
 
     def add1(k, c):
         for v in range(2):
-            value = u1[v, k] + u2[v, 0]
+            value = u1i[v, k] + u2[v, 0]
             u1[v, k] = value
             l1.put_masked(v, k, value)
         return c
 
-    lax.fori_loop(0, l1.n, add1, 0)
+    loop(0, l1.n, add1, 0)
     for _ in range(2):
         l1.sweep(r1, u1)
 
     def add0(k, c):
         for v in range(2):
             for p in range(2):
-                value = u0[v, 2 * k + p] + u1[v, k]
+                value = u0i[v, 2 * k + p] + u1[v, k]
                 u0[v, 2 * k + p] = value
                 l0.put_masked(v, 2 * k + p, value)
         return c
 
-    lax.fori_loop(0, l1.n, add0, 0)
+    loop(0, l1.n, add0, 0)
     for _ in range(2):
         l0.sweep(r0, u0)
 
@@ -292,17 +324,32 @@
             out[p, o] = value
         return c
 
-    lax.fori_loop(0, d.planes, body, 0)
-
-
-def setup_kernel(d, place, gathered, packed, left, right, mine, *rest):
+    loop(0, d.piece, body, 0)
+
+
+def segments(d):
+    n0, out = d.layers, []
+    for piece in range(PIECES):
+        at, end = piece * d.piece, (piece + 1) * d.piece
+        while at < end:
+            part = min(at // n0, 2)
+            stop = min(end, (part + 1) * n0 if part < 2 else d.planes)
+            out.append((piece, at - piece * d.piece, stop - at, part if part < 2 else None, at - part * n0))
+            at = stop
+    return out
+
+
+def setup_kernel(d, place, *rest):
+    all_gathered, all_packed, rest = rest[:PIECES], rest[PIECES : 2 * PIECES], rest[2 * PIECES :]
+    left, right, mine = rest[:3]
+    rest = rest[3:]
     (f, g0, s0, i0, f0, g1, s1, i1, f1, low, blk, strip_ids) = rest[:12]
     (u0, r1, u1, r2, u2, big) = rest[12:18]
     (win, chunk, e2, pack, mu0, fw0, mu1, fw1, mu2, fw2) = rest[18:]
     n0, n1, rows, cy, cx = d.layers, d.layers // 2, d.rows, d.cy, d.cx
     gx, off, is_left = place[1], place[4], place[5]
 
-    def window(p, put):
+    def window(gathered, packed, p, put):
         lane = lanes((8, cy))
         off_own = lax.rem(off + cy, cy)
         own = jnp.where(is_left == 1, (lane >= off).astype(jnp.int32), (lane < cy + off).astype(jnp.int32)) == 1
@@ -313,24 +360,22 @@
             mid = turn(gathered[block, p, at : at + 8, :], off_own, 1)
             o, s = rg // d.slots, rg % d.slots
             side = turn(packed[p, o], lax.rem(lo - REACH * s + 2 * cy, cy), 1)
-            put(rg, jnp.where(own, mid, jnp.where(near, side, 0.0)))
-
-    def put_forcing(p, c):
-        for v in range(2):
-            def put(rg, value, v=v):
-                f[v, p, rg * 8 : rg * 8 + 8, :] = value
-            window(v * n0 + p, put)
-        return c
-
-    lax.fori_loop(0, n0, put_forcing, 0)
-
-    def put_rest(p, c):
-        def put(rg, value):
-            win[p, rg * 8 : rg * 8 + 8, :] = value
-        window(2 * n0 + p, put)
-        return c
-
-    lax.fori_loop(0, 2 * n0 + 4, put_rest, 0)
+            put(slice(rg * 8, rg * 8 + 8), jnp.where(own, mid, jnp.where(near, side, 0.0)))
+
+    for piece, first, count, v, there in segments(d):
+        def fill(t, c, piece=piece, first=first, v=v, there=there):
+            def put(at, value):
+                if v is None:
+                    win[there + t, at, :] = value
+                else:
+                    f[v, there + t, at, :] = value
+            window(all_gathered[piece], all_packed[piece], first + t, put)
+            return c
+
+        loop(0, count, fill, 0)
+
+    gathered = all_gathered[PIECES - 1]
+    base = d.planes - d.piece
 
     cpl, frc, msk = win[2 * n0], win[2 * n0 + 1], win[2 * n0 + 2]
     low[4] = msk
@@ -345,7 +390,7 @@
         f0[k + 1] = 0.5 * (win[k] + win[k + 1]) * mask[...]
         return c
 
-    lax.fori_loop(0, n0 - 1, faces, 0)
+    loop(0, n0 - 1, faces, 0)
 
     def diag(k, extra):
         m = mask[...]
@@ -366,7 +411,7 @@
         i0[k] = inv
         return inv
 
-    lax.fori_loop(1, n0, factor0, i0[0])
+    loop(1, n0, factor0, i0[0])
 
     def fold(k, total):
         g1[k] = g0[2 * k] + g0[2 * k + 1] - 2.0 * f0[2 * k + 1]
@@ -375,7 +420,7 @@
         f1[k] = f0[2 * k]
         return total + s
 
-    low[1] = lax.fori_loop(0, n1, fold, nil)
+    low[1] = loop(0, n1, fold, nil)
     f1[n1] = nil
     i1[0] = 1.0 / g1[0]
 
@@ -385,25 +430,25 @@
         i1[k] = inv
         return inv
 
-    lax.fori_loop(1, n1, factor1, i1[0])
+    loop(1, n1, factor1, i1[0])
     diag2 = 4.0 * low[1] + mask[...] * win[2 * n0 + 1] + n0 * (1.0 - mask[...])
     low[0] = diag2
     low[2] = 1.0 / diag2
 
     def column_sum(block):
         def add(k, t):
-            return t + gathered[block, 3 * n0 + k]
-        total = lax.fori_loop(0, n0, add, jnp.zeros((cx, cy), F32))
-        return total * gathered[block, 4 * n0 + 2]
+            return t + gathered[block, 3 * n0 + k - base]
+        total = loop(0, n0, add, jnp.zeros((cx, cy), F32))
+        return total * gathered[block, 4 * n0 + 2 - base]
 
     prev_at, next_at = jnp.maximum(gx - 1, 0), jnp.minimum(gx + 1, d.ngx - 1)
     has_prev, has_next = (gx > 0).astype(F32), (gx < d.ngx - 1).astype(F32)
     m, ids, s2 = mine[0], mine[1], mine[2]
-    fr, cp = gathered[gx, 4 * n0 + 1], gathered[gx, 4 * n0]
+    fr, cp = gathered[gx, 4 * n0 + 1 - base], gathered[gx, 4 * n0 - base]
     row = lax.broadcasted_iota(jnp.int32, (cx, cy), 0)
     lane = lanes((cx, cy))
-    prev = (gathered[prev_at, 4 * n0 + 2] * has_prev, gathered[prev_at, 4 * n0 + 3], column_sum(prev_at) * has_prev)
-    after = (gathered[next_at, 4 * n0 + 2] * has_next, gathered[next_at, 4 * n0 + 3], column_sum(next_at) * has_next)
+    prev = (gathered[prev_at, 4 * n0 + 2 - base] * has_prev, gathered[prev_at, 4 * n0 + 3 - base], column_sum(prev_at) * has_prev)
+    after = (gathered[next_at, 4 * n0 + 2 - base] * has_next, gathered[next_at, 4 * n0 + 3 - base], column_sum(next_at) * has_next)
     inside = (row > 0, row < cx - 1, lane > 0, lane < cy - 1)
 
     def around(t, q):
@@ -440,7 +485,7 @@
     def square(k, t):
         return t + f[0, k] * f[0, k] + f[1, k] * f[1, k]
 
-    total = lax.fori_loop(0, n0, square, nil)
+    total = loop(0, n0, square, nil)
     total = jnp.where(own_lanes(d, (rows, cy)), total, 0.0)
     chunk[d.parts + 7 : d.parts + 8, :] = total.sum(axis=0, keepdims=True)
 
@@ -606,19 +651,7 @@
         u2[v, 0] = u2i[v, 0]
     correct_columns(d, place, parts, table, y_in, r3, y, low, u2)
 
-    def copy1(k, c):
-        for v in range(2):
-            u1[v, k] = u1i[v, k]
-        return c
-
-    def copy0(k, c):
-        for v in range(2):
-            u0[v, k] = u0i[v, k]
-        return c
-
-    lax.fori_loop(0, n1, copy1, 0)
-    lax.fori_loop(0, n0, copy0, 0)
-    ascend(d, levels, r_in, u0, r1i, u1, r2i, u2)
+    ascend(d, levels, r_in, u0, u0i, r1i, u1, u1i, r2i, u2)
 
     if step == 0:
         norm = jnp.sqrt(grid_total(d, table, d.parts + 7))
@@ -644,7 +677,7 @@
             l0.put_masked(v, k, z)
         return c
 
-    lax.fori_loop(0, n0, scaled, 0)
+    loop(0, n0, scaled, 0)
     basis = list(olds_v) + [v_out]
 
     def image(k, acc, bottom=False):
@@ -659,7 +692,7 @@
 
     nil = jnp.zeros((d.rows, d.cy), F32)
     acc = image(0, (nil,) * (step + 2), True)
-    acc = lax.fori_loop(1, n0, image, acc)
+    acc = loop(1, n0, image, acc)
     own = own_lanes(d, (d.rows, d.cy))
     dots_out[...] = jnp.zeros(dots_out.shape, F32)
     for t in range(step + 2):
@@ -721,14 +754,14 @@
             l0.put_masked(v, k, value)
         return c
 
-    lax.fori_loop(0, n0, combine, 0)
+    loop(0, n0, combine, 0)
 
     def rest(k, bottom):
         for v in range(2):
             res[v, k] = f[v, k] - l0.apply(x, v, k, bottom)
 
     rest(0, True)
-    lax.fori_loop(1, n0, lambda k, c: (rest(k, False), c)[1], 0)
+    loop(1, n0, lambda k, c: (rest(k, False), c)[1], 0)
 
     per = 4 * n0 // d.ngx
     lane = lanes((d.cx, d.cy))
@@ -750,7 +783,7 @@
                     out[dest, p] = jnp.where(keep, value, out[dest, p])
             return c
 
-        lax.fori_loop(0, per, place_plane, 0)
+        loop(0, per, place_plane, 0)
 
 
 def unpack_kernel(d, got, solution_out, residual_out):
@@ -769,7 +802,7 @@
             target[v, first % n0 + p] = value
             return c
 
-        lax.fori_loop(0, per, body, 0)
+        loop(0, per, body, 0)
 
 
 def body(forcing, viscosity, spread, coupling, friction, ice_mask, aggregates):
@@ -797,20 +830,23 @@
     west = [(i + 1, i) for i in range(ngy - 1)]
     left = lax.ppermute(mine, "gy", east)
     right = lax.ppermute(mine, "gy", west)
-    gathered = lax.all_gather(stacked, "gx")
-    (packed,) = call(
-        functools.partial(pack_kernel, d),
-        [(d.planes, d.packed, 8, cy)],
-        [place, gathered],
-        name="pack",
-    )
     pairs = []
     for i in range(ngx):
         for j in range(ngy):
             to = j + 1 if i < ngx // 2 else j - 1
             if 0 <= to < ngy:
                 pairs.append((i * ngy + j, i * ngy + to))
-    packed = lax.ppermute(packed, both, pairs)
+    gathered, packed = [], []
+    for t in range(PIECES):
+        got = lax.all_gather(stacked[t * d.piece : (t + 1) * d.piece], "gx")
+        (sent,) = call(
+            functools.partial(pack_kernel, d),
+            [(d.piece, d.packed, 8, cy)],
+            [place, got],
+            name="pack",
+        )
+        gathered.append(got)
+        packed.append(lax.ppermute(sent, both, pairs))
 
     n0, n1, rows = layers, layers // 2, d.rows
     fields = [field(d, n0), field(d, n1), field(d, n1), field(d, 1), field(d, 1)]
@@ -820,7 +856,7 @@
     outs = call(
         functools.partial(setup_kernel, d),
         [field(d, n0)] + coef_shapes(d) + [(19, cx, cy), (cx, cy)] + fields + [big_shape(wide)],
-        [place, gathered, packed, left, right, mine],
+        [place, *gathered, *packed, left, right, mine],
         [(2 * n0 + 4, rows, cy), (wide, cy)] + state_work,
         name="setup",
     )

time: 385 us -> 272 us (0.71)
  Pallas kernels: 144 us -> 72.1 us
  waiting for transfers between devices: 46.3 us -> 2.96 us
  blocking collectives: 164 us -> 178 us
  between operations: 14.2 us -> 0.99 us
  starting transfers between devices: 9.3 us -> 16.1 us
  local copies, waits for them, and re-layouts: 5.58 us -> 0.16 us
    pallas_call x16 -> x18, Pallas kernels: 144 us -> 72.1 us  [call(): pl.pallas_call(kernel, out_shape=[jax.ShapeDtypeStruct(s, F32) for s in o...]
    all_gather x0 -> x3, blocking collectives: none -> 29.2 us  [body(): got = lax.all_gather(stacked[t * d.piece:(t + 1) * d.piece], 'gx')]
    all_gather x1 -> x0, waiting for transfers between devices: 28.5 us -> none  [body(): gathered = lax.all_gather(stacked, 'gx')]
    ppermute x1, waiting for transfers between devices: 17.7 us -> 2.95 us  [body(): left = lax.ppermute(mine, 'gy', east)]
    all_to_all x13, blocking collectives: 149 us -> 136 us  [share(): return lax.all_to_all(x, both, 0, 0)]
    ppermute x1 -> x3, starting transfers between devices: 3.42 us -> 10.3 us  [body(): packed.append(lax.ppermute(sent, both, pairs))]
    unnamed x22 -> x15, local copies, waits for them, and re-layouts: 4.38 us -> 0.06 us
  transfers between devices with their start and end apart: 4 -> 5, of which waited for: 2 -> 1; matrix products, arithmetic and copies ran while one was open for 0% -> 0% of each run, Pallas kernels for 0% -> 1%
where the time goes in v2:
time: 272 us; the launch traced here: 271 us
  blocking collectives  178 us (65%)
  Pallas kernels  72.1 us (27%)
  starting transfers between devices  16.1 us (6%)
  waiting for transfers between devices  2.96 us (1%)
    all_to_all x13, blocking collectives, share(): return lax.all_to_all(x, both, 0, 0)  136 us
    pallas_call x18, Pallas kernels, call(): pl.pallas_call(kernel, out_shape=[jax.ShapeDtypeStruct(s, F32) for s in o...  72.1 us
    all_gather x3, blocking collectives, body(): got = lax.all_gather(stacked[t * d.piece:(t + 1) * d.piece], 'gx')  29.2 us
    all_to_all x1, blocking collectives, body(): got = lax.all_to_all(out, 'gx', 0, 0)  12.6 us
    ppermute x3, starting transfers between devices, body(): packed.append(lax.ppermute(sent, both, pairs))  10.3 us
  transfers between devices with their start and end apart: 5, of which 1 were waited for; matrix products, arithmetic and copies ran while one was open for 0% of the time, Pallas kernels for 1%

profile of v2, /device:TPU:0, one launch (start us, length us, event | category | flops | bytes accessed | tf_op | source)
XLA Modules:
  0.0 271.2 jit_solution(2794523832285651556)
XLA Ops:
  0.6 1.1 pad_maximum_fusion
  1.7 0.0 copy-start
  1.7 0.0 copy-start.1
  1.7 0.0 copy-start.4
  1.8 0.0 copy-start.2
  1.8 0.0 copy-start.3
  1.8 10.9 %all-gather.1 = f32[112,16,128]{2,1,0:T(8,128)S(1)} all-gather(f32[28,16,128]{2,1,0:T(8,128)S(1)} %get-tuple-element.130), channel_id=3, replica_groups=mesh['gx'=4,'gy'=8] {'gx'}, dimensions={0}, use_global_device_ids=true | all-gather | bytes 1146880 | tf_op jit(solution)/shard_map/all_gather | solution.py:841
  12.7 0.1 stack.51.place.refs_0_
  12.8 1.4 pack.4
  14.3 3.4 %collective-permute-start.1 = (f32[28,3,8,128]{3,2,1,0:T(8,128)S(1)}, f32[28,3,8,128]{3,2,1,0:T(8,128)S(1)}, u32[]{:S(2)}, u32[]{:S(2)}) collective-permute-start(f32[28,3,8,128]{3,2,1,0:T(8,128)S(1)} %pack.4), channel_id=1, source_target_pairs={{0,1},{1,2},{2,3},{3,4},{4,5},{5,6},{6,7},{8,9},{9,10},{10,11},{11... | collective-permute-start | bytes 1032200 | tf_op jit(solution)/shard_map/ppermute | solution.py:849
  17.9 9.1 %all-gather.2 = f32[112,16,128]{2,1,0:T(8,128)S(1)} all-gather(f32[28,16,128]{2,1,0:T(8,128)S(1)} %slice.15), channel_id=4, replica_groups=mesh['gx'=4,'gy'=8] {'gx'}, dimensions={0}, use_global_device_ids=true | all-gather | bytes 1146880 | tf_op jit(solution)/shard_map/all_gather | solution.py:841
  27.0 1.4 pack.5
  28.4 3.5 %collective-permute-start.2 = (f32[28,3,8,128]{3,2,1,0:T(8,128)S(1)}, f32[28,3,8,128]{3,2,1,0:T(8,128)S(1)}, u32[]{:S(2)}, u32[]{:S(2)}) collective-permute-start(f32[28,3,8,128]{3,2,1,0:T(8,128)S(1)} %pack.5), channel_id=1, source_target_pairs={{0,1},{1,2},{2,3},{3,4},{4,5},{5,6},{6,7},{8,9},{9,10},{10,11},{11... | collective-permute-start | bytes 1032200 | tf_op jit(solution)/shard_map/ppermute | solution.py:849
  31.9 9.1 %all-gather = f32[112,16,128]{2,1,0:T(8,128)S(1)} all-gather(f32[28,16,128]{2,1,0:T(8,128)S(1)} %get-tuple-element.131), channel_id=2, replica_groups=mesh['gx'=4,'gy'=8] {'gx'}, dimensions={0}, use_global_device_ids=true | all-gather | bytes 1146880 | tf_op jit(solution)/shard_map/all_gather | solution.py:841
  41.0 1.4 pack.3
  42.5 3.4 %collective-permute-start = (f32[28,3,8,128]{3,2,1,0:T(8,128)S(1)}, f32[28,3,8,128]{3,2,1,0:T(8,128)S(1)}, u32[]{:S(2)}, u32[]{:S(2)}) collective-permute-start(f32[28,3,8,128]{3,2,1,0:T(8,128)S(1)} %pack.3), channel_id=1, source_target_pairs={{0,1},{1,2},{2,3},{3,4},{4,5},{5,6},{6,7},{8,9},{9,10},{10,11},{11... | collective-permute-start | bytes 1032200 | tf_op jit(solution)/shard_map/ppermute | solution.py:849
  45.9 1.3 collective-permute-start.4
  47.2 4.5 %collective-permute-start.3 = (f32[3,16,128]{2,1,0:T(8,128)S(1)}, f32[3,16,128]{2,1,0:T(8,128)S(1)}, u32[]{:S(2)}, u32[]{:S(2)}) collective-permute-start(f32[3,16,128]{2,1,0:T(8,128)S(1)} %pad_maximum_fusion.1.rest_8_), channel_id=1, source_target_pairs={{0,1},{1,2},{2,3},{3,4},{4,5},{5,6},{6,7},{8,9},{9,10},{10,11},{11... | collective-permute-start | bytes 73736 | tf_op jit(solution)/shard_map/ppermute | solution.py:831
  51.8 2.9 %collective-permute-done.3.rest_6_ = f32[3,16,128]{2,1,0:T(8,128)S(1)} collective-permute-done((f32[3,16,128]{2,1,0:T(8,128)S(1)}, f32[3,16,128]{2,1,0:T(8,128)S(1)}, u32[]{:S(2)}, u32[]{:S(2)}) %collective-permute-start.3) | collective-permute-done | bytes 24608 | tf_op jit(solution)/shard_map/ppermute | solution.py:831
  54.7 11.9 %setup.1 = (f32[2,20,64,128]{3,2,1,0:T(8,128)S(1)}, f32[20,64,128]{2,1,0:T(8,128)S(1)}, f32[20,64,128]{2,1,0:T(8,128)S(1)}, f32[20,64,128]{2,1,0:T(8,128)S(1)}, ...) custom-call(s32[6]{0:T(128)S(1)} %stack.51.place.refs_0_, ...), custom_call_target="tpu_custom_call" | custom-call | tf_op jit(solution)/shard_map/setup/pallas_call | solution.py:38
  66.7 16.2 %all_to_all.70.parts.table.refs_18_ = f32[32,16,128]{2,1,0:T(8,128)S(1)} all-to-all(f32[32,16,128]{2,1,0:T(8,128)S(1)} %get-tuple-element.82), channel_id=1, replica_groups=mesh['gx'=4,'gy'=8] {'gx','gy'}, dimensions={0} | all-to-all | bytes 524288 | tf_op jit(solution)/shard_map/all_to_all | solution.py:868
  82.8 1.0 point_first.3
  83.8 10.1 %all_to_all.71.parts.refs_21_ = f32[32,8,128]{2,1,0:T(8,128)S(1)} all-to-all(f32[32,8,128]{2,1,0:T(8,128)S(1)} %get-tuple-element.84), channel_id=1, replica_groups=mesh['gx'=4,'gy'=8] {'gx','gy'}, dimensions={0} | all-to-all | bytes 262144 | tf_op jit(solution)/shard_map/all_to_all | solution.py:868
  94.0 1.2 point_middle.3
  95.2 10.0 %all_to_all.72.parts = f32[32,8,128]{2,1,0:T(8,128)S(1)} all-to-all(f32[32,8,128]{2,1,0:T(8,128)S(1)} %get-tuple-element.87), channel_id=1, replica_groups=mesh['gx'=4,'gy'=8] {'gx','gy'}, dimensions={0} | all-to-all | bytes 262144 | tf_op jit(solution)/shard_map/all_to_all | solution.py:868
  105.1 1.0 point_last.3
  106.1 10.0 %all_to_all.73.refs_17_ = f32[32,8,128]{2,1,0:T(8,128)S(1)} all-to-all(f32[32,8,128]{2,1,0:T(8,128)S(1)} %get-tuple-element.89), channel_id=1, replica_groups=mesh['gx'=4,'gy'=8] {'gx','gy'}, dimensions={0} | all-to-all | bytes 262144 | tf_op jit(solution)/shard_map/all_to_all | solution.py:868
  116.1 14.5 %step.3 = (f32[2,20,64,128]{3,2,1,0:T(8,128)S(1)}, f32[2,20,64,128]{3,2,1,0:T(8,128)S(1)}, f32[8,128]{1,0:T(8,128)S(1)}, f32[2,20,64,128]{3,2,1,0:T(8,128)S(1)},...) custom-call(s32[6]{0:T(128)S(1)} %stack.51.place.refs_0_, ...), custom_call_target="tpu_custom_call" | custom-call | tf_op jit(solution)/shard_map/step/pallas_call | solution.py:38
  130.6 10.0 %all_to_all.74.parts = f32[32,8,128]{2,1,0:T(8,128)S(1)} all-to-all(f32[32,8,128]{2,1,0:T(8,128)S(1)} %get-tuple-element.97), channel_id=1, replica_groups=mesh['gx'=4,'gy'=8] {'gx','gy'}, dimensions={0} | all-to-all | bytes 262144 | tf_op jit(solution)/shard_map/all_to_all | solution.py:868
  140.6 1.0 point_first.4
  141.5 10.0 %all_to_all.75.parts.refs_21_ = f32[32,8,128]{2,1,0:T(8,128)S(1)} all-to-all(f32[32,8,128]{2,1,0:T(8,128)S(1)} %get-tuple-element.99), channel_id=1, replica_groups=mesh['gx'=4,'gy'=8] {'gx','gy'}, dimensions={0} | all-to-all | bytes 262144 | tf_op jit(solution)/shard_map/all_to_all | solution.py:868
  151.5 1.2 point_middle.4
  152.7 10.0 %all_to_all.76.parts = f32[32,8,128]{2,1,0:T(8,128)S(1)} all-to-all(f32[32,8,128]{2,1,0:T(8,128)S(1)} %get-tuple-element.102), channel_id=1, replica_groups=mesh['gx'=4,'gy'=8] {'gx','gy'}, dimensions={0} | all-to-all | bytes 262144 | tf_op jit(solution)/shard_map/all_to_all | solution.py:868
  162.7 1.0 point_last.4
  163.6 10.0 %all_to_all.77.refs_17_ = f32[32,8,128]{2,1,0:T(8,128)S(1)} all-to-all(f32[32,8,128]{2,1,0:T(8,128)S(1)} %get-tuple-element.104), channel_id=1, replica_groups=mesh['gx'=4,'gy'=8] {'gx','gy'}, dimensions={0} | all-to-all | bytes 262144 | tf_op jit(solution)/shard_map/all_to_all | solution.py:868
  173.6 15.0 %step.4 = (f32[2,20,64,128]{3,2,1,0:T(8,128)S(1)}, f32[2,20,64,128]{3,2,1,0:T(8,128)S(1)}, f32[8,128]{1,0:T(8,128)S(1)}, f32[2,20,64,128]{3,2,1,0:T(8,128)S(1)},...) custom-call(s32[6]{0:T(128)S(1)} %stack.51.place.refs_0_, ...), custom_call_target="tpu_custom_call" | custom-call | tf_op jit(solution)/shard_map/step/pallas_call | solution.py:38
  188.6 10.0 %all_to_all.78.parts = f32[32,8,128]{2,1,0:T(8,128)S(1)} all-to-all(f32[32,8,128]{2,1,0:T(8,128)S(1)} %get-tuple-element.114), channel_id=1, replica_groups=mesh['gx'=4,'gy'=8] {'gx','gy'}, dimensions={0} | all-to-all | bytes 262144 | tf_op jit(solution)/shard_map/all_to_all | solution.py:868
  198.6 1.0 point_first.5
  199.6 10.0 %all_to_all.79.parts.refs_21_ = f32[32,8,128]{2,1,0:T(8,128)S(1)} all-to-all(f32[32,8,128]{2,1,0:T(8,128)S(1)} %get-tuple-element.116), channel_id=1, replica_groups=mesh['gx'=4,'gy'=8] {'gx','gy'}, dimensions={0} | all-to-all | bytes 262144 | tf_op jit(solution)/shard_map/all_to_all | solution.py:868
  209.6 1.2 point_middle.5
  210.7 10.0 %all_to_all.80.parts = f32[32,8,128]{2,1,0:T(8,128)S(1)} all-to-all(f32[32,8,128]{2,1,0:T(8,128)S(1)} %get-tuple-element.119), channel_id=1, replica_groups=mesh['gx'=4,'gy'=8] {'gx','gy'}, dimensions={0} | all-to-all | bytes 262144 | tf_op jit(solution)/shard_map/all_to_all | solution.py:868
  220.7 1.0 point_last.5
  221.7 10.0 %all_to_all.81.refs_17_ = f32[32,8,128]{2,1,0:T(8,128)S(1)} all-to-all(f32[32,8,128]{2,1,0:T(8,128)S(1)} %get-tuple-element.121), channel_id=1, replica_groups=mesh['gx'=4,'gy'=8] {'gx','gy'}, dimensions={0} | all-to-all | bytes 262144 | tf_op jit(solution)/shard_map/all_to_all | solution.py:868
  231.7 9.8 %step.5 = (f32[2,20,64,128]{3,2,1,0:T(8,128)}, f32[2,20,64,128]{3,2,1,0:T(8,128)S(1)}, f32[8,128]{1,0:T(8,128)S(1)}, f32[8,128]{1,0:T(8,128)}, f32[32,8,128]{2,1,0:T(8,128)S(1)}) custom-call(s32[6]{0:T(128)S(1)} %stack.51.place.refs_0_, f32[20,64,128]{2,1,0:T(8,128)S(1)} %get-tuple-element.66.refs_1_.g0, f32[20,64,128]{2,1,0:T(8,128)S(1)} %get-tuple-element.67.refs_2_.s0, ...), custom_call_target="tpu_custom_call" | custom-call | tf_op jit(solution)/shard_map/step/pallas_call | solution.py:38
  241.5 10.0 %all_to_all.82.dots = f32[32,8,128]{2,1,0:T(8,128)S(1)} all-to-all(f32[32,8,128]{2,1,0:T(8,128)S(1)} %get-tuple-element.125), channel_id=1, replica_groups=mesh['gx'=4,'gy'=8] {'gx','gy'}, dimensions={0} | all-to-all | bytes 262144 | tf_op jit(solution)/shard_map/all_to_all | solution.py:868
  251.4 4.2 %final.1 = f32[4,20,16,128]{3,2,1,0:T(8,128)S(1)} custom-call(f32[20,64,128]{2,1,0:T(8,128)S(1)} %get-tuple-element.66.refs_1_.g0, f32[20,64,128]{2,1,0:T(8,128)S(1)} %get-tuple-element.67.refs_2_.s0, f32[20,64,128]{2,1,0:T(8,128)S(1)} %get-tuple-element.68.refs_3_.i0, f32[21,64,128]{2,1,0:T(8,128)S(1)} %get-tuple-element.69.refs_4_.f0, ...), custom_call_target="tpu_custom_call" | custom-call | tf_op jit(solution)/shard_map/final/pallas_call | solution.py:38
  255.7 12.6 %all_to_all.83.got = f32[4,20,16,128]{3,2,1,0:T(8,128)S(1)} all-to-all(f32[4,20,16,128]{3,2,1,0:T(8,128)S(1)} %final.1), channel_id=1, replica_groups=mesh['gx'=4,'gy'=8] {'gx'}, dimensions={0} | all-to-all | bytes 1310720 | tf_op jit(solution)/shard_map/all_to_all | solution.py:932
  268.3 3.0 %unpack.1 = (f32[2,20,16,128]{3,2,1,0:T(8,128)}, f32[2,20,16,128]{3,2,1,0:T(8,128)}) custom-call(f32[4,20,16,128]{3,2,1,0:T(8,128)S(1)} %all_to_all.83.got), custom_call_target="tpu_custom_call" | custom-call | tf_op jit(solution)/shard_map/unpack/pallas_call | solution.py:38
  (22 shorter events, 0.1 us)
Async XLA Ops:
  1.7 16.0 %copy-start = (f32[20,16,128]{2,1,0:T(8,128)S(1)}, f32[20,16,128]{2,1,0:T(8,128)}, u32[]{:S(2)}) copy-start(f32[20,16,128]{2,1,0:T(8,128)} %param.8) | copy-start | bytes 491524
  1.7 16.0 %copy-start.1 = (f32[20,16,128]{2,1,0:T(8,128)S(1)}, f32[20,16,128]{2,1,0:T(8,128)}, u32[]{:S(2)}) copy-start(f32[20,16,128]{2,1,0:T(8,128)} %param.9) | copy-start | bytes 491524
  1.7 16.0 %copy-start.4 = (f32[16,128]{1,0:T(8,128)S(1)}, f32[16,128]{1,0:T(8,128)}, u32[]{:S(2)}) copy-start(f32[16,128]{1,0:T(8,128)} %param.10) | copy-start | bytes 24580
  1.8 16.0 %copy-start.5 = (f32[16,128]{1,0:T(8,128)S(1)}, f32[16,128]{1,0:T(8,128)}, u32[]{:S(2)}) copy-start(f32[16,128]{1,0:T(8,128)} %param.11) | copy-start | bytes 24580
  1.8 16.0 %copy-start.2 = (s32[16,128]{1,0:T(8,128)S(1)}, s32[16,128]{1,0:T(8,128)}, u32[]{:S(2)}) copy-start(s32[16,128]{1,0:T(8,128)} %param.12) | copy-start | bytes 24580
  1.8 16.0 %copy-start.3 = (s32[16,128]{1,0:T(8,128)S(1)}, s32[16,128]{1,0:T(8,128)}, u32[]{:S(2)}) copy-start(s32[16,128]{1,0:T(8,128)} %param.13) | copy-start | bytes 24580
  14.3 40.5 %collective-permute-start.1 = (f32[28,3,8,128]{3,2,1,0:T(8,128)S(1)}, f32[28,3,8,128]{3,2,1,0:T(8,128)S(1)}, u32[]{:S(2)}, u32[]{:S(2)}) collective-permute-start(f32[28,3,8,128]{3,2,1,0:T(8,128)S(1)} %pack.4), channel_id=1, source_target_pairs={{0,1},{1,2},{2,3},{3,4},{4,5},{5,6},{6,7},{8,9},{9,10},{10,11},{11... | collective-permute-start | bytes 1032200 | tf_op jit(solution)/shard_map/ppermute | solution.py:849
  28.4 26.3 %collective-permute-start.2 = (f32[28,3,8,128]{3,2,1,0:T(8,128)S(1)}, f32[28,3,8,128]{3,2,1,0:T(8,128)S(1)}, u32[]{:S(2)}, u32[]{:S(2)}) collective-permute-start(f32[28,3,8,128]{3,2,1,0:T(8,128)S(1)} %pack.5), channel_id=1, source_target_pairs={{0,1},{1,2},{2,3},{3,4},{4,5},{5,6},{6,7},{8,9},{9,10},{10,11},{11... | collective-permute-start | bytes 1032200 | tf_op jit(solution)/shard_map/ppermute | solution.py:849
  42.5 12.3 %collective-permute-start = (f32[28,3,8,128]{3,2,1,0:T(8,128)S(1)}, f32[28,3,8,128]{3,2,1,0:T(8,128)S(1)}, u32[]{:S(2)}, u32[]{:S(2)}) collective-permute-start(f32[28,3,8,128]{3,2,1,0:T(8,128)S(1)} %pack.3), channel_id=1, source_target_pairs={{0,1},{1,2},{2,3},{3,4},{4,5},{5,6},{6,7},{8,9},{9,10},{10,11},{11... | collective-permute-start | bytes 1032200 | tf_op jit(solution)/shard_map/ppermute | solution.py:849
  45.9 5.9 %collective-permute-start.4 = (f32[3,16,128]{2,1,0:T(8,128)S(1)}, f32[3,16,128]{2,1,0:T(8,128)S(1)}, u32[]{:S(2)}, u32[]{:S(2)}) collective-permute-start(f32[3,16,128]{2,1,0:T(8,128)S(1)} %pad_maximum_fusion.1.rest_8_), channel_id=1, source_target_pairs={{1,0},{2,1},{3,2},{4,3},{5,4},{6,5},{7,6},{9,8},{10,9},{11,10},{12... | collective-permute-start | bytes 73736 | tf_op jit(solution)/shard_map/ppermute | solution.py:832
  47.2 7.5 %collective-permute-start.3 = (f32[3,16,128]{2,1,0:T(8,128)S(1)}, f32[3,16,128]{2,1,0:T(8,128)S(1)}, u32[]{:S(2)}, u32[]{:S(2)}) collective-permute-start(f32[3,16,128]{2,1,0:T(8,128)S(1)} %pad_maximum_fusion.1.rest_8_), channel_id=1, source_target_pairs={{0,1},{1,2},{2,3},{3,4},{4,5},{5,6},{6,7},{8,9},{9,10},{10,11},{11... | collective-permute-start | bytes 73736 | tf_op jit(solution)/shard_map/ppermute | solution.py:831

commit v3 on v2

--- a/solution.py
+++ b/solution.py
@@ -56,10 +56,11 @@
         self.groups = self.rows // 8
         self.slots = cy // REACH
         self.packed = -(-self.groups // self.slots)
-        self.planes = 4 * layers + 4
+        self.window = 4 * layers + 4
+        self.planes = self.window + 6
         self.parts = -(-2 * ngx // 8) * 8
         self.piece = self.planes // PIECES
-        assert self.piece * PIECES == self.planes and self.piece >= layers + 4
+        assert self.piece * PIECES == self.planes and self.piece >= layers + 10
 
 
 def loop(lo, hi, step, init, by=UNROLL):
@@ -204,12 +205,12 @@
     return (lane >= d.halo) & (lane < d.halo + d.strip)
 
 
-def segment_acc(d, ids_ref, fetch, count):
+def segment_acc(d, ids_row, fetch, count):
     cy = d.cy
     wanted = lax.broadcasted_iota(jnp.int32, (cy, cy), 0).astype(F32)
     acc = [jnp.zeros((cy, cy), F32) for _ in range(count)]
     for r in range(d.cx):
-        hit = ids_ref[r : r + 1, :] == wanted
+        hit = ids_row(r) == wanted
         for t in range(count):
             acc[t] = acc[t] + jnp.where(hit, fetch(t, r), 0.0)
     return acc
@@ -224,7 +225,7 @@
             part = turn(e_ref[v, g * d.cx : (g + 1) * d.cx, :], shift, 1)
             out = jnp.where(lane // d.strip == g, part, out)
         pack[v] = out
-    acc = segment_acc(d, strip_ids, lambda t, r: pack[t, r : r + 1, :], 2)
+    acc = segment_acc(d, lambda r: strip_ids[r : r + 1, :], lambda t, r: pack[t, r : r + 1, :], 2)
     for v in range(2):
         sums = acc[v].T.reshape(d.ngx, d.strip, d.cy).sum(axis=1)
         chunk[v * d.ngx : (v + 1) * d.ngx, :] = sums
@@ -305,7 +306,7 @@
         out[i] = value
 
 
-def pack_kernel(d, place, gathered, out):
+def pack_planes(d, place, gathered, count, put):
     first = place[3]
 
     def body(p, c):
@@ -321,33 +322,41 @@
                 x = turn(x, lax.rem(REACH * s - first + d.cy, d.cy), 1)
                 keep = (lane >= REACH * s) & (lane < REACH * (s + 1))
                 value = jnp.where(keep, x, value)
-            out[p, o] = value
+            put(p * d.packed + o, value)
         return c
 
-    loop(0, d.piece, body, 0)
+    loop(0, count, body, 0)
+
+
+def pack_kernel(d, count, place, *refs):
+    *pieces, out = refs
+    for t, piece in enumerate(pieces):
+        def put(at, value, t=t):
+            out[t * d.piece * d.packed + at] = value
+        pack_planes(d, place, piece, count, put)
 
 
 def segments(d):
     n0, out = d.layers, []
     for piece in range(PIECES):
-        at, end = piece * d.piece, (piece + 1) * d.piece
+        at, end = piece * d.piece, min((piece + 1) * d.piece, d.window)
         while at < end:
             part = min(at // n0, 2)
-            stop = min(end, (part + 1) * n0 if part < 2 else d.planes)
+            stop = min(end, (part + 1) * n0 if part < 2 else d.window)
             out.append((piece, at - piece * d.piece, stop - at, part if part < 2 else None, at - part * n0))
             at = stop
     return out
 
 
 def setup_kernel(d, place, *rest):
-    all_gathered, all_packed, rest = rest[:PIECES], rest[PIECES : 2 * PIECES], rest[2 * PIECES :]
-    left, right, mine = rest[:3]
-    rest = rest[3:]
-    (f, g0, s0, i0, f0, g1, s1, i1, f1, low, blk, strip_ids) = rest[:12]
-    (u0, r1, u1, r2, u2, big) = rest[12:18]
-    (win, chunk, e2, pack, mu0, fw0, mu1, fw1, mu2, fw2) = rest[18:]
+    all_gathered, bulk, last_ref, rest = rest[:PIECES], rest[PIECES], rest[PIECES + 1], rest[PIECES + 2 :]
+    (f, g0, s0, i0, f0, g1, s1, i1, f1, low, strip_ids) = rest[:11]
+    (u0, r1, u1, r2, u2, big) = rest[11:17]
+    (win, chunk, e2, pack, mu0, fw0, mu1, fw1, mu2, fw2) = rest[17:]
     n0, n1, rows, cy, cx = d.layers, d.layers // 2, d.rows, d.cy, d.cx
-    gx, off, is_left = place[1], place[4], place[5]
+    off, is_left = place[4], place[5]
+    if d.parts > 2 * d.ngx:
+        chunk[...] = jnp.zeros(chunk.shape, F32)
 
     def window(gathered, packed, p, put):
         lane = lanes((8, cy))
@@ -359,7 +368,7 @@
             block, at = rg * 8 // cx, rg * 8 % cx
             mid = turn(gathered[block, p, at : at + 8, :], off_own, 1)
             o, s = rg // d.slots, rg % d.slots
-            side = turn(packed[p, o], lax.rem(lo - REACH * s + 2 * cy, cy), 1)
+            side = turn(packed[p * d.packed + o], lax.rem(lo - REACH * s + 2 * cy, cy), 1)
             put(slice(rg * 8, rg * 8 + 8), jnp.where(own, mid, jnp.where(near, side, 0.0)))
 
     for piece, first, count, v, there in segments(d):
@@ -369,13 +378,11 @@
                     win[there + t, at, :] = value
                 else:
                     f[v, there + t, at, :] = value
-            window(all_gathered[piece], all_packed[piece], first + t, put)
+            packed = last_ref if piece == PIECES - 1 else bulk.at[pl.ds(piece * d.piece * d.packed, d.piece * d.packed)]
+            window(all_gathered[piece], packed, first + t, put)
             return c
 
         loop(0, count, fill, 0)
-
-    gathered = all_gathered[PIECES - 1]
-    base = d.planes - d.piece
 
     cpl, frc, msk = win[2 * n0], win[2 * n0 + 1], win[2 * n0 + 2]
     low[4] = msk
@@ -435,60 +442,13 @@
     low[0] = diag2
     low[2] = 1.0 / diag2
 
-    def column_sum(block):
-        def add(k, t):
-            return t + gathered[block, 3 * n0 + k - base]
-        total = loop(0, n0, add, jnp.zeros((cx, cy), F32))
-        return total * gathered[block, 4 * n0 + 2 - base]
-
-    prev_at, next_at = jnp.maximum(gx - 1, 0), jnp.minimum(gx + 1, d.ngx - 1)
-    has_prev, has_next = (gx > 0).astype(F32), (gx < d.ngx - 1).astype(F32)
-    m, ids, s2 = mine[0], mine[1], mine[2]
-    fr, cp = gathered[gx, 4 * n0 + 1 - base], gathered[gx, 4 * n0 - base]
-    row = lax.broadcasted_iota(jnp.int32, (cx, cy), 0)
     lane = lanes((cx, cy))
-    prev = (gathered[prev_at, 4 * n0 + 2 - base] * has_prev, gathered[prev_at, 4 * n0 + 3 - base], column_sum(prev_at) * has_prev)
-    after = (gathered[next_at, 4 * n0 + 2 - base] * has_next, gathered[next_at, 4 * n0 + 3 - base], column_sum(next_at) * has_next)
-    inside = (row > 0, row < cx - 1, lane > 0, lane < cy - 1)
-
-    def around(t, q):
-        return (
-            jnp.where(inside[0], turn(q, 1, 0), turn(prev[t], 1, 0)),
-            jnp.where(inside[1], turn(q, cx - 1, 0), turn(after[t], cx - 1, 0)),
-            jnp.where(inside[2], turn(q, 1, 1), turn(left[t], 1, 1)),
-            jnp.where(inside[3], turn(q, cy - 1, 1), turn(right[t], cy - 1, 1)),
-        )
-
-    m_d, ids_d, s_d = around(0, m), around(1, ids), around(2, s2)
-    g2b = 4.0 * s2 + m * fr + n0 * (1.0 - m)
-    cb = fr * cp * m
-    blk[0], blk[1], blk[2], blk[7] = g2b, s2, cb, ids
-    weight3, weight4 = g2b, g2b
-    for t in range(4):
-        blk[3 + t] = m_d[t]
-        blk[8 + t] = ids_d[t]
-        weight3 = weight3 - jnp.where(inside[t] & (ids_d[t] == ids), s2 * m_d[t], 0.0)
-        weight4 = weight4 - jnp.where(inside[t], s_d[t] * m, 0.0)
-        blk[15 + t] = jnp.where(inside[t], 0.0, s_d[t] * m)
-    blk[12], blk[13], blk[14] = weight3, cb, weight4
-    chunk[...] = jnp.zeros(chunk.shape, F32)
-    for t in range(7):
-        acc = segment_acc(d, blk.at[7], lambda _, r: blk[12 + t, r : r + 1, :], 1)
-        chunk[d.parts + t : d.parts + t + 1, :] = acc[0].T.sum(axis=0, keepdims=True)
-
     packed_ids = jnp.zeros((cx, cy), F32)
     for g in range(d.ngx):
         part = turn(low[5, g * cx : (g + 1) * cx, :], (d.strip * g - d.halo) % cy, 1)
         packed_ids = jnp.where(lane // d.strip == g, part, packed_ids)
     strip_ids[...] = packed_ids
 
-    def square(k, t):
-        return t + f[0, k] * f[0, k] + f[1, k] * f[1, k]
-
-    total = loop(0, n0, square, nil)
-    total = jnp.where(own_lanes(d, (rows, cy)), total, 0.0)
-    chunk[d.parts + 7 : d.parts + 8, :] = total.sum(axis=0, keepdims=True)
-
     levels = level_set(d, (g0, s0, i0, f0, g1, s1, i1, f1, low), mu0, fw0, mu1, fw1, mu2, fw2)
     for one in levels:
         one.clear_rim()
@@ -496,58 +456,153 @@
     spread_chunk(d, big, chunk)
 
 
-def apply_own(d, place, y, blk, tmp, chunk):
-    me, n, ngy = place[0], d.n, d.ngy
+COLUMN = 9
+
+
+def inside_of(d):
     shape = (d.cx, d.cy)
     row = lax.broadcasted_iota(jnp.int32, shape, 0)
     lane = lanes(shape)
-    inside = (row > 0, row < d.cx - 1, lane > 0, lane < d.cy - 1)
-    at = (
-        jnp.maximum(me - ngy, 0),
-        jnp.minimum(me + ngy, n - 1),
-        jnp.maximum(me - 1, 0),
-        jnp.minimum(me + 1, n - 1),
-    )
-    ids = blk[7].astype(jnp.int32)
-    mine = [y[v, pl.ds(me, 1), :] for v in range(2)]
-    here = [pick(mine[v], ids) for v in range(2)]
+    return (row > 0, row < d.cx - 1, lane > 0, lane < d.cy - 1)
+
+
+def column_kernel(d, place, got, out, table, tmp):
+    n0, cx, cy = d.layers, d.cx, d.cy
+    base = d.planes - d.piece
+    at_spread, at_misc = 3 * n0 - base, 4 * n0 - base
+    inside = inside_of(d)
+    nil = jnp.zeros((cx, cy), F32)
+
+    def sums(g):
+        total = loop(0, n0, lambda k, t: t + got[g, at_spread + k], nil)
+        return total * got[g, at_misc + 2]
+
+    s2_all = [sums(g) for g in range(d.ngx)]
+    table[...] = jnp.zeros(table.shape, F32)
+    for g in range(d.ngx):
+        fr, cp = got[g, at_misc + 1], got[g, at_misc]
+        own = (got[g, at_misc + 2], got[g, at_misc + 3], s2_all[g])
+
+        def around(t):
+            q = own[t]
+            up = (got[g - 1, at_misc + 2 + t] if t < 2 else s2_all[g - 1]) if g > 0 else nil
+            down = (got[g + 1, at_misc + 2 + t] if t < 2 else s2_all[g + 1]) if g + 1 < d.ngx else nil
+            left, right = got[g, at_misc + 4 + t], got[g, at_misc + 7 + t]
+            return (
+                jnp.where(inside[0], turn(q, 1, 0), turn(up, 1, 0)),
+                jnp.where(inside[1], turn(q, cx - 1, 0), turn(down, cx - 1, 0)),
+                jnp.where(inside[2], turn(q, 1, 1), turn(left, 1, 1)),
+                jnp.where(inside[3], turn(q, cy - 1, 1), turn(right, cy - 1, 1)),
+            )
+
+        m, ids, s2 = own
+        m_d, ids_d, s_d = around(0), around(1), around(2)
+        g2 = 4.0 * s2 + m * fr + n0 * (1.0 - m)
+        cross = fr * cp * m
+        at = slice(g * cx, (g + 1) * cx)
+        out[0, at, :], out[1, at, :], out[2, at, :], out[3, at, :] = g2, s2, cross, ids
+        weight3, weight4 = g2, g2
+        for t in range(4):
+            out[4 + t, at, :] = m_d[t] * (1.0 + ids_d[t])
+            weight3 = weight3 - jnp.where(inside[t] & (ids_d[t] == ids), s2 * m_d[t], 0.0)
+            weight4 = weight4 - jnp.where(inside[t], s_d[t] * m, 0.0)
+            tmp[3 + t] = jnp.where(inside[t], 0.0, s_d[t] * m)
+        tmp[0], tmp[1], tmp[2] = weight3, cross, weight4
+        ids_row = lambda r: out[3, g * cx + r : g * cx + r + 1, :]
+        acc = segment_acc(d, ids_row, lambda _, r: tmp[0, r : r + 1, :], 1)
+        out[8, at, :] = jnp.broadcast_to(acc[0].T.sum(axis=0, keepdims=True), (cx, cy))
+
+        @pl.when(place[1] == g)
+        def _():
+            def one(t, c):
+                acc = segment_acc(d, ids_row, lambda _, r: tmp[1 + t, r : r + 1, :], 1)
+                table[pl.ds(2 + t, 1), :] = acc[0].T.sum(axis=0, keepdims=True)
+                return c
+
+            loop(0, 6, one, 0, 1)
+
+
+def apply_block(d, cols, pos, g, rows, tmp, inside):
+    at = pl.ds(pl.multiple_of(g * d.cx, d.cx), d.cx)
+    shape = (d.cx, d.cy)
+    ids = cols[pos, 3, at, :].astype(jnp.int32)
+    here = [pick(rows[0][v], ids) for v in range(2)]
     side = [jnp.zeros(shape, F32), jnp.zeros(shape, F32)]
     for t in range(4):
-        ids_t = blk[8 + t].astype(jnp.int32)
-        for v in range(2):
-            outer = pick(y[v, pl.ds(at[t], 1), :], ids_t)
-            value = jnp.where(inside[t], pick(mine[v], ids_t), outer)
-            side[v] = side[v] + blk[3 + t] * value
+        code = cols[pos, 4 + t, at, :].astype(jnp.int32) - 1
+        live = code >= 0
+        code = jnp.maximum(code, 0)
+        for v in range(2):
+            value = jnp.where(inside[t], pick(rows[0][v], code), pick(rows[1 + t][v], code))
+            side[v] = side[v] + jnp.where(live, value, 0.0)
+    g2, s2, cross = cols[pos, 0, at, :], cols[pos, 1, at, :], cols[pos, 2, at, :]
     for v in range(2):
-        tmp[v] = blk[0] * here[v] + blk[2] * here[1 - v] - blk[1] * side[v]
-    acc = segment_acc(d, blk.at[7], lambda t, r: tmp[t, r : r + 1, :], 2)
-    for v in range(2):
-        chunk[v : v + 1, :] = acc[v].T.sum(axis=0, keepdims=True)
-
-
-def point_first(d, place, parts, table, blk, dots, y, r3, big, tmp, chunk):
-    n, ngx, ngy = d.n, d.ngx, d.ngy
+        tmp[v] = g2 * here[v] + cross * here[1 - v] - s2 * side[v]
+    acc = segment_acc(
+        d,
+        lambda r: cols[pos, 3, pl.ds(g * d.cx + r, 1), :],
+        lambda t, r: tmp[t, r : r + 1, :],
+        2,
+    )
+    return [acc[v].T.sum(axis=0, keepdims=True) for v in range(2)]
+
+
+def diagonal(d, cols, pos, g):
+    x = cols[pos, 8, pl.ds(g * d.cx, 1), :]
+    return jnp.where(x == 0.0, 1.0, x)
+
+
+def clip(x, top):
+    return jnp.clip(x, 0, top - 1)
+
+
+def point_first(d, step, place, parts, extra, *rest):
+    if step == 0:
+        near, column, opposite, far, cols, r3, big, tmp, chunk = rest
+        at_near = jnp.where(place[5] == 1, 0, 2)
+
+        def stack(p, c):
+            cols[1, p], cols[3, p] = column[p], far[p]
+            cols[at_near, p], cols[2 - at_near, p] = near[p], opposite[p]
+            return c
+
+        loop(0, COLUMN, stack, 0)
+    else:
+        cols, r3, big, tmp, chunk = rest
+    ngx, ngy = d.ngx, d.ngy
     for v in range(2):
         for g in range(ngx):
             total = parts[0:ngy, v * ngx + g, :]
             for i in range(1, ngx):
                 total = total + parts[i * ngy : (i + 1) * ngy, v * ngx + g, :]
             r3[v, g * ngy : (g + 1) * ngy, :] = total
-    diag = table[:, d.parts, :]
+    gx, gy = place[1], place[2]
+    up, down = clip(gx - 1, ngx), clip(gx + 1, ngx)
+    spots = (
+        (1, gx, gy),
+        (1, up, gy),
+        (1, down, gy),
+        (0, gx, clip(gy - 1, ngy)),
+        (2, gx, clip(gy + 1, ngy)),
+    )
+    right, diag, rows = [], [], []
+    for pos, g, c in spots:
+        right.append([r3[v, pl.ds(g * ngy + c, 1), :] for v in range(2)])
+        diag.append(diagonal(d, cols, pos, g))
+        rows.append([POINT_WEIGHT * right[-1][v] / diag[-1] for v in range(2)])
+    image = apply_block(d, cols, 1, gx, rows, tmp, inside_of(d))
+    count = chunk.shape[0]
+    chunk[2:count, :] = extra[2:count, :]
     for v in range(2):
-        y[v] = POINT_WEIGHT * r3[v] / diag
-    chunk[2:8, :] = dots[2:8, :]
-    apply_own(d, place, y, blk, tmp, chunk)
+        chunk[v : v + 1, :] = rows[0][v] + POINT_WEIGHT * (right[0][v] - image[v]) / diag[0]
     spread_chunk(d, big, chunk)
 
 
-def point_middle(d, place, parts, table, blk, y_in, r3, y, big, tmp, chunk):
-    n, ngy = d.n, d.ngy
-    base = d.parts
-    diag = table[:, base, :]
-    cross = table[:, base + 1, :]
-    inner = table[:, base + 2, :]
-    sides = [table[:, base + 3 + t, :] for t in range(4)]
+def correct_columns(d, place, parts, table, r3, cols, low, u2, y3, y4, y5, tmp):
+    n, ngx, ngy = d.n, d.ngx, d.ngy
+    gy, off, is_left = place[2], place[4], place[5]
+    cross, inner = table[:, 2, :], table[:, 3, :]
+    sides = [table[:, 4 + t, :] for t in range(4)]
     shape = (n, d.cy)
 
     def total(x):
@@ -561,7 +616,7 @@
             + turn(values[2], n - 1, 0)
         )
 
-    y2 = [y_in[v] + POINT_WEIGHT * (r3[v] - parts[:, v, :]) / diag for v in range(2)]
+    y2 = [parts[:, v, :] for v in range(2)]
     right = []
     for v in range(2):
         local = total(r3[v] - (inner * y2[v] + cross * y2[1 - v]))
@@ -578,50 +633,87 @@
             for v in range(2)
         ]
     for v in range(2):
-        y[v] = y2[v] + x[v]
-    chunk[...] = jnp.zeros(chunk.shape, F32)
-    apply_own(d, place, y, blk, tmp, chunk)
-    spread_chunk(d, big, chunk)
-
-
-def point_last(d, place, parts, table, blk, y_in, r3, y, big, tmp, chunk):
-    diag = table[:, d.parts, :]
-    for v in range(2):
-        y[v] = y_in[v] + POINT_WEIGHT * (r3[v] - parts[:, v, :]) / diag
-    chunk[...] = jnp.zeros(chunk.shape, F32)
-    apply_own(d, place, y, blk, tmp, chunk)
-    spread_chunk(d, big, chunk)
-
-
-def correct_columns(d, place, parts, table, y_in, r3, y, low, u2):
-    diag = table[:, d.parts, :]
-    for v in range(2):
-        y[v] = y_in[v] + POINT_WEIGHT * (r3[v] - parts[:, v, :]) / diag
-    gy, off, is_left = place[2], place[4], place[5]
-    shape = (d.cx, d.cy)
-    lane = lanes(shape)
+        y3[v] = y2[v] + x[v]
+
+    def column(pos):
+        far = jnp.where(is_left == 1, -2, 2)
+        return gy + jnp.where(pos == 3, far, pos - 1)
+
+    inside = inside_of(d)
+
+    def relax(pos, g, rows, c, q):
+        image = apply_block(d, cols, pos, g, rows, tmp.at[q], inside)
+        diag = diagonal(d, cols, pos, g)
+        at = pl.ds(g * ngy + c, 1)
+        return [
+            rows[0][v] + POINT_WEIGHT * (r3[v, at, :] - image[v]) / diag for v in range(2)
+        ]
+
+    def fourth(b, carry):
+        for q in range(2):
+            pos, g = lax.div(2 * b + q, ngx), lax.rem(2 * b + q, ngx)
+            c = column(pos)
+            get = lambda g, c: [
+                y3[v, pl.ds(clip(g, ngx) * ngy + clip(c, ngy), 1), :] for v in range(2)
+            ]
+            rows = [get(g, c), get(g - 1, c), get(g + 1, c), get(g, c - 1), get(g, c + 1)]
+            new = relax(pos, g, rows, clip(c, ngy), q)
+            for v in range(2):
+                y4[v, pl.ds(pos * ngx + g, 1), :] = new[v]
+        return carry
+
+    def fifth(b, carry):
+        for q in range(2):
+            t, g = lax.div(2 * b + q, ngx), lax.rem(2 * b + q, ngx)
+            pos = t + 1 - is_left
+            west = jnp.where(pos == 0, 3, pos - 1)
+            east = jnp.where(pos == 2, 3, pos + 1)
+            get = lambda g, p: [
+                y4[v, pl.ds(p * ngx + clip(g, ngx), 1), :] for v in range(2)
+            ]
+            rows = [get(g, pos), get(g - 1, pos), get(g + 1, pos), get(g, west), get(g, east)]
+            new = relax(pos, g, rows, clip(column(pos), ngy), q)
+            for v in range(2):
+                y5[v, pl.ds(t * ngx + g, 1), :] = new[v]
+        return carry
+
+    lax.fori_loop(0, 2 * ngx, fourth, 0)
+    lax.fori_loop(0, ngx, fifth, 0)
+
+    block = (d.cx, d.cy)
+    lane = lanes(block)
     own = jnp.where(is_left == 1, (lane >= off).astype(jnp.int32), (lane < d.cy + off).astype(jnp.int32)) == 1
-    other = jnp.where(is_left == 1, jnp.maximum(gy - 1, 0), jnp.minimum(gy + 1, d.ngy - 1))
-    for g in range(d.ngx):
+    for g in range(ngx):
         at = slice(g * d.cx, (g + 1) * d.cx)
         ids = low[5, at, :].astype(jnp.int32)
         for v in range(2):
-            here = pick(y[v, pl.ds(g * d.ngy + gy, 1), :], ids)
-            there = pick(y[v, pl.ds(g * d.ngy + other, 1), :], ids)
+            here = pick(y5[v, pl.ds(is_left * ngx + g, 1), :], ids)
+            there = pick(y5[v, pl.ds((1 - is_left) * ngx + g, 1), :], ids)
             u2[v, 0, at, :] = u2[v, 0, at, :] + jnp.where(own, here, there)
 
 
-def grid_total(d, dots, row):
-    x = dots[:, row, :].sum(axis=0, keepdims=True)
-    return jnp.broadcast_to(x.sum(axis=1, keepdims=True), (1, d.cy))
-
-
-def column_of(d, dots, step):
-    inner = [grid_total(d, dots, 2 + i) for i in range(step + 1)]
-    square = grid_total(d, dots, 3 + step)
+def grid_totals(d, dots, count):
+    x = dots[:, 2, :].sum(axis=0, keepdims=True)
+    lane = lanes((1, d.cy))
+    return [
+        jnp.broadcast_to(
+            jnp.where(lane == t, x, 0.0).sum(axis=1, keepdims=True), (1, d.cy)
+        )
+        for t in range(count)
+    ]
+
+
+def column_of(d, dots, step, norm=None):
+    values = grid_totals(d, dots, step + 2 + (step == 0))
+    if step == 0:
+        square = values[2]
+        norm = jnp.sqrt(square)
+        inner, height = [values[0] / square], values[1] / square
+    else:
+        inner, height = [values[0] / norm] + values[1:-1], values[-1]
     for value in inner:
-        square = square - value * value
-    return inner + [jnp.sqrt(square)]
+        height = height - value * value
+    return inner + [jnp.sqrt(height)], norm
 
 
 def step_kernel(d, step, last, *refs):
@@ -630,17 +722,20 @@
     (place,) = take(1)
     coefs = take(9)
     (strip_ids, r_in, u0i, r1i, u1i, r2i, u2i) = take(7)
-    (parts, table, y_in, r3, dots) = take(5)
+    (parts, table, r3, cols) = take(4)
+    norm_in = take(1)[0] if step > 1 else None
     olds_v = take(step)
     olds_z = take(step)
-    (v_out, z_out, col) = take(3)
+    if step:
+        (v_out, col) = take(2)
+    (z_out,) = take(1)
     if last:
         (dots_out, big) = take(2)
         w = take(1)[0]
         u0n = None
     else:
         (w, u0n, r1n, u1n, r2n, u2n, dots_out, big) = take(8)
-    (u0, u1, u2, y, chunk, e2, pack, mu0, fw0, mu1, fw1, mu2, fw2) = take(13)
+    (u0, u1, u2, y3, y4, y5, tmp, chunk, e2, pack, mu0, fw0, mu1, fw1, mu2, fw2) = take(16)
     low = coefs[8]
     levels = level_set(d, coefs, mu0, fw0, mu1, fw1, mu2, fw2)
     for one in levels:
@@ -649,36 +744,40 @@
 
     for v in range(2):
         u2[v, 0] = u2i[v, 0]
-    correct_columns(d, place, parts, table, y_in, r3, y, low, u2)
+    correct_columns(d, place, parts, table, r3, cols, low, u2, y3, y4, y5, tmp)
+    if not last and d.parts > 2 * d.ngx:
+        chunk[...] = jnp.zeros(chunk.shape, F32)
 
     ascend(d, levels, r_in, u0, u0i, r1i, u1, u1i, r2i, u2)
 
-    if step == 0:
-        norm = jnp.sqrt(grid_total(d, table, d.parts + 7))
-        inner, height = [], norm
-        col[...] = jnp.broadcast_to(norm, col.shape)
-    else:
-        column = column_of(d, dots, step - 1)
-        inner, height = column[:-1], column[-1]
-        for t, value in enumerate(column):
+    l0 = levels[0]
+    if step:
+        norm = norm_in[step : step + 1, :] if step > 1 else None
+        column, norm = column_of(d, parts, step - 1, norm)
+        height = column[-1]
+        if step == 1:
+            inner, scale = [column[0]], 1.0 / (height * norm)
+        else:
+            inner, scale = [column[0] / norm] + column[1:-1], 1.0 / height
+        for t, value in enumerate(column + [norm]):
             col[t : t + 1, :] = value
-    scale = 1.0 / height
-    l0 = levels[0]
 
     def scaled(k, c):
         for v in range(2):
-            vec, z = r_in[v, k], u0[v, k]
-            for t in range(step):
-                vec = vec - inner[t] * olds_v[t][v, k]
-                z = z - inner[t] * olds_z[t][v, k]
-            v_out[v, k] = vec * scale
-            z = z * scale
+            z = u0[v, k]
+            if step:
+                vec = r_in[v, k]
+                for t in range(step):
+                    vec = vec - inner[t] * olds_v[t][v, k]
+                    z = z - inner[t] * olds_z[t][v, k]
+                v_out[v, k] = vec * scale
+                z = z * scale
             z_out[v, k] = z
             l0.put_masked(v, k, z)
         return c
 
     loop(0, n0, scaled, 0)
-    basis = list(olds_v) + [v_out]
+    basis = list(olds_v) + [v_out if step else r_in]
 
     def image(k, acc, bottom=False):
         acc = list(acc)
@@ -687,16 +786,22 @@
             w[v, k] = value
             for t, vec in enumerate(basis):
                 acc[t] = acc[t] + vec[v, k] * value
-            acc[-1] = acc[-1] + value * value
+            acc[step + 1] = acc[step + 1] + value * value
+            if step == 0:
+                acc[2] = acc[2] + r_in[v, k] * r_in[v, k]
         return tuple(acc)
 
     nil = jnp.zeros((d.rows, d.cy), F32)
-    acc = image(0, (nil,) * (step + 2), True)
+    acc = image(0, (nil,) * (step + 2 + (step == 0)), True)
     acc = loop(1, n0, image, acc)
     own = own_lanes(d, (d.rows, d.cy))
+    lane = lanes((1, d.cy))
+    row = jnp.zeros((1, d.cy), F32)
+    for t, value in enumerate(acc):
+        value = jnp.where(own, value, 0.0).sum(axis=0, keepdims=True)
+        row = jnp.where(lane == t, value.sum(axis=1, keepdims=True), row)
     dots_out[...] = jnp.zeros(dots_out.shape, F32)
-    for t in range(step + 2):
-        dots_out[2 + t : 3 + t, :] = jnp.where(own, acc[t], 0.0).sum(axis=0, keepdims=True)
+    dots_out[2:3, :] = row
     if last:
         spread_chunk(d, big, dots_out)
     else:
@@ -729,19 +834,20 @@
 
 
 def final_kernel(d, g0, s0, i0, f0, low, f, dots, *refs):
-    cols, zs = refs[:ITERS], refs[ITERS : 2 * ITERS]
-    out, x, res, mu0 = refs[2 * ITERS :]
+    cols, zs = refs[: ITERS - 1], refs[ITERS - 1 : 2 * ITERS - 1]
+    out, x, res, mu0 = refs[2 * ITERS - 1 :]
     n0 = d.layers
-    norm = cols[0][0:1, :]
-    nil = jnp.zeros_like(norm)
+    nil = jnp.zeros((1, d.cy), F32)
     columns = []
+    norm = cols[0][2:3, :]
     for j in range(ITERS):
         if j + 1 < ITERS:
-            column = [cols[j + 1][t : t + 1, :] for t in range(j + 2)]
+            column = [cols[j][t : t + 1, :] for t in range(j + 2)]
         else:
-            column = column_of(d, dots, j)
+            column, _ = column_of(d, dots, j, norm)
         columns.append(column + [nil] * (ITERS - 1 - j))
     weights = least_squares(columns, norm)
+    weights[0] = weights[0] / norm
     l0 = Level(d, n0, g0, s0, i0, f0, low.at[3], low.at[4], mu0, None)
     l0.clear_rim()
 
@@ -817,115 +923,129 @@
     place = jnp.stack([gx * ngy + gy, gx, gy, first, off, is_left.astype(jnp.int32)]).astype(jnp.int32)
 
     mask_f, ids_f = ice_mask.astype(F32), aggregates.astype(F32)
-    stacked = jnp.concatenate(
-        [
-            forcing.reshape(2 * layers, cx, cy),
-            viscosity,
-            spread,
-            jnp.stack([coupling, friction, mask_f, ids_f]),
+    mine = jnp.stack([mask_f, ids_f, spread.sum(axis=0) * mask_f])
+    shift = lambda by: [(i, i + by) for i in range(ngy) if 0 <= i + by < ngy]
+    left = lax.ppermute(mine, "gy", shift(1))
+    right = lax.ppermute(mine, "gy", shift(-1))
+    planes = [
+        forcing.reshape(2 * layers, cx, cy),
+        viscosity,
+        spread,
+        jnp.stack([coupling, friction, mask_f, ids_f]),
+        left,
+        right,
+    ]
+    pieces, start = [[] for _ in range(PIECES)], 0
+    for part in planes:
+        end = start + part.shape[0]
+        for t in range(PIECES):
+            low, high = max(start, t * d.piece), min(end, (t + 1) * d.piece)
+            if low < high:
+                pieces[t].append(part[low - start : high - start])
+        start = end
+    def sided(by):
+        return [
+            (i * ngy + j, i * ngy + to)
+            for i in range(ngx)
+            for j in range(ngy)
+            for to in [j + by if i < ngx // 2 else j - by]
+            if 0 <= to < ngy
         ]
-    )
-    mine = jnp.stack([mask_f, ids_f, spread.sum(axis=0) * mask_f])
-    east = [(i, i + 1) for i in range(ngy - 1)]
-    west = [(i + 1, i) for i in range(ngy - 1)]
-    left = lax.ppermute(mine, "gy", east)
-    right = lax.ppermute(mine, "gy", west)
-    pairs = []
-    for i in range(ngx):
-        for j in range(ngy):
-            to = j + 1 if i < ngx // 2 else j - 1
-            if 0 <= to < ngy:
-                pairs.append((i * ngy + j, i * ngy + to))
+
     gathered, packed = [], []
     for t in range(PIECES):
-        got = lax.all_gather(stacked[t * d.piece : (t + 1) * d.piece], "gx")
-        (sent,) = call(
-            functools.partial(pack_kernel, d),
-            [(d.piece, d.packed, 8, cy)],
-            [place, got],
-            name="pack",
-        )
+        got = lax.all_gather(jnp.concatenate(pieces[t]), "gx")
         gathered.append(got)
-        packed.append(lax.ppermute(sent, both, pairs))
+        if t >= PIECES - 2:
+            use = gathered[t:] if t == PIECES - 1 else gathered
+            count = d.window - t * d.piece if t == PIECES - 1 else d.piece
+            (sent,) = call(
+                functools.partial(pack_kernel, d, count),
+                [(len(use) * count * d.packed, 8, cy)],
+                [place, *use],
+                name="pack",
+            )
+            packed.append(lax.ppermute(sent, both, sided(1)))
+    column, table_own = call(
+        functools.partial(column_kernel, d),
+        [(COLUMN, d.rows, cy), (8, cy)],
+        [place, gathered[-1]],
+        [(7, cx, cy)],
+        name="column",
+    )
+    near = lax.ppermute(column, both, sided(1))
+    opposite = lax.ppermute(column, both, sided(-1))
+    far = lax.ppermute(column, both, sided(2))
 
     n0, n1, rows = layers, layers // 2, d.rows
     fields = [field(d, n0), field(d, n1), field(d, n1), field(d, 1), field(d, 1)]
     big_shape = lambda count: (d.n, count, cy)
-    wide = d.parts + 8
     state_work = [(2, rows, cy), (2, cx, cy)] + work_shapes(d)
     outs = call(
         functools.partial(setup_kernel, d),
-        [field(d, n0)] + coef_shapes(d) + [(19, cx, cy), (cx, cy)] + fields + [big_shape(wide)],
-        [place, *gathered, *packed, left, right, mine],
-        [(2 * n0 + 4, rows, cy), (wide, cy)] + state_work,
+        [field(d, n0)] + coef_shapes(d) + [(cx, cy)] + fields + [big_shape(d.parts)],
+        [place, *gathered, *packed],
+        [(2 * n0 + 4, rows, cy), (d.parts, cy)] + state_work,
         name="setup",
     )
-    f, coefs, blk, strip_ids, state, big = (
-        outs[0], outs[1:10], outs[10], outs[11], outs[12:17], outs[17],
-    )
+    f, coefs, strip_ids, state, big = outs[0], outs[1:10], outs[10], outs[11:16], outs[16]
 
     def share(x):
         return lax.all_to_all(x, both, 0, 0)
 
-    table = parts = share(big)
-    dots = jnp.zeros((8, cy), F32)
-    vs, zs, cols = [], [], []
+    big, near, opposite, far = lax.optimization_barrier((big, near, opposite, far))
+    parts = share(big)
+    extra = table_own
+    vs, zs, norms = [f], [], []
     pair = (2, d.n, cy)
-    small = [(2, cx, cy), (8, cy)]
     r_in = f
     for step in range(ITERS):
-        y, r3, big = call(
-            functools.partial(point_first, d),
-            [pair, pair, big_shape(8)],
-            [place, parts, table, blk, dots],
-            small,
+        count = 4 if step else 8
+        outs = call(
+            functools.partial(point_first, d, step),
+            ([] if step else [(4, COLUMN, rows, cy)]) + [pair, big_shape(count)],
+            [place, parts, extra] + ([cols] if step else [near, column, opposite, far]),
+            [(2, cx, cy), (count, cy)],
             name="point_first",
         )
-        with_dots = parts = share(big)
-        y, big = call(
-            functools.partial(point_middle, d),
-            [pair, big_shape(8)],
-            [place, parts, table, blk, y, r3],
-            small,
-            name="point_middle",
-        )
+        r3, big = outs[-2:]
         parts = share(big)
-        y, big = call(
-            functools.partial(point_last, d),
-            [pair, big_shape(8)],
-            [place, parts, table, blk, y, r3],
-            small,
-            name="point_last",
-        )
-        parts = share(big)
+        if step == 0:
+            cols, table = outs[0], parts
         last = step + 1 == ITERS
-        outs_shapes = [field(d, n0), field(d, n0), (8, cy)]
+        outs_shapes = [field(d, n0), (8, cy)] if step else []
+        outs_shapes += [field(d, n0)]
         if last:
-            outs_shapes += [(8, cy), big_shape(8)]
+            outs_shapes += [(4, cy), big_shape(4)]
         else:
-            outs_shapes += [field(d, n0)] + fields + [(8, cy), big_shape(d.parts)]
+            outs_shapes += [field(d, n0)] + fields + [(4, cy), big_shape(d.parts)]
         scratch = [field(d, n0)] if last else []
-        scratch += [field(d, n0), field(d, n1), field(d, 1), pair, (d.parts, cy)] + state_work
+        scratch += [field(d, n0), field(d, n1), field(d, 1), pair]
+        scratch += [(2, 4 * ngx, cy), (2, 2 * ngx, cy), (2, 2, cx, cy), (d.parts, cy)] + state_work
         outs = call(
             functools.partial(step_kernel, d, step, last),
             outs_shapes,
-            [place, *coefs, strip_ids, r_in, *state, parts, table, y, r3, with_dots, *vs, *zs],
+            [place, *coefs, strip_ids, r_in, *state, parts, table, r3, cols]
+            + norms[step - 2 : step - 1 if step > 1 else 0]
+            + (vs[:step] + zs),
             scratch,
             name="step",
         )
-        vs.append(outs[0])
-        zs.append(outs[1])
-        cols.append(outs[2])
+        if step:
+            vs.append(outs[0])
+            norms.append(outs[1])
+            outs = outs[2:]
+        zs.append(outs[0])
         if last:
-            dots_all = share(outs[4])
+            dots_all = share(outs[2])
         else:
-            r_in, state, dots = outs[3], outs[4:9], outs[9]
-            parts = share(outs[10])
+            r_in, state, extra = outs[1], outs[2:7], outs[7]
+            parts = share(outs[8])
 
     (out,) = call(
         functools.partial(final_kernel, d),
         [(ngx, 4 * n0 // ngx, cx, cy)],
-        [*coefs[:4], coefs[8], f, dots_all, *cols, *zs],
+        [*coefs[:4], coefs[8], f, dots_all, *norms, *zs],
         [field(d, n0), field(d, n0), (2, n0, rows + 16, cy)],
         name="final",
     )

time: 272 us -> 232 us (0.85)
  blocking collectives: 178 us -> 110 us
  Pallas kernels: 72.1 us -> 92 us
  starting transfers between devices: 16.1 us -> 23.4 us
    all_to_all x13 -> x7, blocking collectives: 136 us -> 68.1 us  [share(): return lax.all_to_all(x, both, 0, 0)]
    pallas_call x18 -> x12, Pallas kernels: 72.1 us -> 92 us  [call(): pl.pallas_call(kernel, out_shape=[jax.ShapeDtypeStruct(s, F32) for s in o...]
    ppermute x5 -> x7, starting transfers between devices: 16.1 us -> 23.4 us  [the longest x2 6.87 us: body(): packed.append(lax.ppermute(sent, both, sided(1)))]
  transfers between devices with their start and end apart: 5 -> 7, of which waited for: 1 -> 1; matrix products, arithmetic and copies ran while one was open for 0% -> 1% of each run, Pallas kernels for 1% -> 8%
where the time goes in v3:
time: 232 us
  blocking collectives  110 us (47%)
  Pallas kernels  92 us (40%)
  starting transfers between devices  23.4 us (10%)
  other arithmetic  2.43 us (1%)
    pallas_call x12, Pallas kernels, call(): pl.pallas_call(kernel, out_shape=[jax.ShapeDtypeStruct(s, F32) for s in o...  92 us
    all_to_all x7, blocking collectives, share(): return lax.all_to_all(x, both, 0, 0)  68.1 us
    all_gather x3, blocking collectives, body(): got = lax.all_gather(jnp.concatenate(pieces[t]), 'gx')  29.5 us
    all_to_all x1, blocking collectives, body(): got = lax.all_to_all(out, 'gx', 0, 0)  12.6 us
    ppermute x2, starting transfers between devices, body(): packed.append(lax.ppermute(sent, both, sided(1)))  6.87 us
    ppermute x1, starting transfers between devices, body(): left = lax.ppermute(mine, 'gy', shift(1))  5.5 us
    ppermute x1, starting transfers between devices, body(): near = lax.ppermute(column, both, sided(1))  4.94 us
  transfers between devices with their start and end apart: 7, of which 1 were waited for; matrix products, arithmetic and copies ran while one was open for 1% of the time, Pallas kernels for 8%

profile of v3, /device:TPU:0, one launch (start us, length us, event | category | flops | bytes accessed | tf_op | source)
XLA Modules:
  0.0 231.5 jit_solution(12721717271932127014)
XLA Ops:
  0.6 0.0 copy-start
  0.6 1.0 fusion
  1.6 0.7 convert_bitcast_fusion
  2.3 0.7 multiply_bitcast_fusion
  3.0 1.3 collective-permute-start.1
  4.3 5.5 %collective-permute-start = (f32[3,16,128]{2,1,0:T(8,128)S(1)}, f32[3,16,128]{2,1,0:T(8,128)S(1)}, u32[]{:S(2)}, u32[]{:S(2)}) collective-permute-start(f32[3,16,128]{2,1,0:T(8,128)S(1)} %pad_maximum_fusion.1), channel_id=1, source_target_pairs={{0,1},{1,2},{2,3},{3,4},{4,5},{5,6},{6,7},{8,9},{9,10},{10,11},{11... | collective-permute-start | bytes 73736 | tf_op jit(solution)/shard_map/ppermute | solution.py:928
  9.8 0.9 slice.9
  10.7 1.0 slice.8
  11.7 10.2 %all-gather = f32[120,16,128]{2,1,0:T(8,128)S(1)} all-gather(f32[30,16,128]{2,1,0:T(8,128)S(1)} %slice.8), channel_id=2, replica_groups=mesh['gx'=4,'gy'=8] {'gx'}, dimensions={0}, use_global_device_ids=true | all-gather | bytes 1228800 | tf_op jit(solution)/shard_map/all_gather | solution.py:957
  21.9 0.0 copy-done
  22.0 9.8 %all-gather.1 = f32[120,16,128]{2,1,0:T(8,128)S(1)} all-gather(f32[30,16,128]{2,1,0:T(8,128)S(1)} %pad_maximum_fusion), channel_id=3, replica_groups=mesh['gx'=4,'gy'=8] {'gx'}, dimensions={0}, use_global_device_ids=true | all-gather | bytes 1228800 | tf_op jit(solution)/shard_map/all_gather | solution.py:957
  31.7 0.1 stack.51.place.refs_0_
  31.8 0.0 copy-start.2
  31.8 2.4 %pack.2 = f32[180,8,128]{2,1,0:T(8,128)S(1)} custom-call(s32[6]{0:T(128)S(1)} %stack.51.place.refs_0_, f32[4,30,16,128]{3,2,1,0:T(8,128)S(1)} %bitcast.27, f32[4,30,16,128]{3,2,1,0:T(8,128)S(1)} %bitcast.29), custom_call_target="tpu_custom_call" | custom-call | tf_op jit(solution)/shard_map/pack/pallas_call | solution.py:38
  34.3 4.3 %collective-permute-start.2 = (f32[180,8,128]{2,1,0:T(8,128)S(1)}, f32[180,8,128]{2,1,0:T(8,128)S(1)}, u32[]{:S(2)}, u32[]{:S(2)}) collective-permute-start(f32[180,8,128]{2,1,0:T(8,128)S(1)} %pack.2), channel_id=1, source_target_pairs={{0,1},{1,2},{2,3},{3,4},{4,5},{5,6},{6,7},{8,9},{9,10},{10,11},{11... | collective-permute-start | bytes 2211848 | tf_op jit(solution)/shard_map/ppermute | solution.py:968
  38.6 0.0 copy-done.3
  38.7 0.0 copy-done.4
  38.7 0.0 collective-permute-done
  38.7 0.0 collective-permute-done.1
  38.8 9.5 %all-gather.2 = f32[120,16,128]{2,1,0:T(8,128)S(1)} all-gather(f32[30,16,128]{2,1,0:T(8,128)S(1)} %constant_dynamic-update-slice_fusion), channel_id=4, replica_groups=mesh['gx'=4,'gy'=8] {'gx'}, dimensions={0}, use_global_device_ids=true | all-gather | bytes 1228800 | tf_op jit(solution)/shard_map/all_gather | solution.py:957
  48.3 1.3 pack.3
  49.6 2.5 %collective-permute-start.3 = (f32[72,8,128]{2,1,0:T(8,128)S(1)}, f32[72,8,128]{2,1,0:T(8,128)S(1)}, u32[]{:S(2)}, u32[]{:S(2)}) collective-permute-start(f32[72,8,128]{2,1,0:T(8,128)S(1)} %pack.3), channel_id=1, source_target_pairs={{0,1},{1,2},{2,3},{3,4},{4,5},{5,6},{6,7},{8,9},{9,10},{10,11},{11... | collective-permute-start | bytes 884744 | tf_op jit(solution)/shard_map/ppermute | solution.py:968
  52.1 2.9 %column.1 = (f32[9,64,128]{2,1,0:T(8,128)S(1)}, f32[8,128]{1,0:T(8,128)S(1)}) custom-call(s32[6]{0:T(128)S(1)} %stack.51.place.refs_0_, f32[4,30,16,128]{3,2,1,0:T(8,128)S(1)} %bitcast.25), custom_call_target="tpu_custom_call" | custom-call | tf_op jit(solution)/shard_map/column/pallas_call | solution.py:38
  55.0 3.5 %collective-permute-start.6 = (f32[9,64,128]{2,1,0:T(8,128)S(1)}, f32[9,64,128]{2,1,0:T(8,128)S(1)}, u32[]{:S(2)}, u32[]{:S(2)}) collective-permute-start(f32[9,64,128]{2,1,0:T(8,128)S(1)} %get-tuple-element.72.rest_1_), channel_id=1, source_target_pairs={{0,2},{1,3},{2,4},{3,5},{4,6},{5,7},{8,10},{9,11},{10,12},{11,13},... | collective-permute-start | bytes 884744 | tf_op jit(solution)/shard_map/ppermute | solution.py:978
  58.5 1.3 collective-permute-start.5
  59.8 4.9 %collective-permute-start.4 = (f32[9,64,128]{2,1,0:T(8,128)S(1)}, f32[9,64,128]{2,1,0:T(8,128)S(1)}, u32[]{:S(2)}, u32[]{:S(2)}) collective-permute-start(f32[9,64,128]{2,1,0:T(8,128)S(1)} %get-tuple-element.72.rest_1_), channel_id=1, source_target_pairs={{0,1},{1,2},{2,3},{3,4},{4,5},{5,6},{6,7},{8,9},{9,10},{10,11},{11... | collective-permute-start | bytes 884744 | tf_op jit(solution)/shard_map/ppermute | solution.py:976
  64.7 0.0 collective-permute-done.3.rest_4_
  64.8 0.0 collective-permute-done.2.rest_3_
  64.8 10.9 %setup.1 = (f32[2,20,64,128]{3,2,1,0:T(8,128)S(1)}, f32[20,64,128]{2,1,0:T(8,128)S(1)}, f32[20,64,128]{2,1,0:T(8,128)S(1)}, f32[20,64,128]{2,1,0:T(8,128)S(1)}, ...) custom-call(s32[6]{0:T(128)S(1)} %stack.51.place.refs_0_, ...), custom_call_target="tpu_custom_call" | custom-call | tf_op jit(solution)/shard_map/setup/pallas_call | solution.py:38
  75.7 0.0 collective-permute-done.6.rest_3_
  75.7 0.0 collective-permute-done.5.rest_2_
  75.7 0.5 collective-permute-done.4.rest_0_
  76.2 10.9 %all_to_all.40.parts = f32[32,8,128]{2,1,0:T(8,128)S(1)} all-to-all(f32[32,8,128]{2,1,0:T(8,128)S(1)} %get-tuple-element.73), channel_id=1, replica_groups=mesh['gx'=4,'gy'=8] {'gx','gy'}, dimensions={0} | all-to-all | bytes 262144 | tf_op jit(solution)/shard_map/all_to_all | solution.py:994
  87.1 1.1 point_first.3
  88.2 10.0 %all_to_all.41.refs_17_.refs_18_ = f32[32,8,128]{2,1,0:T(8,128)S(1)} all-to-all(f32[32,8,128]{2,1,0:T(8,128)S(1)} %get-tuple-element.78), channel_id=1, replica_groups=mesh['gx'=4,'gy'=8] {'gx','gy'}, dimensions={0} | all-to-all | bytes 262144 | tf_op jit(solution)/shard_map/all_to_all | solution.py:994
  98.2 22.7 %step.3 = (f32[2,20,64,128]{3,2,1,0:T(8,128)S(1)}, f32[2,20,64,128]{3,2,1,0:T(8,128)S(1)}, f32[2,20,64,128]{3,2,1,0:T(8,128)S(1)}, f32[2,10,64,128]{3,2,1,0:T(8,...) custom-call(s32[6]{0:T(128)S(1)} %stack.51.place.refs_0_, ...), custom_call_target="tpu_custom_call" | custom-call | tf_op jit(solution)/shard_map/step/pallas_call | solution.py:38
  120.9 10.0 %all_to_all.42.parts = f32[32,8,128]{2,1,0:T(8,128)S(1)} all-to-all(f32[32,8,128]{2,1,0:T(8,128)S(1)} %get-tuple-element.87), channel_id=1, replica_groups=mesh['gx'=4,'gy'=8] {'gx','gy'}, dimensions={0} | all-to-all | bytes 262144 | tf_op jit(solution)/shard_map/all_to_all | solution.py:994
  130.9 1.0 point_first.4
  131.9 9.4 %all_to_all.43.refs_17_ = f32[32,4,128]{2,1,0:T(4,128)S(1)} all-to-all(f32[32,4,128]{2,1,0:T(4,128)S(1)} %get-tuple-element.89), channel_id=1, replica_groups=mesh['gx'=4,'gy'=8] {'gx','gy'}, dimensions={0} | all-to-all | bytes 131072 | tf_op jit(solution)/shard_map/all_to_all | solution.py:994
  141.3 23.3 %step.4 = (f32[2,20,64,128]{3,2,1,0:T(8,128)S(1)}, f32[8,128]{1,0:T(8,128)S(1)}, f32[2,20,64,128]{3,2,1,0:T(8,128)S(1)}, f32[2,20,64,128]{3,2,1,0:T(8,128)S(1)},...) custom-call(s32[6]{0:T(128)S(1)} %stack.51.place.refs_0_, ...), custom_call_target="tpu_custom_call" | custom-call | tf_op jit(solution)/shard_map/step/pallas_call | solution.py:38
  164.6 9.5 %all_to_all.44.parts = f32[32,8,128]{2,1,0:T(8,128)S(1)} all-to-all(f32[32,8,128]{2,1,0:T(8,128)S(1)} %get-tuple-element.98), channel_id=1, replica_groups=mesh['gx'=4,'gy'=8] {'gx','gy'}, dimensions={0} | all-to-all | bytes 262144 | tf_op jit(solution)/shard_map/all_to_all | solution.py:994
  174.1 1.0 point_first.5
  175.1 9.3 %all_to_all.45.refs_17_ = f32[32,4,128]{2,1,0:T(4,128)S(1)} all-to-all(f32[32,4,128]{2,1,0:T(4,128)S(1)} %get-tuple-element.100), channel_id=1, replica_groups=mesh['gx'=4,'gy'=8] {'gx','gy'}, dimensions={0} | all-to-all | bytes 131072 | tf_op jit(solution)/shard_map/all_to_all | solution.py:994
  184.5 18.2 %step.5 = (f32[2,20,64,128]{3,2,1,0:T(8,128)}, f32[8,128]{1,0:T(8,128)S(1)}, f32[2,20,64,128]{3,2,1,0:T(8,128)S(1)}, f32[4,128]{1,0:T(4,128)}, f32[32,4,128]{2,1,0:T(4,128)S(1)}) custom-call(s32[6]{0:T(128)S(1)} %stack.51.place.refs_0_, f32[20,64,128]{2,1,0:T(8,128)S(1)} %get-tuple-element.55.refs_1_.g0, f32[20,64,128]{2,1,0:T(8,128)S(1)} %get-tuple-element.56.refs_2_.s0, ...), custom_call_target="tpu_custom_call" | custom-call | tf_op jit(solution)/shard_map/step/pallas_call | solution.py:38
  202.6 9.0 %all_to_all.46.dots = f32[32,4,128]{2,1,0:T(4,128)S(1)} all-to-all(f32[32,4,128]{2,1,0:T(4,128)S(1)} %get-tuple-element.105), channel_id=1, replica_groups=mesh['gx'=4,'gy'=8] {'gx','gy'}, dimensions={0} | all-to-all | bytes 131072 | tf_op jit(solution)/shard_map/all_to_all | solution.py:994
  211.6 4.4 %final.1 = f32[4,20,16,128]{3,2,1,0:T(8,128)S(1)} custom-call(f32[20,64,128]{2,1,0:T(8,128)S(1)} %get-tuple-element.55.refs_1_.g0, f32[20,64,128]{2,1,0:T(8,128)S(1)} %get-tuple-element.56.refs_2_.s0, f32[20,64,128]{2,1,0:T(8,128)S(1)} %get-tuple-element.57.refs_3_.i0, f32[21,64,128]{2,1,0:T(8,128)S(1)} %get-tuple-element.58.refs_4_.f0, ...), custom_call_target="tpu_custom_call" | custom-call | tf_op jit(solution)/shard_map/final/pallas_call | solution.py:38
  216.0 12.6 %all_to_all.47.got = f32[4,20,16,128]{3,2,1,0:T(8,128)S(1)} all-to-all(f32[4,20,16,128]{3,2,1,0:T(8,128)S(1)} %final.1), channel_id=1, replica_groups=mesh['gx'=4,'gy'=8] {'gx'}, dimensions={0} | all-to-all | bytes 1310720 | tf_op jit(solution)/shard_map/all_to_all | solution.py:1052
  228.6 3.0 %unpack.1 = (f32[2,20,16,128]{3,2,1,0:T(8,128)}, f32[2,20,16,128]{3,2,1,0:T(8,128)}) custom-call(f32[4,20,16,128]{3,2,1,0:T(8,128)S(1)} %all_to_all.47.got), custom_call_target="tpu_custom_call" | custom-call | tf_op jit(solution)/shard_map/unpack/pallas_call | solution.py:38
  (13 shorter events, 0.1 us)
Async XLA Ops:
  0.6 21.3 %copy-start = (f32[20,16,128]{2,1,0:T(8,128)S(1)}, f32[20,16,128]{2,1,0:T(8,128)}, u32[]{:S(2)}) copy-start(f32[20,16,128]{2,1,0:T(8,128)} %param.8) | copy-start | bytes 491524
  3.0 35.7 %collective-permute-start.1 = (f32[3,16,128]{2,1,0:T(8,128)S(1)}, f32[3,16,128]{2,1,0:T(8,128)S(1)}, u32[]{:S(2)}, u32[]{:S(2)}) collective-permute-start(f32[3,16,128]{2,1,0:T(8,128)S(1)} %pad_maximum_fusion.1), channel_id=1, source_target_pairs={{1,0},{2,1},{3,2},{4,3},{5,4},{6,5},{7,6},{9,8},{10,9},{11,10},{12... | collective-permute-start | bytes 73736 | tf_op jit(solution)/shard_map/ppermute | solution.py:929
  4.3 34.4 %collective-permute-start = (f32[3,16,128]{2,1,0:T(8,128)S(1)}, f32[3,16,128]{2,1,0:T(8,128)S(1)}, u32[]{:S(2)}, u32[]{:S(2)}) collective-permute-start(f32[3,16,128]{2,1,0:T(8,128)S(1)} %pad_maximum_fusion.1), channel_id=1, source_target_pairs={{0,1},{1,2},{2,3},{3,4},{4,5},{5,6},{6,7},{8,9},{9,10},{10,11},{11... | collective-permute-start | bytes 73736 | tf_op jit(solution)/shard_map/ppermute | solution.py:928
  31.8 6.8 %copy-start.3 = (f32[16,128]{1,0:T(8,128)S(1)}, f32[16,128]{1,0:T(8,128)}, u32[]{:S(2)}) copy-start(f32[16,128]{1,0:T(8,128)} %param.10) | copy-start | bytes 24580
  31.8 6.8 %copy-start.4 = (f32[16,128]{1,0:T(8,128)S(1)}, f32[16,128]{1,0:T(8,128)}, u32[]{:S(2)}) copy-start(f32[16,128]{1,0:T(8,128)} %param.11) | copy-start | bytes 24580
  31.8 6.9 %copy-start.1 = (s32[16,128]{1,0:T(8,128)S(1)}, s32[16,128]{1,0:T(8,128)}, u32[]{:S(2)}) copy-start(s32[16,128]{1,0:T(8,128)} %param.12) | copy-start | bytes 24580
  31.8 6.9 %copy-start.2 = (s32[16,128]{1,0:T(8,128)S(1)}, s32[16,128]{1,0:T(8,128)}, u32[]{:S(2)}) copy-start(s32[16,128]{1,0:T(8,128)} %param.13) | copy-start | bytes 24580
  34.3 30.5 %collective-permute-start.2 = (f32[180,8,128]{2,1,0:T(8,128)S(1)}, f32[180,8,128]{2,1,0:T(8,128)S(1)}, u32[]{:S(2)}, u32[]{:S(2)}) collective-permute-start(f32[180,8,128]{2,1,0:T(8,128)S(1)} %pack.2), channel_id=1, source_target_pairs={{0,1},{1,2},{2,3},{3,4},{4,5},{5,6},{6,7},{8,9},{9,10},{10,11},{11... | collective-permute-start | bytes 2211848 | tf_op jit(solution)/shard_map/ppermute | solution.py:968
  49.6 15.2 %collective-permute-start.3 = (f32[72,8,128]{2,1,0:T(8,128)S(1)}, f32[72,8,128]{2,1,0:T(8,128)S(1)}, u32[]{:S(2)}, u32[]{:S(2)}) collective-permute-start(f32[72,8,128]{2,1,0:T(8,128)S(1)} %pack.3), channel_id=1, source_target_pairs={{0,1},{1,2},{2,3},{3,4},{4,5},{5,6},{6,7},{8,9},{9,10},{10,11},{11... | collective-permute-start | bytes 884744 | tf_op jit(solution)/shard_map/ppermute | solution.py:968
  55.0 20.7 %collective-permute-start.6 = (f32[9,64,128]{2,1,0:T(8,128)S(1)}, f32[9,64,128]{2,1,0:T(8,128)S(1)}, u32[]{:S(2)}, u32[]{:S(2)}) collective-permute-start(f32[9,64,128]{2,1,0:T(8,128)S(1)} %get-tuple-element.72.rest_1_), channel_id=1, source_target_pairs={{0,2},{1,3},{2,4},{3,5},{4,6},{5,7},{8,10},{9,11},{10,12},{11,13},... | collective-permute-start | bytes 884744 | tf_op jit(solution)/shard_map/ppermute | solution.py:978
  58.5 17.2 %collective-permute-start.5 = (f32[9,64,128]{2,1,0:T(8,128)S(1)}, f32[9,64,128]{2,1,0:T(8,128)S(1)}, u32[]{:S(2)}, u32[]{:S(2)}) collective-permute-start(f32[9,64,128]{2,1,0:T(8,128)S(1)} %get-tuple-element.72.rest_1_), channel_id=1, source_target_pairs={{1,0},{2,1},{3,2},{4,3},{5,4},{6,5},{7,6},{9,8},{10,9},{11,10},{12... | collective-permute-start | bytes 884744 | tf_op jit(solution)/shard_map/ppermute | solution.py:977
  59.8 16.4 %collective-permute-start.4 = (f32[9,64,128]{2,1,0:T(8,128)S(1)}, f32[9,64,128]{2,1,0:T(8,128)S(1)}, u32[]{:S(2)}, u32[]{:S(2)}) collective-permute-start(f32[9,64,128]{2,1,0:T(8,128)S(1)} %get-tuple-element.72.rest_1_), channel_id=1, source_target_pairs={{0,1},{1,2},{2,3},{3,4},{4,5},{5,6},{6,7},{8,9},{9,10},{10,11},{11... | collective-permute-start | bytes 884744 | tf_op jit(solution)/shard_map/ppermute | solution.py:976

commit v4 on v3

--- a/solution.py
+++ b/solution.py
@@ -20,7 +20,7 @@
 
 
 MOST_VMEM = 60 * 1024 * 1024
-UNROLL = 3
+UNROLL = 6
 PIECES = 3
 
 
@@ -63,7 +63,9 @@
         assert self.piece * PIECES == self.planes and self.piece >= layers + 10
 
 
-def loop(lo, hi, step, init, by=UNROLL):
+def loop(lo, hi, step, init, by=None):
+    if by is None:
+        by = UNROLL
     trips = (hi - lo) // by
 
     def trip(t, carry):
@@ -125,7 +127,7 @@
         for v in range(2):
             right = r[v, 0]
             if not first:
-                right = right - self.apply(u, v, 0, True)
+                right = right + self.s[0] * self.beside(v, 0) - self.cross[...] * u[1 - v, 0]
             start.append(right * self.inv[0])
         for v in range(2):
             self.fw[v, 0] = start[v]
@@ -135,7 +137,7 @@
             for v in range(2):
                 right = r[v, k]
                 if not first:
-                    right = right - self.apply(u, v, k)
+                    right = right + self.s[k] * self.beside(v, k)
                 value = (right + self.face[k] * carry[v]) * self.inv[k]
                 self.fw[v, k] = value
                 out.append(value)
@@ -146,7 +148,7 @@
         def store(v, k, value):
             new = LINE_WEIGHT * value
             if not first:
-                new = u[v, k] + new
+                new = (1.0 - LINE_WEIGHT) * u[v, k] + new
             u[v, k] = new
             self.put_masked(v, k, new)
 
@@ -779,22 +781,29 @@
     loop(0, n0, scaled, 0)
     basis = list(olds_v) + [v_out if step else r_in]
 
+    own = own_lanes(d, (8, d.cy))
+
+    def fold(x):
+        total = x[0:8]
+        for t in range(1, d.groups):
+            total = total + x[8 * t : 8 * t + 8]
+        return total
+
     def image(k, acc, bottom=False):
         acc = list(acc)
         for v in range(2):
             value = l0.apply(z_out, v, k, bottom)
             w[v, k] = value
             for t, vec in enumerate(basis):
-                acc[t] = acc[t] + vec[v, k] * value
-            acc[step + 1] = acc[step + 1] + value * value
+                acc[t] = acc[t] + fold(vec[v, k] * value)
+            acc[step + 1] = acc[step + 1] + fold(value * value)
             if step == 0:
-                acc[2] = acc[2] + r_in[v, k] * r_in[v, k]
+                acc[2] = acc[2] + fold(r_in[v, k] * r_in[v, k])
         return tuple(acc)
 
-    nil = jnp.zeros((d.rows, d.cy), F32)
+    nil = jnp.zeros((8, d.cy), F32)
     acc = image(0, (nil,) * (step + 2 + (step == 0)), True)
     acc = loop(1, n0, image, acc)
-    own = own_lanes(d, (d.rows, d.cy))
     lane = lanes((1, d.cy))
     row = jnp.zeros((1, d.cy), F32)
     for t, value in enumerate(acc):

time: 232 us -> 223 us (0.961)
  Pallas kernels: 92 us -> 78.5 us
  waiting for transfers between devices: 0.56 us -> 2.89 us
    pallas_call x12, Pallas kernels: 92 us -> 78.5 us  [call(): pl.pallas_call(kernel, out_shape=[jax.ShapeDtypeStruct(s, F32) for s in o...]
    ppermute x1, waiting for transfers between devices: 0.54 us -> 2.87 us  [body(): near = lax.ppermute(column, both, sided(1))]
  transfers between devices with their start and end apart: 7 -> 7, of which waited for: 1 -> 1; matrix products, arithmetic and copies ran while one was open for 1% -> 1% of each run, Pallas kernels for 8% -> 6%
where the time goes in v4:
time: 223 us; the launch traced here: 222 us
  blocking collectives  112 us (50%)
  Pallas kernels  78.5 us (35%)
  starting transfers between devices  23.4 us (10%)
  waiting for transfers between devices  2.89 us (1%)
  other arithmetic  2.43 us (1%)
    pallas_call x12, Pallas kernels, call(): pl.pallas_call(kernel, out_shape=[jax.ShapeDtypeStruct(s, F32) for s in o...  78.5 us
    all_to_all x7, blocking collectives, share(): return lax.all_to_all(x, both, 0, 0)  69.9 us
    all_gather x3, blocking collectives, body(): got = lax.all_gather(jnp.concatenate(pieces[t]), 'gx')  29.5 us
    all_to_all x1, blocking collectives, body(): got = lax.all_to_all(out, 'gx', 0, 0)  12.6 us
    ppermute x2, starting transfers between devices, body(): packed.append(lax.ppermute(sent, both, sided(1)))  6.87 us
    ppermute x1, starting transfers between devices, body(): left = lax.ppermute(mine, 'gy', shift(1))  5.5 us
    ppermute x1, starting transfers between devices, body(): near = lax.ppermute(column, both, sided(1))  4.94 us
  transfers between devices with their start and end apart: 7, of which 1 were waited for; matrix products, arithmetic and copies ran while one was open for 1% of the time, Pallas kernels for 6%

profile of v4, /device:TPU:0, one launch (start us, length us, event | category | flops | bytes accessed | tf_op | source)
XLA Modules:
  0.0 222.1 jit_solution(6493566761916145550)
XLA Ops:
  0.6 0.0 copy-start
  0.6 1.0 fusion
  1.6 0.7 convert_bitcast_fusion
  2.3 0.7 multiply_bitcast_fusion
  3.0 1.3 collective-permute-start.1
  4.3 5.5 %collective-permute-start = (f32[3,16,128]{2,1,0:T(8,128)S(1)}, f32[3,16,128]{2,1,0:T(8,128)S(1)}, u32[]{:S(2)}, u32[]{:S(2)}) collective-permute-start(f32[3,16,128]{2,1,0:T(8,128)S(1)} %pad_maximum_fusion.1), channel_id=1, source_target_pairs={{0,1},{1,2},{2,3},{3,4},{4,5},{5,6},{6,7},{8,9},{9,10},{10,11},{11... | collective-permute-start | bytes 73736 | tf_op jit(solution)/shard_map/ppermute | solution.py:937
  9.8 0.9 slice.9
  10.7 1.0 slice.8
  11.7 10.2 %all-gather = f32[120,16,128]{2,1,0:T(8,128)S(1)} all-gather(f32[30,16,128]{2,1,0:T(8,128)S(1)} %slice.8), channel_id=2, replica_groups=mesh['gx'=4,'gy'=8] {'gx'}, dimensions={0}, use_global_device_ids=true | all-gather | bytes 1228800 | tf_op jit(solution)/shard_map/all_gather | solution.py:966
  21.9 0.0 copy-done
  22.0 9.8 %all-gather.1 = f32[120,16,128]{2,1,0:T(8,128)S(1)} all-gather(f32[30,16,128]{2,1,0:T(8,128)S(1)} %pad_maximum_fusion), channel_id=3, replica_groups=mesh['gx'=4,'gy'=8] {'gx'}, dimensions={0}, use_global_device_ids=true | all-gather | bytes 1228800 | tf_op jit(solution)/shard_map/all_gather | solution.py:966
  31.7 0.1 stack.51.place.refs_0_
  31.8 0.0 copy-start.2
  31.8 1.8 pack.2
  33.6 4.3 %collective-permute-start.2 = (f32[180,8,128]{2,1,0:T(8,128)S(1)}, f32[180,8,128]{2,1,0:T(8,128)S(1)}, u32[]{:S(2)}, u32[]{:S(2)}) collective-permute-start(f32[180,8,128]{2,1,0:T(8,128)S(1)} %pack.2), channel_id=1, source_target_pairs={{0,1},{1,2},{2,3},{3,4},{4,5},{5,6},{6,7},{8,9},{9,10},{10,11},{11... | collective-permute-start | bytes 2211848 | tf_op jit(solution)/shard_map/ppermute | solution.py:977
  38.0 0.0 copy-done.3
  38.0 0.0 copy-done.4
  38.0 0.0 collective-permute-done
  38.1 0.0 collective-permute-done.1
  38.1 9.5 %all-gather.2 = f32[120,16,128]{2,1,0:T(8,128)S(1)} all-gather(f32[30,16,128]{2,1,0:T(8,128)S(1)} %constant_dynamic-update-slice_fusion), channel_id=4, replica_groups=mesh['gx'=4,'gy'=8] {'gx'}, dimensions={0}, use_global_device_ids=true | all-gather | bytes 1228800 | tf_op jit(solution)/shard_map/all_gather | solution.py:966
  47.6 1.0 pack.3
  48.6 2.5 %collective-permute-start.3 = (f32[72,8,128]{2,1,0:T(8,128)S(1)}, f32[72,8,128]{2,1,0:T(8,128)S(1)}, u32[]{:S(2)}, u32[]{:S(2)}) collective-permute-start(f32[72,8,128]{2,1,0:T(8,128)S(1)} %pack.3), channel_id=1, source_target_pairs={{0,1},{1,2},{2,3},{3,4},{4,5},{5,6},{6,7},{8,9},{9,10},{10,11},{11... | collective-permute-start | bytes 884744 | tf_op jit(solution)/shard_map/ppermute | solution.py:977
  51.2 2.8 %column.1 = (f32[9,64,128]{2,1,0:T(8,128)S(1)}, f32[8,128]{1,0:T(8,128)S(1)}) custom-call(s32[6]{0:T(128)S(1)} %stack.51.place.refs_0_, f32[4,30,16,128]{3,2,1,0:T(8,128)S(1)} %bitcast.25), custom_call_target="tpu_custom_call" | custom-call | tf_op jit(solution)/shard_map/column/pallas_call | solution.py:38
  54.0 3.5 %collective-permute-start.6 = (f32[9,64,128]{2,1,0:T(8,128)S(1)}, f32[9,64,128]{2,1,0:T(8,128)S(1)}, u32[]{:S(2)}, u32[]{:S(2)}) collective-permute-start(f32[9,64,128]{2,1,0:T(8,128)S(1)} %get-tuple-element.72.rest_1_), channel_id=1, source_target_pairs={{0,2},{1,3},{2,4},{3,5},{4,6},{5,7},{8,10},{9,11},{10,12},{11,13},... | collective-permute-start | bytes 884744 | tf_op jit(solution)/shard_map/ppermute | solution.py:987
  57.5 1.3 collective-permute-start.5
  58.8 4.9 %collective-permute-start.4 = (f32[9,64,128]{2,1,0:T(8,128)S(1)}, f32[9,64,128]{2,1,0:T(8,128)S(1)}, u32[]{:S(2)}, u32[]{:S(2)}) collective-permute-start(f32[9,64,128]{2,1,0:T(8,128)S(1)} %get-tuple-element.72.rest_1_), channel_id=1, source_target_pairs={{0,1},{1,2},{2,3},{3,4},{4,5},{5,6},{6,7},{8,9},{9,10},{10,11},{11... | collective-permute-start | bytes 884744 | tf_op jit(solution)/shard_map/ppermute | solution.py:985
  63.7 0.0 collective-permute-done.3.rest_4_
  63.7 0.0 collective-permute-done.2.rest_3_
  63.8 8.6 %setup.1 = (f32[2,20,64,128]{3,2,1,0:T(8,128)S(1)}, f32[20,64,128]{2,1,0:T(8,128)S(1)}, f32[20,64,128]{2,1,0:T(8,128)S(1)}, f32[20,64,128]{2,1,0:T(8,128)S(1)}, ...) custom-call(s32[6]{0:T(128)S(1)} %stack.51.place.refs_0_, ...), custom_call_target="tpu_custom_call" | custom-call | tf_op jit(solution)/shard_map/setup/pallas_call | solution.py:38
  72.3 0.0 collective-permute-done.6.rest_3_
  72.3 0.0 collective-permute-done.5.rest_2_
  72.3 2.9 %collective-permute-done.4.rest_0_ = f32[9,64,128]{2,1,0:T(8,128)S(1)} collective-permute-done((f32[9,64,128]{2,1,0:T(8,128)S(1)}, f32[9,64,128]{2,1,0:T(8,128)S(1)}, u32[]{:S(2)}, u32[]{:S(2)}) %collective-permute-start.4) | collective-permute-done | bytes 294944 | tf_op jit(solution)/shard_map/ppermute | solution.py:985
  75.2 12.7 %all_to_all.40.parts = f32[32,8,128]{2,1,0:T(8,128)S(1)} all-to-all(f32[32,8,128]{2,1,0:T(8,128)S(1)} %get-tuple-element.73), channel_id=1, replica_groups=mesh['gx'=4,'gy'=8] {'gx','gy'}, dimensions={0} | all-to-all | bytes 262144 | tf_op jit(solution)/shard_map/all_to_all | solution.py:1003
  87.9 1.1 point_first.3
  88.9 10.0 %all_to_all.41.refs_17_.refs_18_ = f32[32,8,128]{2,1,0:T(8,128)S(1)} all-to-all(f32[32,8,128]{2,1,0:T(8,128)S(1)} %get-tuple-element.78), channel_id=1, replica_groups=mesh['gx'=4,'gy'=8] {'gx','gy'}, dimensions={0} | all-to-all | bytes 262144 | tf_op jit(solution)/shard_map/all_to_all | solution.py:1003
  98.9 19.7 %step.3 = (f32[2,20,64,128]{3,2,1,0:T(8,128)S(1)}, f32[2,20,64,128]{3,2,1,0:T(8,128)S(1)}, f32[2,20,64,128]{3,2,1,0:T(8,128)S(1)}, f32[2,10,64,128]{3,2,1,0:T(8,...) custom-call(s32[6]{0:T(128)S(1)} %stack.51.place.refs_0_, ...), custom_call_target="tpu_custom_call" | custom-call | tf_op jit(solution)/shard_map/step/pallas_call | solution.py:38
  118.6 10.0 %all_to_all.42.parts = f32[32,8,128]{2,1,0:T(8,128)S(1)} all-to-all(f32[32,8,128]{2,1,0:T(8,128)S(1)} %get-tuple-element.87), channel_id=1, replica_groups=mesh['gx'=4,'gy'=8] {'gx','gy'}, dimensions={0} | all-to-all | bytes 262144 | tf_op jit(solution)/shard_map/all_to_all | solution.py:1003
  128.5 1.0 point_first.4
  129.5 9.4 %all_to_all.43.refs_17_ = f32[32,4,128]{2,1,0:T(4,128)S(1)} all-to-all(f32[32,4,128]{2,1,0:T(4,128)S(1)} %get-tuple-element.89), channel_id=1, replica_groups=mesh['gx'=4,'gy'=8] {'gx','gy'}, dimensions={0} | all-to-all | bytes 131072 | tf_op jit(solution)/shard_map/all_to_all | solution.py:1003
  139.0 19.9 %step.4 = (f32[2,20,64,128]{3,2,1,0:T(8,128)S(1)}, f32[8,128]{1,0:T(8,128)S(1)}, f32[2,20,64,128]{3,2,1,0:T(8,128)S(1)}, f32[2,20,64,128]{3,2,1,0:T(8,128)S(1)},...) custom-call(s32[6]{0:T(128)S(1)} %stack.51.place.refs_0_, ...), custom_call_target="tpu_custom_call" | custom-call | tf_op jit(solution)/shard_map/step/pallas_call | solution.py:38
  158.9 9.5 %all_to_all.44.parts = f32[32,8,128]{2,1,0:T(8,128)S(1)} all-to-all(f32[32,8,128]{2,1,0:T(8,128)S(1)} %get-tuple-element.98), channel_id=1, replica_groups=mesh['gx'=4,'gy'=8] {'gx','gy'}, dimensions={0} | all-to-all | bytes 262144 | tf_op jit(solution)/shard_map/all_to_all | solution.py:1003
  168.4 1.0 point_first.5
  169.4 9.3 %all_to_all.45.refs_17_ = f32[32,4,128]{2,1,0:T(4,128)S(1)} all-to-all(f32[32,4,128]{2,1,0:T(4,128)S(1)} %get-tuple-element.100), channel_id=1, replica_groups=mesh['gx'=4,'gy'=8] {'gx','gy'}, dimensions={0} | all-to-all | bytes 131072 | tf_op jit(solution)/shard_map/all_to_all | solution.py:1003
  178.8 16.1 %step.5 = (f32[2,20,64,128]{3,2,1,0:T(8,128)}, f32[8,128]{1,0:T(8,128)S(1)}, f32[2,20,64,128]{3,2,1,0:T(8,128)S(1)}, f32[4,128]{1,0:T(4,128)}, f32[32,4,128]{2,1,0:T(4,128)S(1)}) custom-call(s32[6]{0:T(128)S(1)} %stack.51.place.refs_0_, f32[20,64,128]{2,1,0:T(8,128)S(1)} %get-tuple-element.55.refs_1_.g0, f32[20,64,128]{2,1,0:T(8,128)S(1)} %get-tuple-element.56.refs_2_.s0, ...), custom_call_target="tpu_custom_call" | custom-call | tf_op jit(solution)/shard_map/step/pallas_call | solution.py:38
  194.9 9.0 %all_to_all.46.dots = f32[32,4,128]{2,1,0:T(4,128)S(1)} all-to-all(f32[32,4,128]{2,1,0:T(4,128)S(1)} %get-tuple-element.105), channel_id=1, replica_groups=mesh['gx'=4,'gy'=8] {'gx','gy'}, dimensions={0} | all-to-all | bytes 131072 | tf_op jit(solution)/shard_map/all_to_all | solution.py:1003
  203.8 3.3 %final.1 = f32[4,20,16,128]{3,2,1,0:T(8,128)S(1)} custom-call(f32[20,64,128]{2,1,0:T(8,128)S(1)} %get-tuple-element.55.refs_1_.g0, f32[20,64,128]{2,1,0:T(8,128)S(1)} %get-tuple-element.56.refs_2_.s0, f32[20,64,128]{2,1,0:T(8,128)S(1)} %get-tuple-element.57.refs_3_.i0, f32[21,64,128]{2,1,0:T(8,128)S(1)} %get-tuple-element.58.refs_4_.f0, ...), custom_call_target="tpu_custom_call" | custom-call | tf_op jit(solution)/shard_map/final/pallas_call | solution.py:38
  207.1 12.6 %all_to_all.47.got = f32[4,20,16,128]{3,2,1,0:T(8,128)S(1)} all-to-all(f32[4,20,16,128]{3,2,1,0:T(8,128)S(1)} %final.1), channel_id=1, replica_groups=mesh['gx'=4,'gy'=8] {'gx'}, dimensions={0} | all-to-all | bytes 1310720 | tf_op jit(solution)/shard_map/all_to_all | solution.py:1061
  219.8 2.3 %unpack.1 = (f32[2,20,16,128]{3,2,1,0:T(8,128)}, f32[2,20,16,128]{3,2,1,0:T(8,128)}) custom-call(f32[4,20,16,128]{3,2,1,0:T(8,128)S(1)} %all_to_all.47.got), custom_call_target="tpu_custom_call" | custom-call | tf_op jit(solution)/shard_map/unpack/pallas_call | solution.py:38
  (13 shorter events, 0.1 us)
Async XLA Ops:
  0.6 21.3 %copy-start = (f32[20,16,128]{2,1,0:T(8,128)S(1)}, f32[20,16,128]{2,1,0:T(8,128)}, u32[]{:S(2)}) copy-start(f32[20,16,128]{2,1,0:T(8,128)} %param.8) | copy-start | bytes 491524
  3.0 35.0 %collective-permute-start.1 = (f32[3,16,128]{2,1,0:T(8,128)S(1)}, f32[3,16,128]{2,1,0:T(8,128)S(1)}, u32[]{:S(2)}, u32[]{:S(2)}) collective-permute-start(f32[3,16,128]{2,1,0:T(8,128)S(1)} %pad_maximum_fusion.1), channel_id=1, source_target_pairs={{1,0},{2,1},{3,2},{4,3},{5,4},{6,5},{7,6},{9,8},{10,9},{11,10},{12... | collective-permute-start | bytes 73736 | tf_op jit(solution)/shard_map/ppermute | solution.py:938
  4.3 33.7 %collective-permute-start = (f32[3,16,128]{2,1,0:T(8,128)S(1)}, f32[3,16,128]{2,1,0:T(8,128)S(1)}, u32[]{:S(2)}, u32[]{:S(2)}) collective-permute-start(f32[3,16,128]{2,1,0:T(8,128)S(1)} %pad_maximum_fusion.1), channel_id=1, source_target_pairs={{0,1},{1,2},{2,3},{3,4},{4,5},{5,6},{6,7},{8,9},{9,10},{10,11},{11... | collective-permute-start | bytes 73736 | tf_op jit(solution)/shard_map/ppermute | solution.py:937
  31.8 6.1 %copy-start.3 = (f32[16,128]{1,0:T(8,128)S(1)}, f32[16,128]{1,0:T(8,128)}, u32[]{:S(2)}) copy-start(f32[16,128]{1,0:T(8,128)} %param.10) | copy-start | bytes 24580
  31.8 6.2 %copy-start.4 = (f32[16,128]{1,0:T(8,128)S(1)}, f32[16,128]{1,0:T(8,128)}, u32[]{:S(2)}) copy-start(f32[16,128]{1,0:T(8,128)} %param.11) | copy-start | bytes 24580
  31.8 6.2 %copy-start.1 = (s32[16,128]{1,0:T(8,128)S(1)}, s32[16,128]{1,0:T(8,128)}, u32[]{:S(2)}) copy-start(s32[16,128]{1,0:T(8,128)} %param.12) | copy-start | bytes 24580
  31.8 6.2 %copy-start.2 = (s32[16,128]{1,0:T(8,128)S(1)}, s32[16,128]{1,0:T(8,128)}, u32[]{:S(2)}) copy-start(s32[16,128]{1,0:T(8,128)} %param.13) | copy-start | bytes 24580
  33.6 30.1 %collective-permute-start.2 = (f32[180,8,128]{2,1,0:T(8,128)S(1)}, f32[180,8,128]{2,1,0:T(8,128)S(1)}, u32[]{:S(2)}, u32[]{:S(2)}) collective-permute-start(f32[180,8,128]{2,1,0:T(8,128)S(1)} %pack.2), channel_id=1, source_target_pairs={{0,1},{1,2},{2,3},{3,4},{4,5},{5,6},{6,7},{8,9},{9,10},{10,11},{11... | collective-permute-start | bytes 2211848 | tf_op jit(solution)/shard_map/ppermute | solution.py:977
  48.6 15.1 %collective-permute-start.3 = (f32[72,8,128]{2,1,0:T(8,128)S(1)}, f32[72,8,128]{2,1,0:T(8,128)S(1)}, u32[]{:S(2)}, u32[]{:S(2)}) collective-permute-start(f32[72,8,128]{2,1,0:T(8,128)S(1)} %pack.3), channel_id=1, source_target_pairs={{0,1},{1,2},{2,3},{3,4},{4,5},{5,6},{6,7},{8,9},{9,10},{10,11},{11... | collective-permute-start | bytes 884744 | tf_op jit(solution)/shard_map/ppermute | solution.py:977
  54.0 18.3 %collective-permute-start.6 = (f32[9,64,128]{2,1,0:T(8,128)S(1)}, f32[9,64,128]{2,1,0:T(8,128)S(1)}, u32[]{:S(2)}, u32[]{:S(2)}) collective-permute-start(f32[9,64,128]{2,1,0:T(8,128)S(1)} %get-tuple-element.72.rest_1_), channel_id=1, source_target_pairs={{0,2},{1,3},{2,4},{3,5},{4,6},{5,7},{8,10},{9,11},{10,12},{11,13},... | collective-permute-start | bytes 884744 | tf_op jit(solution)/shard_map/ppermute | solution.py:987
  57.5 14.8 %collective-permute-start.5 = (f32[9,64,128]{2,1,0:T(8,128)S(1)}, f32[9,64,128]{2,1,0:T(8,128)S(1)}, u32[]{:S(2)}, u32[]{:S(2)}) collective-permute-start(f32[9,64,128]{2,1,0:T(8,128)S(1)} %get-tuple-element.72.rest_1_), channel_id=1, source_target_pairs={{1,0},{2,1},{3,2},{4,3},{5,4},{6,5},{7,6},{9,8},{10,9},{11,10},{12... | collective-permute-start | bytes 884744 | tf_op jit(solution)/shard_map/ppermute | solution.py:986
  58.8 16.4 %collective-permute-start.4 = (f32[9,64,128]{2,1,0:T(8,128)S(1)}, f32[9,64,128]{2,1,0:T(8,128)S(1)}, u32[]{:S(2)}, u32[]{:S(2)}) collective-permute-start(f32[9,64,128]{2,1,0:T(8,128)S(1)} %get-tuple-element.72.rest_1_), channel_id=1, source_target_pairs={{0,1},{1,2},{2,3},{3,4},{4,5},{5,6},{6,7},{8,9},{9,10},{10,11},{11... | collective-permute-start | bytes 884744 | tf_op jit(solution)/shard_map/ppermute | solution.py:985

commit v5 on v4

--- a/solution.py
+++ b/solution.py
@@ -56,11 +56,10 @@
         self.groups = self.rows // 8
         self.slots = cy // REACH
         self.packed = -(-self.groups // self.slots)
-        self.window = 4 * layers + 4
-        self.planes = self.window + 6
+        self.planes = 4 * layers + 4
         self.parts = -(-2 * ngx // 8) * 8
         self.piece = self.planes // PIECES
-        assert self.piece * PIECES == self.planes and self.piece >= layers + 10
+        assert self.piece * PIECES == self.planes and self.piece >= layers + 4
 
 
 def loop(lo, hi, step, init, by=None):
@@ -330,24 +329,39 @@
     loop(0, count, body, 0)
 
 
-def pack_kernel(d, count, place, *refs):
+def pack_kernel(d, place, *refs):
     *pieces, out = refs
     for t, piece in enumerate(pieces):
         def put(at, value, t=t):
             out[t * d.piece * d.packed + at] = value
-        pack_planes(d, place, piece, count, put)
+        pack_planes(d, place, piece, d.piece, put)
+
+
+def layout(d):
+    n0 = d.layers
+    return [(n0, None, n0), (4, None, 2 * n0), (n0, 0, 0), (n0, 1, 0), (n0, None, 0)]
 
 
 def segments(d):
-    n0, out = d.layers, []
-    for piece in range(PIECES):
-        at, end = piece * d.piece, min((piece + 1) * d.piece, d.window)
+    out, start = [], 0
+    for count, v, there in layout(d):
+        at, end = start, start + count
         while at < end:
-            part = min(at // n0, 2)
-            stop = min(end, (part + 1) * n0 if part < 2 else d.window)
-            out.append((piece, at - piece * d.piece, stop - at, part if part < 2 else None, at - part * n0))
+            piece = at // d.piece
+            stop = min(end, (piece + 1) * d.piece)
+            out.append((piece, at - piece * d.piece, stop - at, v, there + at - start))
             at = stop
+        start = end
     return out
+
+
+def edge_kernel(d, got, out):
+    n0, cx = d.layers, d.cx
+    for g in range(d.ngx):
+        at = slice(g * cx, (g + 1) * cx)
+        total = loop(0, n0, lambda k, t: t + got[g, k], jnp.zeros((cx, d.cy), F32))
+        mask = got[g, n0 + 2]
+        out[0, at, :], out[1, at, :], out[2, at, :] = mask, got[g, n0 + 3], total * mask
 
 
 def setup_kernel(d, place, *rest):
@@ -459,6 +473,8 @@
 
 
 COLUMN = 9
+SENT = 6
+SOME = 256.0
 
 
 def inside_of(d):
@@ -468,28 +484,26 @@
     return (row > 0, row < d.cx - 1, lane > 0, lane < d.cy - 1)
 
 
-def column_kernel(d, place, got, out, table, tmp):
+def column_kernel(d, place, got, own_edges, near_edges, opposite, out, table, tmp):
     n0, cx, cy = d.layers, d.cx, d.cy
-    base = d.planes - d.piece
-    at_spread, at_misc = 3 * n0 - base, 4 * n0 - base
+    at_misc = n0
     inside = inside_of(d)
     nil = jnp.zeros((cx, cy), F32)
-
-    def sums(g):
-        total = loop(0, n0, lambda k, t: t + got[g, at_spread + k], nil)
-        return total * got[g, at_misc + 2]
-
-    s2_all = [sums(g) for g in range(d.ngx)]
+    is_left = place[5]
     table[...] = jnp.zeros(table.shape, F32)
     for g in range(d.ngx):
         fr, cp = got[g, at_misc + 1], got[g, at_misc]
-        own = (got[g, at_misc + 2], got[g, at_misc + 3], s2_all[g])
+        rows_of = lambda g: slice(g * cx, (g + 1) * cx)
+        own = [own_edges[t, rows_of(g), :] for t in range(3)]
 
         def around(t):
             q = own[t]
-            up = (got[g - 1, at_misc + 2 + t] if t < 2 else s2_all[g - 1]) if g > 0 else nil
-            down = (got[g + 1, at_misc + 2 + t] if t < 2 else s2_all[g + 1]) if g + 1 < d.ngx else nil
-            left, right = got[g, at_misc + 4 + t], got[g, at_misc + 7 + t]
+            up = own_edges[t, rows_of(g - 1), :] if g > 0 else nil
+            down = own_edges[t, rows_of(g + 1), :] if g + 1 < d.ngx else nil
+            near = near_edges[t, rows_of(g), :]
+            other = opposite[t, rows_of(g), :]
+            left = jnp.where(is_left == 1, near, other)
+            right = jnp.where(is_left == 1, other, near)
             return (
                 jnp.where(inside[0], turn(q, 1, 0), turn(up, 1, 0)),
                 jnp.where(inside[1], turn(q, cx - 1, 0), turn(down, cx - 1, 0)),
@@ -502,17 +516,18 @@
         g2 = 4.0 * s2 + m * fr + n0 * (1.0 - m)
         cross = fr * cp * m
         at = slice(g * cx, (g + 1) * cx)
-        out[0, at, :], out[1, at, :], out[2, at, :], out[3, at, :] = g2, s2, cross, ids
+        out[0, at, :], out[1, at, :], out[2, at, :] = g2, s2, cross
+        out[3, at, :] = ids + SOME * m
+        out[4, at, :] = jnp.where(inside[2], m_d[3] * (1.0 + ids_d[3]), m_d[2] * (1.0 + ids_d[2]))
         weight3, weight4 = g2, g2
         for t in range(4):
-            out[4 + t, at, :] = m_d[t] * (1.0 + ids_d[t])
             weight3 = weight3 - jnp.where(inside[t] & (ids_d[t] == ids), s2 * m_d[t], 0.0)
             weight4 = weight4 - jnp.where(inside[t], s_d[t] * m, 0.0)
             tmp[3 + t] = jnp.where(inside[t], 0.0, s_d[t] * m)
         tmp[0], tmp[1], tmp[2] = weight3, cross, weight4
-        ids_row = lambda r: out[3, g * cx + r : g * cx + r + 1, :]
+        ids_row = lambda r: own_edges[1, g * cx + r : g * cx + r + 1, :]
         acc = segment_acc(d, ids_row, lambda _, r: tmp[0, r : r + 1, :], 1)
-        out[8, at, :] = jnp.broadcast_to(acc[0].T.sum(axis=0, keepdims=True), (cx, cy))
+        out[5, at, :] = jnp.broadcast_to(acc[0].T.sum(axis=0, keepdims=True), (cx, cy))
 
         @pl.when(place[1] == g)
         def _():
@@ -563,12 +578,21 @@
         near, column, opposite, far, cols, r3, big, tmp, chunk = rest
         at_near = jnp.where(place[5] == 1, 0, 2)
 
-        def stack(p, c):
-            cols[1, p], cols[3, p] = column[p], far[p]
-            cols[at_near, p], cols[2 - at_near, p] = near[p], opposite[p]
-            return c
-
-        loop(0, COLUMN, stack, 0)
+        rows, cy = d.rows, d.cy
+        line = lax.broadcasted_iota(jnp.int32, (rows, cy), 0)
+        lane = lanes((rows, cy))
+        for source, pos in ((column, 1), (far, 3), (near, at_near), (opposite, 2 - at_near)):
+            cols[pos, 0], cols[pos, 1], cols[pos, 2] = source[0], source[1], source[2]
+            cols[pos, 8] = source[5]
+            both = source[3]
+            live = both >= SOME
+            ids = both - jnp.where(live, SOME, 0.0)
+            code = jnp.where(live, 1.0 + ids, 0.0)
+            cols[pos, 3] = ids
+            cols[pos, 4] = jnp.where(line == 0, 0.0, turn(code, 1, 0))
+            cols[pos, 5] = jnp.where(line == rows - 1, 0.0, turn(code, rows - 1, 0))
+            cols[pos, 6] = jnp.where(lane == 0, source[4], turn(code, 1, 1))
+            cols[pos, 7] = jnp.where(lane == cy - 1, source[4], turn(code, cy - 1, 1))
     else:
         cols, r3, big, tmp, chunk = rest
     ngx, ngy = d.ngx, d.ngy
@@ -931,27 +955,6 @@
     first = jnp.where(is_left, cy - REACH, 0)
     place = jnp.stack([gx * ngy + gy, gx, gy, first, off, is_left.astype(jnp.int32)]).astype(jnp.int32)
 
-    mask_f, ids_f = ice_mask.astype(F32), aggregates.astype(F32)
-    mine = jnp.stack([mask_f, ids_f, spread.sum(axis=0) * mask_f])
-    shift = lambda by: [(i, i + by) for i in range(ngy) if 0 <= i + by < ngy]
-    left = lax.ppermute(mine, "gy", shift(1))
-    right = lax.ppermute(mine, "gy", shift(-1))
-    planes = [
-        forcing.reshape(2 * layers, cx, cy),
-        viscosity,
-        spread,
-        jnp.stack([coupling, friction, mask_f, ids_f]),
-        left,
-        right,
-    ]
-    pieces, start = [[] for _ in range(PIECES)], 0
-    for part in planes:
-        end = start + part.shape[0]
-        for t in range(PIECES):
-            low, high = max(start, t * d.piece), min(end, (t + 1) * d.piece)
-            if low < high:
-                pieces[t].append(part[low - start : high - start])
-        start = end
     def sided(by):
         return [
             (i * ngy + j, i * ngy + to)
@@ -961,24 +964,43 @@
             if 0 <= to < ngy
         ]
 
+    small = jnp.stack([coupling, friction, ice_mask.astype(F32), aggregates.astype(F32)])
+    pieces, start = [[] for _ in range(PIECES)], 0
+    for part in [spread, small, forcing.reshape(2 * layers, cx, cy), viscosity]:
+        end = start + part.shape[0]
+        for t in range(PIECES):
+            low, high = max(start, t * d.piece), min(end, (t + 1) * d.piece)
+            if low < high:
+                pieces[t].append(part[low - start : high - start])
+        start = end
     gathered, packed = [], []
     for t in range(PIECES):
         got = lax.all_gather(jnp.concatenate(pieces[t]), "gx")
+        if t == 1:
+            got, near_edges, opposite_edges = lax.optimization_barrier(
+                (got, near_edges, opposite_edges)
+            )
         gathered.append(got)
+        if t == 0:
+            (edges,) = call(
+                functools.partial(edge_kernel, d), [(3, d.rows, cy)], [got], name="edge"
+            )
+            opposite_edges = lax.ppermute(edges, both, sided(-1))
+            near_edges = lax.ppermute(edges, both, sided(1))
         if t >= PIECES - 2:
             use = gathered[t:] if t == PIECES - 1 else gathered
-            count = d.window - t * d.piece if t == PIECES - 1 else d.piece
+            tiles = len(use) * d.piece * d.packed
             (sent,) = call(
-                functools.partial(pack_kernel, d, count),
-                [(len(use) * count * d.packed, 8, cy)],
+                functools.partial(pack_kernel, d),
+                [(tiles, 8, cy)],
                 [place, *use],
                 name="pack",
             )
             packed.append(lax.ppermute(sent, both, sided(1)))
     column, table_own = call(
         functools.partial(column_kernel, d),
-        [(COLUMN, d.rows, cy), (8, cy)],
-        [place, gathered[-1]],
+        [(SENT, d.rows, cy), (8, cy)],
+        [place, gathered[0], edges, near_edges, opposite_edges],
         [(7, cx, cy)],
         name="column",
     )

time: 223 us -> 220 us (0.987)
  waiting for transfers between devices: 2.89 us -> 0.02 us
    ppermute x1, waiting for transfers between devices: 2.87 us -> 0.01 us  [body(): near = lax.ppermute(column, both, sided(1))]
    unnamed x13 -> x7, local copies, waits for them, and re-layouts: 0.03 us -> 2.38 us
    pallas_call x12 -> x13, Pallas kernels: 78.5 us -> 78.6 us  [call(): pl.pallas_call(kernel, out_shape=[jax.ShapeDtypeStruct(s, F32) for s in o...]
  transfers between devices with their start and end apart: 7 -> 7, of which waited for: 1 -> 0; matrix products, arithmetic and copies ran while one was open for 1% -> 0% of each run, Pallas kernels for 6% -> 6%
where the time goes in v5:
time: 220 us; the launch traced here: 219 us
  blocking collectives  112 us (51%)
  Pallas kernels  78.6 us (36%)
  starting transfers between devices  23 us (10%)
  local copies, waits for them, and re-layouts  3.25 us (1%)
    pallas_call x13, Pallas kernels, call(): pl.pallas_call(kernel, out_shape=[jax.ShapeDtypeStruct(s, F32) for s in o...  78.6 us
    all_to_all x7, blocking collectives, share(): return lax.all_to_all(x, both, 0, 0)  70.7 us
    all_gather x3, blocking collectives, body(): got = lax.all_gather(jnp.concatenate(pieces[t]), 'gx')  28.8 us
    all_to_all x1, blocking collectives, body(): got = lax.all_to_all(out, 'gx', 0, 0)  12.6 us
    ppermute x2, starting transfers between devices, body(): packed.append(lax.ppermute(sent, both, sided(1)))  7.81 us
    ppermute x1, starting transfers between devices, body(): near = lax.ppermute(column, both, sided(1))  4.56 us
    ppermute x1, starting transfers between devices, body(): near_edges = lax.ppermute(edges, both, sided(1))  4.55 us
  transfers between devices with their start and end apart: 7, of which 0 were waited for; matrix products, arithmetic and copies ran while one was open for 0% of the time, Pallas kernels for 6%

profile of v5, /device:TPU:0, one launch (start us, length us, event | category | flops | bytes accessed | tf_op | source)
XLA Modules:
  0.0 219.2 jit_solution(9953253029655301599)
XLA Ops:
  0.6 0.0 copy-start
  0.6 1.0 constant_dynamic-update-slice_fusion.4
  1.6 0.7 constant_dynamic-update-slice_fusion.3
  2.3 0.7 constant_dynamic-update-slice_fusion.2
  3.0 0.7 constant_dynamic-update-slice_fusion.1
  3.7 0.7 constant_dynamic-update-slice_fusion
  4.4 0.8 slice_dynamic-update-slice_fusion
  5.2 10.8 %all-gather = f32[112,16,128]{2,1,0:T(8,128)S(1)} all-gather(f32[28,16,128]{2,1,0:T(8,128)S(1)} %slice_dynamic-update-slice_fusion), channel_id=2, replica_groups=mesh['gx'=4,'gy'=8] {'gx'}, dimensions={0}, use_global_device_ids=true | all-gather | bytes 1146880 | tf_op jit(solution)/shard_map/all_gather | solution.py:978
  16.0 0.1 edge.1.own_edges
  16.1 1.3 collective-permute-start.1
  17.4 4.6 %collective-permute-start = (f32[3,64,128]{2,1,0:T(8,128)S(1)}, f32[3,64,128]{2,1,0:T(8,128)S(1)}, u32[]{:S(2)}, u32[]{:S(2)}) collective-permute-start(f32[3,64,128]{2,1,0:T(8,128)S(1)} %edge.1.own_edges), channel_id=1, source_target_pairs={{0,1},{1,2},{2,3},{3,4},{4,5},{5,6},{6,7},{8,9},{9,10},{10,11},{11... | collective-permute-start | bytes 294920 | tf_op jit(solution)/shard_map/ppermute | solution.py:989
  21.9 0.0 copy-done
  22.0 8.9 %all-gather.1 = f32[112,16,128]{2,1,0:T(8,128)S(1)} all-gather(f32[28,16,128]{2,1,0:T(8,128)S(1)} %slice.13), channel_id=3, replica_groups=mesh['gx'=4,'gy'=8] {'gx'}, dimensions={0}, use_global_device_ids=true | all-gather | bytes 1146880 | tf_op jit(solution)/shard_map/all_gather | solution.py:978
  30.9 0.1 stack.43.place.refs_0_
  31.0 0.0 copy-done.1
  31.0 0.0 collective-permute-done.1.opposite
  31.0 0.0 collective-permute-done.near_edges
  31.0 1.7 pack.2
  32.7 4.3 %collective-permute-start.2 = (f32[168,8,128]{2,1,0:T(8,128)S(1)}, f32[168,8,128]{2,1,0:T(8,128)S(1)}, u32[]{:S(2)}, u32[]{:S(2)}) collective-permute-start(f32[168,8,128]{2,1,0:T(8,128)S(1)} %pack.2), channel_id=1, source_target_pairs={{0,1},{1,2},{2,3},{3,4},{4,5},{5,6},{6,7},{8,9},{9,10},{10,11},{11... | collective-permute-start | bytes 2064392 | tf_op jit(solution)/shard_map/ppermute | solution.py:999
  37.0 9.1 %all-gather.2 = f32[112,16,128]{2,1,0:T(8,128)S(1)} all-gather(f32[28,16,128]{2,1,0:T(8,128)S(1)} %pad_maximum_fusion), channel_id=4, replica_groups=mesh['gx'=4,'gy'=8] {'gx'}, dimensions={0}, use_global_device_ids=true | all-gather | bytes 1146880 | tf_op jit(solution)/shard_map/all_gather | solution.py:978
  46.2 1.1 pack.3
  47.3 3.5 %collective-permute-start.3 = (f32[84,8,128]{2,1,0:T(8,128)S(1)}, f32[84,8,128]{2,1,0:T(8,128)S(1)}, u32[]{:S(2)}, u32[]{:S(2)}) collective-permute-start(f32[84,8,128]{2,1,0:T(8,128)S(1)} %pack.3), channel_id=1, source_target_pairs={{0,1},{1,2},{2,3},{3,4},{4,5},{5,6},{6,7},{8,9},{9,10},{10,11},{11... | collective-permute-start | bytes 1032200 | tf_op jit(solution)/shard_map/ppermute | solution.py:999
  50.8 2.7 %column.1 = (f32[6,64,128]{2,1,0:T(8,128)S(1)}, f32[8,128]{1,0:T(8,128)S(1)}) custom-call(s32[6]{0:T(128)S(1)} %stack.43.place.refs_0_, f32[4,28,16,128]{3,2,1,0:T(8,128)S(1)} %bitcast.20, f32[3,64,128]{2,1,0:T(8,128)S(1)} %edge.1.own_edges, f32[3,64,128]{2,1,0:T(8,128)S(1)} %collective-permute-done.near_edges, f32[3,64,128]{2,1,0:T(8,128)S(1)} %collective-permute-done.1.opposite), custom_call_target="tpu_custom_call" | custom-call | tf_op jit(solution)/shard_map/column/pallas_call | solution.py:38
  53.5 3.5 %collective-permute-start.6 = (f32[6,64,128]{2,1,0:T(8,128)S(1)}, f32[6,64,128]{2,1,0:T(8,128)S(1)}, u32[]{:S(2)}, u32[]{:S(2)}) collective-permute-start(f32[6,64,128]{2,1,0:T(8,128)S(1)} %get-tuple-element.78.rest_1_), channel_id=1, source_target_pairs={{0,2},{1,3},{2,4},{3,5},{4,6},{5,7},{8,10},{9,11},{10,12},{11,13},... | collective-permute-start | bytes 589832 | tf_op jit(solution)/shard_map/ppermute | solution.py:1009
  57.0 1.3 collective-permute-start.5
  58.3 4.6 %collective-permute-start.4 = (f32[6,64,128]{2,1,0:T(8,128)S(1)}, f32[6,64,128]{2,1,0:T(8,128)S(1)}, u32[]{:S(2)}, u32[]{:S(2)}) collective-permute-start(f32[6,64,128]{2,1,0:T(8,128)S(1)} %get-tuple-element.78.rest_1_), channel_id=1, source_target_pairs={{0,1},{1,2},{2,3},{3,4},{4,5},{5,6},{6,7},{8,9},{9,10},{10,11},{11... | collective-permute-start | bytes 589832 | tf_op jit(solution)/shard_map/ppermute | solution.py:1007
  62.8 0.0 collective-permute-done.3.rest_4_
  62.8 0.0 collective-permute-done.2.rest_3_
  62.8 8.6 %setup.1 = (f32[2,20,64,128]{3,2,1,0:T(8,128)S(1)}, f32[20,64,128]{2,1,0:T(8,128)S(1)}, f32[20,64,128]{2,1,0:T(8,128)S(1)}, f32[20,64,128]{2,1,0:T(8,128)S(1)}, ...) custom-call(s32[6]{0:T(128)S(1)} %stack.43.place.refs_0_, ...), custom_call_target="tpu_custom_call" | custom-call | tf_op jit(solution)/shard_map/setup/pallas_call | solution.py:38
  71.5 0.0 collective-permute-done.6.rest_3_
  71.5 0.0 collective-permute-done.5.rest_2_
  71.5 0.0 collective-permute-done.4.rest_0_
  71.5 13.5 %all_to_all.40.parts = f32[32,8,128]{2,1,0:T(8,128)S(1)} all-to-all(f32[32,8,128]{2,1,0:T(8,128)S(1)} %get-tuple-element.79), channel_id=1, replica_groups=mesh['gx'=4,'gy'=8] {'gx','gy'}, dimensions={0} | all-to-all | bytes 262144 | tf_op jit(solution)/shard_map/all_to_all | solution.py:1025
  85.0 1.1 point_first.3
  86.1 10.0 %all_to_all.41.refs_17_.refs_18_ = f32[32,8,128]{2,1,0:T(8,128)S(1)} all-to-all(f32[32,8,128]{2,1,0:T(8,128)S(1)} %get-tuple-element.84), channel_id=1, replica_groups=mesh['gx'=4,'gy'=8] {'gx','gy'}, dimensions={0} | all-to-all | bytes 262144 | tf_op jit(solution)/shard_map/all_to_all | solution.py:1025
  96.0 19.7 %step.3 = (f32[2,20,64,128]{3,2,1,0:T(8,128)S(1)}, f32[2,20,64,128]{3,2,1,0:T(8,128)S(1)}, f32[2,20,64,128]{3,2,1,0:T(8,128)S(1)}, f32[2,10,64,128]{3,2,1,0:T(8,...) custom-call(s32[6]{0:T(128)S(1)} %stack.43.place.refs_0_, ...), custom_call_target="tpu_custom_call" | custom-call | tf_op jit(solution)/shard_map/step/pallas_call | solution.py:38
  115.7 10.0 %all_to_all.42.parts = f32[32,8,128]{2,1,0:T(8,128)S(1)} all-to-all(f32[32,8,128]{2,1,0:T(8,128)S(1)} %get-tuple-element.93), channel_id=1, replica_groups=mesh['gx'=4,'gy'=8] {'gx','gy'}, dimensions={0} | all-to-all | bytes 262144 | tf_op jit(solution)/shard_map/all_to_all | solution.py:1025
  125.7 1.0 point_first.4
  126.7 9.4 %all_to_all.43.refs_17_ = f32[32,4,128]{2,1,0:T(4,128)S(1)} all-to-all(f32[32,4,128]{2,1,0:T(4,128)S(1)} %get-tuple-element.95), channel_id=1, replica_groups=mesh['gx'=4,'gy'=8] {'gx','gy'}, dimensions={0} | all-to-all | bytes 131072 | tf_op jit(solution)/shard_map/all_to_all | solution.py:1025
  136.1 19.9 %step.4 = (f32[2,20,64,128]{3,2,1,0:T(8,128)S(1)}, f32[8,128]{1,0:T(8,128)S(1)}, f32[2,20,64,128]{3,2,1,0:T(8,128)S(1)}, f32[2,20,64,128]{3,2,1,0:T(8,128)S(1)},...) custom-call(s32[6]{0:T(128)S(1)} %stack.43.place.refs_0_, ...), custom_call_target="tpu_custom_call" | custom-call | tf_op jit(solution)/shard_map/step/pallas_call | solution.py:38
  156.1 9.5 %all_to_all.44.parts = f32[32,8,128]{2,1,0:T(8,128)S(1)} all-to-all(f32[32,8,128]{2,1,0:T(8,128)S(1)} %get-tuple-element.104), channel_id=1, replica_groups=mesh['gx'=4,'gy'=8] {'gx','gy'}, dimensions={0} | all-to-all | bytes 262144 | tf_op jit(solution)/shard_map/all_to_all | solution.py:1025
  165.6 1.0 point_first.5
  166.6 9.3 %all_to_all.45.refs_17_ = f32[32,4,128]{2,1,0:T(4,128)S(1)} all-to-all(f32[32,4,128]{2,1,0:T(4,128)S(1)} %get-tuple-element.106), channel_id=1, replica_groups=mesh['gx'=4,'gy'=8] {'gx','gy'}, dimensions={0} | all-to-all | bytes 131072 | tf_op jit(solution)/shard_map/all_to_all | solution.py:1025
  175.9 16.1 %step.5 = (f32[2,20,64,128]{3,2,1,0:T(8,128)}, f32[8,128]{1,0:T(8,128)S(1)}, f32[2,20,64,128]{3,2,1,0:T(8,128)S(1)}, f32[4,128]{1,0:T(4,128)}, f32[32,4,128]{2,1,0:T(4,128)S(1)}) custom-call(s32[6]{0:T(128)S(1)} %stack.43.place.refs_0_, f32[20,64,128]{2,1,0:T(8,128)S(1)} %get-tuple-element.59.refs_1_.g0, f32[20,64,128]{2,1,0:T(8,128)S(1)} %get-tuple-element.60.refs_2_.s0, ...), custom_call_target="tpu_custom_call" | custom-call | tf_op jit(solution)/shard_map/step/pallas_call | solution.py:38
  192.0 9.0 %all_to_all.46.dots = f32[32,4,128]{2,1,0:T(4,128)S(1)} all-to-all(f32[32,4,128]{2,1,0:T(4,128)S(1)} %get-tuple-element.111), channel_id=1, replica_groups=mesh['gx'=4,'gy'=8] {'gx','gy'}, dimensions={0} | all-to-all | bytes 131072 | tf_op jit(solution)/shard_map/all_to_all | solution.py:1025
  201.0 3.3 %final.1 = f32[4,20,16,128]{3,2,1,0:T(8,128)S(1)} custom-call(f32[20,64,128]{2,1,0:T(8,128)S(1)} %get-tuple-element.59.refs_1_.g0, f32[20,64,128]{2,1,0:T(8,128)S(1)} %get-tuple-element.60.refs_2_.s0, f32[20,64,128]{2,1,0:T(8,128)S(1)} %get-tuple-element.61.refs_3_.i0, f32[21,64,128]{2,1,0:T(8,128)S(1)} %get-tuple-element.62.refs_4_.f0, ...), custom_call_target="tpu_custom_call" | custom-call | tf_op jit(solution)/shard_map/final/pallas_call | solution.py:38
  204.3 12.6 %all_to_all.47.got = f32[4,20,16,128]{3,2,1,0:T(8,128)S(1)} all-to-all(f32[4,20,16,128]{3,2,1,0:T(8,128)S(1)} %final.1), channel_id=1, replica_groups=mesh['gx'=4,'gy'=8] {'gx'}, dimensions={0} | all-to-all | bytes 1310720 | tf_op jit(solution)/shard_map/all_to_all | solution.py:1083
  216.9 2.3 %unpack.1 = (f32[2,20,16,128]{3,2,1,0:T(8,128)}, f32[2,20,16,128]{3,2,1,0:T(8,128)}) custom-call(f32[4,20,16,128]{3,2,1,0:T(8,128)S(1)} %all_to_all.47.got), custom_call_target="tpu_custom_call" | custom-call | tf_op jit(solution)/shard_map/unpack/pallas_call | solution.py:38
  (4 shorter events, 0.0 us)
Async XLA Ops:
  0.6 21.3 %copy-start = (f32[2,20,16,128]{3,2,1,0:T(8,128)S(1)}, f32[2,20,16,128]{3,2,1,0:T(8,128)}, u32[]{:S(2)}) copy-start(f32[2,20,16,128]{3,2,1,0:T(8,128)} %param.7) | copy-start | bytes 983044
  16.0 15.0 %copy-start.1 = (f32[20,16,128]{2,1,0:T(8,128)S(1)}, f32[20,16,128]{2,1,0:T(8,128)}, u32[]{:S(2)}) copy-start(f32[20,16,128]{2,1,0:T(8,128)} %param.8) | copy-start | bytes 491524
  16.1 14.9 %collective-permute-start.1 = (f32[3,64,128]{2,1,0:T(8,128)S(1)}, f32[3,64,128]{2,1,0:T(8,128)S(1)}, u32[]{:S(2)}, u32[]{:S(2)}) collective-permute-start(f32[3,64,128]{2,1,0:T(8,128)S(1)} %edge.1.own_edges), channel_id=1, source_target_pairs={{1,0},{2,1},{3,2},{4,3},{5,4},{6,5},{7,6},{9,8},{10,9},{11,10},{12... | collective-permute-start | bytes 294920 | tf_op jit(solution)/shard_map/ppermute | solution.py:988
  17.4 13.6 %collective-permute-start = (f32[3,64,128]{2,1,0:T(8,128)S(1)}, f32[3,64,128]{2,1,0:T(8,128)S(1)}, u32[]{:S(2)}, u32[]{:S(2)}) collective-permute-start(f32[3,64,128]{2,1,0:T(8,128)S(1)} %edge.1.own_edges), channel_id=1, source_target_pairs={{0,1},{1,2},{2,3},{3,4},{4,5},{5,6},{6,7},{8,9},{9,10},{10,11},{11... | collective-permute-start | bytes 294920 | tf_op jit(solution)/shard_map/ppermute | solution.py:989
  32.7 30.2 %collective-permute-start.2 = (f32[168,8,128]{2,1,0:T(8,128)S(1)}, f32[168,8,128]{2,1,0:T(8,128)S(1)}, u32[]{:S(2)}, u32[]{:S(2)}) collective-permute-start(f32[168,8,128]{2,1,0:T(8,128)S(1)} %pack.2), channel_id=1, source_target_pairs={{0,1},{1,2},{2,3},{3,4},{4,5},{5,6},{6,7},{8,9},{9,10},{10,11},{11... | collective-permute-start | bytes 2064392 | tf_op jit(solution)/shard_map/ppermute | solution.py:999
  47.3 15.6 %collective-permute-start.3 = (f32[84,8,128]{2,1,0:T(8,128)S(1)}, f32[84,8,128]{2,1,0:T(8,128)S(1)}, u32[]{:S(2)}, u32[]{:S(2)}) collective-permute-start(f32[84,8,128]{2,1,0:T(8,128)S(1)} %pack.3), channel_id=1, source_target_pairs={{0,1},{1,2},{2,3},{3,4},{4,5},{5,6},{6,7},{8,9},{9,10},{10,11},{11... | collective-permute-start | bytes 1032200 | tf_op jit(solution)/shard_map/ppermute | solution.py:999
  53.5 18.0 %collective-permute-start.6 = (f32[6,64,128]{2,1,0:T(8,128)S(1)}, f32[6,64,128]{2,1,0:T(8,128)S(1)}, u32[]{:S(2)}, u32[]{:S(2)}) collective-permute-start(f32[6,64,128]{2,1,0:T(8,128)S(1)} %get-tuple-element.78.rest_1_), channel_id=1, source_target_pairs={{0,2},{1,3},{2,4},{3,5},{4,6},{5,7},{8,10},{9,11},{10,12},{11,13},... | collective-permute-start | bytes 589832 | tf_op jit(solution)/shard_map/ppermute | solution.py:1009
  57.0 14.5 %collective-permute-start.5 = (f32[6,64,128]{2,1,0:T(8,128)S(1)}, f32[6,64,128]{2,1,0:T(8,128)S(1)}, u32[]{:S(2)}, u32[]{:S(2)}) collective-permute-start(f32[6,64,128]{2,1,0:T(8,128)S(1)} %get-tuple-element.78.rest_1_), channel_id=1, source_target_pairs={{1,0},{2,1},{3,2},{4,3},{5,4},{6,5},{7,6},{9,8},{10,9},{11,10},{12... | collective-permute-start | bytes 589832 | tf_op jit(solution)/shard_map/ppermute | solution.py:1008
  58.3 13.2 %collective-permute-start.4 = (f32[6,64,128]{2,1,0:T(8,128)S(1)}, f32[6,64,128]{2,1,0:T(8,128)S(1)}, u32[]{:S(2)}, u32[]{:S(2)}) collective-permute-start(f32[6,64,128]{2,1,0:T(8,128)S(1)} %get-tuple-element.78.rest_1_), channel_id=1, source_target_pairs={{0,1},{1,2},{2,3},{3,4},{4,5},{5,6},{6,7},{8,9},{9,10},{10,11},{11... | collective-permute-start | bytes 589832 | tf_op jit(solution)/shard_map/ppermute | solution.py:1007
